TPU v7x, 128 devices: a whole 4x4x4 slice. The times are simulated.
128 devices in a mesh: swath: 32 (over x, y, core), chan: 4 (over z).
Axes of the slice: x: 4, y: 4, z: 4, core: 2. Of those that a mesh axis runs over, the one named last changes fastest.
Arguments:
- innovations: float32 [2097152], P(('swath', 'chan')), may hold values from -6 to 6
- obs_precision: float32 [2097152], P(('swath', 'chan')), may hold values from 0.25 to 4
- jacobian: bfloat16 [2097152, 128], P(('swath', 'chan')), may hold values from -0.5 to 0.5
- predictors: float32 [8, 2097152], P(None, ('swath', 'chan')), may hold values from -5 to 5
- obs_column: int32 [2097152], P(('swath', 'chan')), may hold values from 0 to 2047, as said below
- obs_channel: int32 [2097152], P(('swath', 'chan')), may hold values from 0 to 5119
- obs_count: int32 [32, 4], P('swath', 'chan'), may hold values from 5461 to 16384, as said below
- smoothing: float32 [128], replicated, may hold values from 0.02 to 0.12
- bias_precision: float32 [8, 5120], P(None, 'chan'), may hold values from 1 to 100
Outputs:
- control_state: float32 [1024, 256, 128], P('swath', 'chan')
- bias_increment: float32 [8, 5120], P(None, 'chan')
- residual_norms: float32 [3], replicated
Inputs may be any that keep to these rules, and one draw needn't show every extreme that they name: `obs_column`: Row-major index latitude row * 64 + longitude column within the tile of the device that holds the slot; all slots of an aligned block of 128 slots lie in one latitude row. `obs_channel`: channel c belongs to block c // 256, whose coefficients are owned by chan index c // 1280. `obs_count`: slots below the count hold live observations, the rest are ignored; some device is full in every draw.
All inputs are finite; a program needn't handle non-finite values.
Results may differ from a plain program's by a relative error of at most 0.0003.
Values sent between devices are 32-bit elements; how exact they have to be, the bound alone decides.
No kernel may reach another device: no remote copies, remote signals or barrier semaphores. Data moves between devices by JAX's collectives and lax.ppermute only.
A program may use at most 128 MiB of HBM per device.

v0:
```python
import functools

import jax
import jax.numpy as jnp
from jax import lax
from jax.experimental import pallas as pl
from jax.experimental.pallas import tpu as pltpu
from jax.sharding import Mesh
from jax.sharding import PartitionSpec as P

LEV = 128
NPRED = 8
LINE = 128
LAT_DEV = 32
LON_DEV = 64
SLOTS = 16384
LINES = SLOTS // LINE
GROUP = 8
KSLOT = GROUP * LINE
LOW = 256
HIGH = 20
CHAN_HIGH = 5
PAD_HIGH = 6
ROWS = 3
DEVICES = 128
TABLE = DEVICES * ROWS
SWATH = ("swath_0", "swath_1", "swath_2")
SWATH_CHAN = ("swath_0", "swath_1", "swath_2", "chan")
OWNERS = ("chan", "swath_0", "swath_1", "swath_2")
F32 = jnp.float32
BF16 = jnp.bfloat16

VMEM = pl.BlockSpec(memory_space=pltpu.VMEM)
SMEM = pl.BlockSpec(memory_space=pltpu.SMEM)


def call(kernel, out_shape, in_specs, args, scratch=(), flops=10**9, limit=40, name=None):
    outs = out_shape if isinstance(out_shape, (tuple, list)) else [out_shape]
    return pl.pallas_call(
        kernel,
        out_shape=out_shape,
        in_specs=in_specs,
        out_specs=jax.tree.map(lambda _: VMEM, out_shape),
        scratch_shapes=list(scratch),
        compiler_params=pltpu.CompilerParams(vmem_limit_bytes=limit * 2**20),
        cost_estimate=pl.CostEstimate(flops=flops, bytes_accessed=4 * 2**20, transcendentals=0),
        name=name,
    )(*args)


def split(x):
    high = x.astype(BF16)
    return high, (x - high.astype(F32)).astype(BF16)


def slot_of(high):
    return high // CHAN_HIGH * PAD_HIGH + high % CHAN_HIGH


def one_hot_low(low8, hot_ref):
    ids = lax.broadcasted_iota(jnp.int32, (LOW, LINE), 0).astype(F32).astype(BF16)
    low = low8.astype(F32)
    for j in range(GROUP):
        row = jnp.broadcast_to(low[j : j + 1], (LOW, LINE)).astype(BF16)
        hot_ref[:, j * LINE : (j + 1) * LINE] = jnp.where(
            ids == row, jnp.ones((), BF16), jnp.zeros((), BF16)
        )


def spread_high(values, high_row, parts):
    offset = (lax.broadcasted_iota(jnp.int32, (16, LINE), 0) // 8).astype(F32)
    base = (jnp.broadcast_to(high_row, (16, LINE)) - offset).astype(BF16)
    pieces = []
    for value in values:
        for half in split(value):
            pieces.append(jnp.concatenate([half, half], axis=0))
    for m in range(HIGH // 2):
        mask = base == jnp.array(2 * m, BF16)
        for piece, (ref, cols) in zip(pieces, parts):
            ref[16 * m : 16 * m + 16, cols] = jnp.where(mask, piece, jnp.zeros((), BF16))


def dot_rows(left, right):
    return lax.dot_general(left, right, (((1,), (1,)), ((), ())), preferred_element_type=F32)


def table_start_kernel(
    count_ref, innov_ref, prec_ref, pred_ref, chan_ref,
    table_ref, weight_ref, source_ref,
    hot_ref, a_hi, a_lo, b_hi, b_lo, acc_ref, acc2_ref,
):
    count = count_ref[0, 0]
    acc_ref[...] = jnp.zeros_like(acc_ref)
    acc2_ref[...] = jnp.zeros_like(acc2_ref)

    def step(g, _):
        rows = pl.ds(pl.multiple_of(g * GROUP, GROUP), GROUP)
        slot = (
            g * KSLOT
            + lax.broadcasted_iota(jnp.int32, (GROUP, LINE), 0) * LINE
            + lax.broadcasted_iota(jnp.int32, (GROUP, LINE), 1)
        )
        weight = jnp.where(slot < count, prec_ref[rows, :], 0.0)
        source = weight * innov_ref[rows, :]
        weight_ref[rows, :] = weight
        source_ref[rows, :] = source
        chan = chan_ref[rows, :]
        one_hot_low(chan & (LOW - 1), hot_ref)
        high = (chan >> 8).astype(F32)
        for j in range(GROUP):
            pred = pred_ref[:, pl.ds(pl.multiple_of(g * KSLOT + j * LINE, LINE), LINE)]
            cols = slice(j * LINE, (j + 1) * LINE)
            spread_high(
                [pred * source[j : j + 1], pred * pred * weight[j : j + 1]],
                high[j : j + 1],
                [(a_hi, cols), (a_lo, cols), (b_hi, cols), (b_lo, cols)],
            )
        hot = hot_ref[...]
        acc_ref[...] += dot_rows(a_hi[...], hot) + dot_rows(a_lo[...], hot)
        acc2_ref[...] += dot_rows(b_hi[...], hot) + dot_rows(b_lo[...], hot)
        return 0

    lax.fori_loop(0, LINES // GROUP, step, 0)
    table_ref[...] = jnp.zeros_like(table_ref)
    for high in range(HIGH):
        for half in range(2):
            at = 16 * (slot_of(high) * 2 + half)
            cols = slice(half * 128, half * 128 + 128)
            table_ref[pl.ds(at, 8, stride=2), :] = acc_ref[high * 8 : high * 8 + 8, cols]
            table_ref[pl.ds(at + 1, 8, stride=2), :] = acc2_ref[high * 8 : high * 8 + 8, cols]


def image_kernel(
    coef_ref, weight_ref, state_ref, pred_ref, chan_ref,
    table_ref, image_ref,
    hot_ref, got_ref, c_hi, c_lo, a_hi, a_lo, acc_ref,
):
    for high in range(HIGH):
        for half in range(2):
            at = 8 * (slot_of(high) * 2 + half)
            acc_ref[high * 8 : high * 8 + 8, half * 128 : half * 128 + 128] = coef_ref[at : at + 8, :]
    high_part, low_part = split(acc_ref[...])
    c_hi[...] = high_part
    c_lo[...] = low_part
    acc_ref[...] = jnp.zeros_like(acc_ref)

    def step(g, _):
        rows = pl.ds(pl.multiple_of(g * GROUP, GROUP), GROUP)
        chan = chan_ref[rows, :]
        one_hot_low(chan & (LOW - 1), hot_ref)
        hot = hot_ref[...]
        got_ref[...] = jnp.dot(c_hi[...], hot, preferred_element_type=F32) + jnp.dot(
            c_lo[...], hot, preferred_element_type=F32
        )
        high_id = chan >> 8
        looked = []
        preds = []
        for j in range(GROUP):
            cols = slice(j * LINE, (j + 1) * LINE)
            pred = pred_ref[:, pl.ds(pl.multiple_of(g * KSLOT + j * LINE, LINE), LINE)]
            ids = jnp.broadcast_to(high_id[j : j + 1], (8, LINE))
            coef = got_ref[0:8, cols]
            for high in range(1, HIGH):
                coef = jnp.where(ids == high, got_ref[high * 8 : high * 8 + 8, cols], coef)
            looked.append(jnp.sum(pred * coef, axis=0, keepdims=True))
            preds.append(pred)
        image = weight_ref[rows, :] * (state_ref[rows, :] + jnp.concatenate(looked, axis=0))
        image_ref[rows, :] = image
        high_f = high_id.astype(F32)
        for j in range(GROUP):
            cols = slice(j * LINE, (j + 1) * LINE)
            spread_high(
                [preds[j] * image[j : j + 1]], high_f[j : j + 1], [(a_hi, cols), (a_lo, cols)]
            )
        acc_ref[...] += dot_rows(a_hi[...], hot) + dot_rows(a_lo[...], hot)
        return 0

    lax.fori_loop(0, LINES // GROUP, step, 0)
    table_ref[...] = jnp.zeros_like(table_ref)
    for high in range(HIGH):
        for half in range(2):
            at = 8 * (slot_of(high) * 2 + half)
            table_ref[at : at + 8, :] = acc_ref[
                high * 8 : high * 8 + 8, half * 128 : half * 128 + 128
            ]


def adjoint_kernel(row_ref, col_ref, value_ref, jac_ref, field_ref):
    field_ref[...] = jnp.zeros_like(field_ref)
    ids = lax.broadcasted_iota(jnp.int32, (LON_DEV, LINE), 0).astype(F32).astype(BF16)

    def step(g, _):
        rows = pl.ds(pl.multiple_of(g * GROUP, GROUP), GROUP)
        col = col_ref[rows, :].astype(F32)
        value = value_ref[rows, :]
        high = value.astype(BF16).astype(F32)
        low = value - high
        for j in range(GROUP):
            mask = ids == jnp.broadcast_to(col[j : j + 1], (LON_DEV, LINE)).astype(BF16)
            hot_hi = jnp.where(
                mask, jnp.broadcast_to(high[j : j + 1], (LON_DEV, LINE)).astype(BF16), jnp.zeros((), BF16)
            )
            hot_lo = jnp.where(
                mask, jnp.broadcast_to(low[j : j + 1], (LON_DEV, LINE)).astype(BF16), jnp.zeros((), BF16)
            )
            jac = jac_ref[pl.ds(pl.multiple_of(g * KSLOT + j * LINE, LINE), LINE), :]
            add = jnp.dot(hot_hi, jac, preferred_element_type=F32) + jnp.dot(
                hot_lo, jac, preferred_element_type=F32
            )
            at = row_ref[g * GROUP + j]
            field_ref[at] += add
        return 0

    lax.fori_loop(0, LINES // GROUP, step, 0)


def smoothed_row(mid, above, below, smoothing, size):
    left = pltpu.roll(mid, 1, 0)
    right = pltpu.roll(mid, size - 1, 0)
    return mid + smoothing * (above + below + left + right - 4.0 * mid)


WIDE = LON_DEV + 16


def forward_kernel(
    row_ref, edge_ref, field_ref, north_ref, south_ref, west_ref, east_ref, smooth_ref, col_ref, jac_ref,
    out_ref, seen_ref,
    ext_ref, mid_ref, f_hi, f_lo,
):
    ext_ref[...] = jnp.zeros_like(ext_ref)
    ext_ref[2 : LAT_DEV + 2, 8 : 8 + LON_DEV] = field_ref[...]
    ext_ref[0:2, 8 : 8 + LON_DEV] = north_ref[...]
    ext_ref[LAT_DEV + 2 : LAT_DEV + 4, 8 : 8 + LON_DEV] = south_ref[...]
    ext_ref[:, 6:8] = west_ref[...]
    ext_ref[:, 8 + LON_DEV : 10 + LON_DEV] = east_ref[...]
    smoothing = smooth_ref[...]

    def first(r, _):
        mid_ref[r] = smoothed_row(ext_ref[r + 1], ext_ref[r], ext_ref[r + 2], smoothing, WIDE)
        return 0

    lax.fori_loop(0, LAT_DEV + 2, first, 0)
    mid_ref[0] = mid_ref[0] * jnp.where(edge_ref[0] > 0, 1.0, 0.0)
    mid_ref[LAT_DEV + 1] = mid_ref[LAT_DEV + 1] * jnp.where(edge_ref[1] > 0, 1.0, 0.0)

    def second(r, _):
        mid = mid_ref[r + 1]
        twice = smoothed_row(mid, mid_ref[r], mid_ref[r + 2], smoothing, WIDE)
        out_ref[r] = mid[8 : 8 + LON_DEV]
        high, low = split(twice[8 : 8 + LON_DEV])
        f_hi[r] = high
        f_lo[r] = low
        return 0

    lax.fori_loop(0, LAT_DEV, second, 0)
    ids = lax.broadcasted_iota(jnp.int32, (LON_DEV, LINE), 0)

    def step(g, _):
        rows = pl.ds(pl.multiple_of(g * GROUP, GROUP), GROUP)
        col = col_ref[rows, :]
        seen = []
        for j in range(GROUP):
            jac = jac_ref[pl.ds(pl.multiple_of(g * KSLOT + j * LINE, LINE), LINE), :]
            at = row_ref[g * GROUP + j]
            grid = dot_rows(f_hi[at], jac) + dot_rows(f_lo[at], jac)
            mask = ids == jnp.broadcast_to(col[j : j + 1], (LON_DEV, LINE))
            seen.append(jnp.sum(jnp.where(mask, grid, 0.0), axis=0, keepdims=True))
        seen_ref[rows, :] = jnp.concatenate(seen, axis=0)
        return 0

    lax.fori_loop(0, LINES // GROUP, step, 0)


def lanes_of(values):
    lane = lax.broadcasted_iota(jnp.int32, (1, 128), 1)
    row = jnp.zeros((1, 128), F32)
    for i, value in enumerate(values):
        row = jnp.where(lane == i, value, row)
    return row


def total(x):
    return jnp.sum(jnp.sum(x, axis=0, keepdims=True), axis=1, keepdims=True)


def state_sums_kernel(
    field_ref, north_ref, south_ref, west_ref, east_ref, smooth_ref,
    source_ref, image1_ref, image2_ref, seen1_ref, seen2_ref,
    sums_ref,
    ext_ref,
):
    ext_ref[...] = jnp.zeros_like(ext_ref)
    ext_ref[1 : LAT_DEV + 1, 8 : 8 + LON_DEV] = field_ref[...]
    ext_ref[0:1, 8 : 8 + LON_DEV] = north_ref[...]
    ext_ref[LAT_DEV + 1 : LAT_DEV + 2, 8 : 8 + LON_DEV] = south_ref[...]
    ext_ref[1 : LAT_DEV + 1, 7:8] = west_ref[...]
    ext_ref[1 : LAT_DEV + 1, 8 + LON_DEV : 9 + LON_DEV] = east_ref[...]
    smoothing = smooth_ref[...]

    def first(r, acc):
        row = smoothed_row(ext_ref[r + 1], ext_ref[r], ext_ref[r + 2], smoothing, WIDE)
        row = row[8 : 8 + LON_DEV]
        return acc + row * row

    acc = lax.fori_loop(0, LAT_DEV, first, jnp.zeros((LON_DEV, LEV), F32))
    source, image1, image2 = (source_ref[...], image1_ref[...], image2_ref[...])
    seen1, seen2 = (seen1_ref[...], seen2_ref[...])
    sums_ref[...] = lanes_of(
        [
            total(seen1 * source),
            total(seen1 * image1),
            total(seen2 * image1),
            total(seen1 * image2),
            total(seen2 * image2),
            total(acc),
        ]
    )


def arrived_sum(ref, rows):
    acc = ref[0:24, :]
    for g in range(1, ref.shape[0] // 24):
        acc = acc + ref[24 * g : 24 * g + 24, :]
    out = acc[0:rows]
    for s in range(1, 24 // rows):
        out = out + acc[rows * s : rows * s + rows]
    return out


def to_everyone(rows, ref):
    tile = jnp.concatenate([rows] * (24 // rows.shape[0]), axis=0)
    for g in range(ref.shape[0] // 24):
        ref[24 * g : 24 * g + 24, :] = tile


def owner_start_kernel(arrived_ref, prior_ref, out_ref, own_ref):
    both = arrived_sum(arrived_ref, 2 * ROWS)
    res = jnp.concatenate([both[2 * i : 2 * i + 1] for i in range(ROWS)], axis=0)
    diag = jnp.concatenate([both[2 * i + 1 : 2 * i + 2] for i in range(ROWS)], axis=0)
    diag = diag + prior_ref[...]
    pre = res / diag
    own_ref[0:3] = res
    own_ref[3:6] = pre
    own_ref[6:9] = diag
    to_everyone(pre, out_ref)


def owner_next_kernel(arrived_ref, prior_ref, own_ref, out_ref, next_ref):
    image = arrived_sum(arrived_ref, ROWS) + prior_ref[...] * own_ref[3:6]
    pre = image / own_ref[6:9]
    next_ref[0:3] = image
    next_ref[3:6] = pre
    to_everyone(pre, out_ref)


def owner_last_kernel(arrived_ref, prior_ref, own_ref, next_ref, sums_ref, out_ref):
    res, pre = (own_ref[0:3], own_ref[3:6])
    image, image_pre = (next_ref[0:3], next_ref[3:6])
    last = arrived_sum(arrived_ref, ROWS) + prior_ref[...] * image_pre
    row = lanes_of(
        [jnp.zeros((1, 1), F32)] * 6
        + [
            total(res * pre),
            total(res * res),
            total(pre * image),
            total(image * image_pre),
            total(res * image),
            total(image * image),
            total(image_pre * last),
            total(res * last),
            total(image * last),
            total(last * last),
        ]
    )
    out_ref[...] = jnp.broadcast_to(row + sums_ref[...], out_ref.shape)


def finish_kernel(chan_ref, arrived_ref, a_ref, b_ref, pre_ref, image_pre_ref, x_ref, bias_ref, norm_ref):
    sums = jnp.sum(arrived_ref[...], axis=0, keepdims=True)
    lane = lax.broadcasted_iota(jnp.int32, (1, 128), 1)
    pick = [
        jnp.sum(jnp.where(lane == i, sums, 0.0), axis=1, keepdims=True) for i in range(16)
    ]
    aa, ab, bb, ac, bc, cc = pick[:6]
    rz_b, rr_b, zq_b, qw_b, rq_b, qq_b, wt_b, rt_b, qt_b, tt_b = pick[6:]
    state_qq = aa + 2.0 * ab + bb
    state_qc = ac + bc
    rz0 = aa + rz_b
    rr0 = aa + rr_b
    zq = aa + ab + zq_b
    qw = state_qq + qw_b
    rq = aa + ab + rq_b
    qq = state_qq + qq_b
    wt = state_qq + state_qc + wt_b
    rt = aa + ab + ac + rt_b
    qt = state_qq + state_qc + qt_b
    tt = state_qq + 2.0 * state_qc + cc + tt_b
    alpha0 = rz0 / zq
    rz1 = rz0 - 2.0 * alpha0 * zq + alpha0 * alpha0 * qw
    rr1 = rr0 - 2.0 * alpha0 * rq + alpha0 * alpha0 * qq
    beta = rz1 / rz0
    grow = 1.0 + beta
    pq = grow * grow * zq - 2.0 * alpha0 * grow * qw + alpha0 * alpha0 * wt
    alpha1 = rz1 / pq
    along = alpha0 + alpha1 * grow
    back = alpha0 * alpha1
    rr2 = (
        rr0
        - 2.0 * along * rq
        + 2.0 * back * rt
        + along * along * qq
        - 2.0 * along * back * qt
        + back * back * tt
    )
    norm_ref[...] = jnp.sqrt(jnp.maximum(lanes_of([rr0, rr1, rr2]), 0.0))
    coef_a = along - back
    x_ref[...] = coef_a[None] * a_ref[...] - back[None] * b_ref[...]
    start = chan_ref[0] * (PAD_HIGH * 16)
    for i in range(2 * CHAN_HIGH):
        rows = pl.ds(pl.multiple_of(start + 8 * i, 8), 8)
        bias_ref[:, 128 * i : 128 * i + 128] = along * pre_ref[rows, :] - back * image_pre_ref[rows, :]


def exchange(array, width):
    moved = lax.all_to_all(
        array.reshape(DEVICES, 1, width), OWNERS, split_axis=0, concat_axis=0, tiled=True
    )
    return moved.reshape(array.shape)


def halo(field, width):
    bands = lax.axis_size(SWATH)
    sectors = lax.axis_size("chan")
    north = lax.ppermute(field[LAT_DEV - width :], SWATH, [(i, i + 1) for i in range(bands - 1)])
    south = lax.ppermute(field[:width], SWATH, [(i + 1, i) for i in range(bands - 1)])

    def columns(part):
        if width == 1:
            return part(field)
        return jnp.concatenate([part(north), part(field), part(south)], axis=0)

    ring = [(i, (i + 1) % sectors) for i in range(sectors)]
    west = lax.ppermute(columns(lambda f: f[:, LON_DEV - width :]), "chan", ring)
    east = lax.ppermute(columns(lambda f: f[:, :width]), "chan", [(b, a) for a, b in ring])
    return north, south, west, east


def shape(*dims):
    return jax.ShapeDtypeStruct(dims, F32)


def body(
    innovations,
    obs_precision,
    jacobian,
    predictors,
    obs_column,
    obs_channel,
    obs_count,
    smoothing,
    bias_precision,
):
    band = lax.axis_index(SWATH)
    sector = lax.axis_index("chan")
    square = (LINES, LINE)
    chan = obs_channel.reshape(square)
    col_all = obs_column.reshape(square)
    line_row = col_all[:, 0] // LON_DEV
    col = col_all % LON_DEV
    smooth = smoothing.reshape(1, LEV)
    edges = jnp.stack([band > 0, band < lax.axis_size(SWATH) - 1]).astype(jnp.int32)
    prior = bias_precision.reshape(NPRED, 2 * CHAN_HIGH, 128).transpose(1, 0, 2).reshape(-1, 128)
    prior = jnp.pad(prior, ((0, 16), (0, 0)), constant_values=1.0)
    prior = lax.dynamic_slice_in_dim(prior, band * ROWS, ROWS, axis=0)
    field_shape = shape(LAT_DEV, LON_DEV, LEV)
    spread = pltpu.VMEM((HIGH * 8, KSLOT), BF16)
    table_acc = pltpu.VMEM((HIGH * 8, LOW), F32)
    hot = pltpu.VMEM((LOW, KSLOT), BF16)

    table0, weights, source = call(
        table_start_kernel,
        (shape(2 * TABLE, 128), shape(*square), shape(*square)),
        [SMEM] + [VMEM] * 4,
        (obs_count, innovations.reshape(square), obs_precision.reshape(square), predictors, chan),
        [hot, spread, spread, spread, spread, table_acc, table_acc],
        flops=4 * 10**9,
        name="table_start",
    )

    def adjoint(values):
        return call(
            adjoint_kernel,
            field_shape,
            [SMEM] + [VMEM] * 3,
            (line_row, col, values, jacobian),
            flops=2 * 10**9,
            name="adjoint",
        )

    def forward(field):
        wide = pltpu.VMEM((LAT_DEV + 4, WIDE, LEV), F32)
        mid = pltpu.VMEM((LAT_DEV + 2, WIDE, LEV), F32)
        half = pltpu.VMEM((LAT_DEV, LON_DEV, LEV), BF16)
        return call(
            forward_kernel,
            (field_shape, shape(*square)),
            [SMEM, SMEM] + [VMEM] * 8,
            (line_row, edges, field, *halo(field, 2), smooth, col, jacobian),
            [wide, mid, half, half],
            flops=2 * 10**9,
            name="forward",
        )

    def image_of(coefs, state):
        return call(
            image_kernel,
            (shape(TABLE, 128), shape(*square)),
            [VMEM] * 5,
            (coefs, weights, state, predictors, chan),
            [
                hot,
                pltpu.VMEM((HIGH * 8, KSLOT), F32),
                pltpu.VMEM((HIGH * 8, LOW), BF16),
                pltpu.VMEM((HIGH * 8, LOW), BF16),
                spread,
                spread,
                table_acc,
            ],
            flops=4 * 10**9,
            name="image",
        )

    arrived0 = exchange(table0, 2 * ROWS * 128)
    send0, own = call(
        owner_start_kernel, (shape(TABLE, 128), shape(9, 128)), [VMEM] * 2, (arrived0, prior), name="owner_start"
    )
    pre = exchange(send0, ROWS * 128)
    a_field, seen1 = forward(adjoint(source))
    table1, image1 = image_of(pre, seen1)
    arrived1 = exchange(table1, ROWS * 128)
    send1, own_next = call(
        owner_next_kernel, (shape(TABLE, 128), shape(6, 128)), [VMEM] * 3, (arrived1, prior, own), name="owner_next"
    )
    image_pre = exchange(send1, ROWS * 128)
    b_field, seen2 = forward(adjoint(image1))
    table2, image2 = image_of(image_pre, seen1 + seen2)
    arrived2 = exchange(table2, ROWS * 128)
    last = adjoint(image2)
    sums = call(
        state_sums_kernel,
        shape(1, 128),
        [VMEM] * 11,
        (last, *halo(last, 1), smooth, source, image1, image2, seen1, seen2),
        [pltpu.VMEM((LAT_DEV + 2, WIDE, LEV), F32)],
        name="state_sums",
    )
    send2 = call(
        owner_last_kernel,
        shape(DEVICES, 128),
        [VMEM] * 5,
        (arrived2, prior, own, own_next, sums),
        name="owner_last",
    )
    arrived3 = exchange(send2, 128)
    state, bias, norms = call(
        finish_kernel,
        (field_shape, shape(NPRED, 2 * CHAN_HIGH * 128), shape(1, 128)),
        [SMEM] + [VMEM] * 5,
        (sector.reshape(1), arrived3, a_field, b_field, pre, image_pre),
        name="finish",
    )
    return state, bias, norms[0, :3]


def solution(mesh):
    torus = Mesh(
        mesh.devices.reshape(4, 4, 2, mesh.shape["chan"]), ("swath_0", "swath_1", "swath_2", "chan")
    )
    placed = (
        P(SWATH_CHAN),
        P(SWATH_CHAN),
        P(SWATH_CHAN, None),
        P(None, SWATH_CHAN),
        P(SWATH_CHAN),
        P(SWATH_CHAN),
        P(SWATH, "chan"),
        P(),
        P(None, "chan"),
    )
    return jax.shard_map(
        body,
        mesh=torus,
        in_specs=placed,
        out_specs=(P(SWATH, "chan", None), P(None, "chan"), P()),
        check_vma=False,
    )
```

profile of v0, /device:TPU:1, one launch (start us, length us, event | category | flops | bytes accessed | tf_op | source)
XLA Modules:
  0.0 204.9 jit_solution(18038343175245082199)
XLA Ops:
  1.3 1.0 copy-done.5
  2.3 0.8 copy-done.7
  3.2 0.8 copy-done.8
  4.0 0.8 copy-done.9
  4.8 14.8 %table_start.1 = (f32[768,128]{1,0:T(8,128)}, f32[128,128]{1,0:T(8,128)S(1)}, f32[128,128]{1,0:T(8,128)S(1)}) custom-call(s32[1,1]{1,0:T(1,128)S(6)} %copy.18.count_ref, f32[128,128]{1,0:T(8,128)S(1)} %bitcast.38, f32[128,128]{1,0:T(8,128)S(1)} %bitcast.39, f32[8,16384]{1,0:T(8,128)S(1)} %copy-done.5, s32[128,128]{1,0:T(8,128)S(1)} %bitcast.40), custom_call_target="tpu_custom_call" | custom-call | flops 4000000000 | bytes 4194304 | tf_op jit(solution)/shard_map/table_start/pallas_call | solution.py:39
  20.3 11.5 %all-to-all-start = ((f32[128,1,768]{2,1,0:T(1,128)}), f32[128,1,768]{2,1,0:T(1,128)S(1)}, u32[]{:S(2)}, u32[]{:S(2)}) async-start(f32[128,1,768]{2,1,0:T(1,128)} %bitcast.4), calls=%async_computation | async-start | bytes 786432 | tf_op jit(solution)/shard_map/all_to_all | solution.py:426
  31.9 2.2 %copy-done = bf16[16384,128]{1,0:T(8,128)(2,1)S(1)} copy-done((bf16[16384,128]{1,0:T(8,128)(2,1)S(1)}, bf16[16384,128]{1,0:T(8,128)(2,1)}, u32[]{:S(2)}) %copy-start) | copy-done | bytes 4194328
  34.1 5.0 %adjoint.3.field_ref = f32[32,64,128]{2,1,0:T(8,128)S(1)} custom-call(s32[128]{0:T(128)S(1)} %and_select_fusion.row_ref, s32[128,128]{1,0:T(8,128)S(1)} %add_select_fusion.col_ref, f32[128,128]{1,0:T(8,128)S(1)} %get-tuple-element.24.value_ref.source_ref, bf16[16384,128]{1,0:T(8,128)(2,1)S(1)} %copy-done), custom_call_target="tpu_custom_call" | custom-call | flops 2000000000 | bytes 4194304 | tf_op jit(solution)/shard_map/adjoint/pallas_call | solution.py:39
  39.2 3.6 %collective-permute-start = (f32[2,64,128]{2,1,0:T(8,128)S(1)}, f32[2,64,128]{2,1,0:T(8,128)S(1)}, u32[]{:S(2)}, u32[]{:S(2)}) collective-permute-start(f32[2,64,128]{2,1,0:T(8,128)S(1)} %get-tuple-element.50), channel_id=1, source_target_pairs={{0,4},{4,8},{8,12},{12,16},{16,20},{20,24},{24,28},{28,32},{32,36}... | collective-permute-start | bytes 196616 | tf_op jit(solution)/shard_map/ppermute | solution.py:435
  42.8 1.9 collective-permute-start.1
  44.8 3.6 %collective-permute-done.1.south_ref = f32[2,64,128]{2,1,0:T(8,128)S(1)} collective-permute-done((f32[2,64,128]{2,1,0:T(8,128)S(1)}, f32[2,64,128]{2,1,0:T(8,128)S(1)}, u32[]{:S(2)}, u32[]{:S(2)}) %collective-permute-start.1) | collective-permute-done | bytes 65568 | tf_op jit(solution)/shard_map/ppermute | solution.py:436
  48.4 1.4 collective-permute-start.2
  49.8 1.8 collective-permute-start.3
  51.7 0.7 owner_start.1
  52.4 9.0 %all-to-all-start.1 = ((f32[128,1,384]{2,1,0:T(1,128)}), f32[128,1,384]{2,1,0:T(1,128)S(1)}, u32[]{:S(2)}, u32[]{:S(2)}) async-start(f32[128,1,384]{2,1,0:T(1,128)} %bitcast.9), calls=%async_computation.1 | async-start | bytes 393216 | tf_op jit(solution)/shard_map/all_to_all | solution.py:426
  61.6 2.2 %copy-done.1 = bf16[16384,128]{1,0:T(8,128)(2,1)S(1)} copy-done((bf16[16384,128]{1,0:T(8,128)(2,1)S(1)}, bf16[16384,128]{1,0:T(8,128)(2,1)}, u32[]{:S(2)}) %copy-start.1) | copy-done | bytes 4194328
  63.8 9.6 %forward.2 = (f32[32,64,128]{2,1,0:T(8,128)S(1)}, f32[128,128]{1,0:T(8,128)S(1)}) custom-call(s32[128]{0:T(128)S(1)} %and_select_fusion.row_ref, s32[2]{0:T(128)S(1)} %add_convert_fusion.edge_ref, f32[32,64,128]{2,1,0:T(8,128)S(1)} %adjoint.3.field_ref, f32[2,64,128]{2,1,0:T(8,128)S(1)} %collective-permute-done.north_ref, ...), custom_call_target="tpu_custom_call" | custom-call | flops 2000000000 | bytes 4194304 | tf_op jit(solution)/shard_map/forward/pallas_call | solution.py:39
  73.4 15.1 %image.2 = (f32[384,128]{1,0:T(8,128)}, f32[128,128]{1,0:T(8,128)S(1)}) custom-call(f32[384,128]{1,0:T(8,128)S(1)} %bitcast.31, f32[128,128]{1,0:T(8,128)S(1)} %copy-done.19, f32[128,128]{1,0:T(8,128)S(1)} %get-tuple-element.25.state_ref.seen1_ref, f32[8,16384]{1,0:T(8,128)S(1)} %copy-done.6, s32[128,128]{1,0:T(8,128)S(1)} %bitcast.41), custom_call_target="tpu_custom_call" | custom-call | flops 4000000000 | bytes 4194304 | tf_op jit(solution)/shard_map/image/pallas_call | solution.py:39
  88.6 5.0 %adjoint.4.field_ref = f32[32,64,128]{2,1,0:T(8,128)S(1)} custom-call(s32[128]{0:T(128)S(1)} %and_select_fusion.row_ref, s32[128,128]{1,0:T(8,128)S(1)} %add_select_fusion.col_ref, f32[128,128]{1,0:T(8,128)S(1)} %get-tuple-element.29.value_ref.image1_ref, bf16[16384,128]{1,0:T(8,128)(2,1)S(1)} %copy-done.2), custom_call_target="tpu_custom_call" | custom-call | flops 2000000000 | bytes 4194304 | tf_op jit(solution)/shard_map/adjoint/pallas_call | solution.py:39
  93.6 0.7 fusion.4
  94.2 3.0 %collective-permute-start.5 = (f32[2,64,128]{2,1,0:T(8,128)}, f32[2,64,128]{2,1,0:T(8,128)S(1)}, u32[]{:S(2)}, u32[]{:S(2)}) collective-permute-start(f32[2,64,128]{2,1,0:T(8,128)} %get-tuple-element.45), channel_id=1, source_target_pairs={{4,0},{8,4},{12,8},{16,12},{20,16},{24,20},{28,24},{32,28},{36,32}... | collective-permute-start | bytes 196616 | tf_op jit(solution)/shard_map/ppermute | solution.py:436
  97.3 9.0 %all-to-all-start.2 = ((f32[128,1,384]{2,1,0:T(1,128)}), f32[128,1,384]{2,1,0:T(1,128)S(1)}, u32[]{:S(2)}, u32[]{:S(2)}) async-start(f32[128,1,384]{2,1,0:T(1,128)} %bitcast.15), calls=%async_computation.2 | async-start | bytes 393216 | tf_op jit(solution)/shard_map/all_to_all | solution.py:426
  106.3 3.5 %collective-permute-start.4 = (f32[2,64,128]{2,1,0:T(8,128)}, f32[2,64,128]{2,1,0:T(8,128)S(1)}, u32[]{:S(2)}, u32[]{:S(2)}) collective-permute-start(f32[2,64,128]{2,1,0:T(8,128)} %get-tuple-element.46), channel_id=1, source_target_pairs={{0,4},{4,8},{8,12},{12,16},{16,20},{20,24},{24,28},{28,32},{32,36}... | collective-permute-start | bytes 196616 | tf_op jit(solution)/shard_map/ppermute | solution.py:435
  109.8 1.6 collective-permute-done.4.north_ref
  111.5 1.4 collective-permute-start.6
  112.9 0.6 pad_maximum_fusion.3
  113.5 1.8 collective-permute-start.7
  115.3 1.5 all-to-all-done.2
  116.8 0.7 owner_next.1
  117.5 7.8 %all-to-all-start.3 = ((f32[128,1,384]{2,1,0:T(1,128)}), f32[128,1,384]{2,1,0:T(1,128)S(1)}, u32[]{:S(2)}, u32[]{:S(2)}) async-start(f32[128,1,384]{2,1,0:T(1,128)} %bitcast.17), calls=%async_computation.3 | async-start | bytes 393216 | tf_op jit(solution)/shard_map/all_to_all | solution.py:426
  125.3 2.2 %copy-done.3 = bf16[16384,128]{1,0:T(8,128)(2,1)S(1)} copy-done((bf16[16384,128]{1,0:T(8,128)(2,1)S(1)}, bf16[16384,128]{1,0:T(8,128)(2,1)}, u32[]{:S(2)}) %copy-start.3) | copy-done | bytes 4194328
  127.5 9.6 %forward.3 = (f32[32,64,128]{2,1,0:T(8,128)S(1)}, f32[128,128]{1,0:T(8,128)S(1)}) custom-call(s32[128]{0:T(128)S(1)} %and_select_fusion.row_ref, s32[2]{0:T(128)S(1)} %add_convert_fusion.edge_ref, f32[32,64,128]{2,1,0:T(8,128)S(1)} %adjoint.4.field_ref, f32[2,64,128]{2,1,0:T(8,128)S(1)} %collective-permute-done.4.north_ref, ...), custom_call_target="tpu_custom_call" | custom-call | flops 2000000000 | bytes 4194304 | tf_op jit(solution)/shard_map/forward/pallas_call | solution.py:39
  137.2 1.0 copy-done.12
  138.1 0.8 copy-done.20
  139.0 15.1 %image.3 = (f32[384,128]{1,0:T(8,128)}, f32[128,128]{1,0:T(8,128)S(1)}) custom-call(f32[384,128]{1,0:T(8,128)S(1)} %bitcast.33, f32[128,128]{1,0:T(8,128)S(1)} %copy-done.20, f32[128,128]{1,0:T(8,128)S(1)} %add.25.state_ref, f32[8,16384]{1,0:T(8,128)S(1)} %copy-done.6, s32[128,128]{1,0:T(8,128)S(1)} %bitcast.42), custom_call_target="tpu_custom_call" | custom-call | flops 4000000000 | bytes 4194304 | tf_op jit(solution)/shard_map/image/pallas_call | solution.py:39
  154.1 9.8 %all-to-all-start.4 = ((f32[128,1,384]{2,1,0:T(1,128)}), f32[128,1,384]{2,1,0:T(1,128)S(1)}, u32[]{:S(2)}, u32[]{:S(2)}) async-start(f32[128,1,384]{2,1,0:T(1,128)} %bitcast.19), calls=%async_computation.4 | async-start | bytes 393216 | tf_op jit(solution)/shard_map/all_to_all | solution.py:426
  163.9 2.2 %copy-done.4 = bf16[16384,128]{1,0:T(8,128)(2,1)S(1)} copy-done((bf16[16384,128]{1,0:T(8,128)(2,1)S(1)}, bf16[16384,128]{1,0:T(8,128)(2,1)}, u32[]{:S(2)}) %copy-start.4) | copy-done | bytes 4194328
  166.0 5.0 %adjoint.5.field_ref = f32[32,64,128]{2,1,0:T(8,128)S(1)} custom-call(s32[128]{0:T(128)S(1)} %and_select_fusion.row_ref, s32[128,128]{1,0:T(8,128)S(1)} %add_select_fusion.col_ref, f32[128,128]{1,0:T(8,128)S(1)} %get-tuple-element.33.value_ref.image2_ref, bf16[16384,128]{1,0:T(8,128)(2,1)S(1)} %copy-done.4), custom_call_target="tpu_custom_call" | custom-call | flops 2000000000 | bytes 4194304 | tf_op jit(solution)/shard_map/adjoint/pallas_call | solution.py:39
  171.1 3.7 %collective-permute-start.8 = (f32[1,64,128]{2,1,0:T(8,128)S(1)}, f32[1,64,128]{2,1,0:T(8,128)S(1)}, u32[]{:S(2)}, u32[]{:S(2)}) collective-permute-start(f32[1,64,128]{2,1,0:T(8,128)S(1)} %get-tuple-element.42), channel_id=1, source_target_pairs={{0,4},{4,8},{8,12},{12,16},{16,20},{20,24},{24,28},{28,32},{32,36}... | collective-permute-start | bytes 98312 | tf_op jit(solution)/shard_map/ppermute | solution.py:435
  174.8 1.9 collective-permute-start.9
  176.8 1.4 collective-permute-start.10
  178.2 1.8 collective-permute-start.11
  180.0 1.0 collective-permute-done.10.west_ref
  181.1 0.8 state_sums.1.sums_ref
  181.9 0.7 owner_last.1
  182.6 10.8 %all-to-all-start.5 = ((f32[128,1,128]{2,1,0:T(1,128)}), f32[128,1,128]{2,1,0:T(1,128)S(1)}, u32[]{:S(2)}, u32[]{:S(2)}) async-start(f32[128,1,128]{2,1,0:T(1,128)} %bitcast.22), calls=%async_computation.5 | async-start | bytes 131072 | tf_op jit(solution)/shard_map/all_to_all | solution.py:426
  193.4 9.6 %all-to-all-done.5 = f32[128,1,128]{2,1,0:T(1,128)S(1)} async-done(((f32[128,1,128]{2,1,0:T(1,128)}), f32[128,1,128]{2,1,0:T(1,128)S(1)}, u32[]{:S(2)}, u32[]{:S(2)}) %all-to-all-start.5) | async-done | bytes 65568 | tf_op jit(solution)/shard_map/all_to_all | solution.py:426
  203.1 1.3 finish.1
  (68 shorter events, 1.7 us)
Async XLA Ops:
  1.3 1.0 copy-start.5
  2.3 0.8 copy-start.7
  3.2 0.8 copy-start.8
  4.0 0.8 copy-start.9
  4.8 26.9 %copy-start.21 = (s32[16384]{0:T(1024)S(1)}, s32[16384]{0:T(1024)}, u32[]{:S(2)}) copy-start(s32[16384]{0:T(1024)} %param.13) | copy-start | bytes 196612
  19.6 0.6 copy-start.18
  20.2 18.9 %copy-start.14 = (f32[128,128]{1,0:T(8,128)}, f32[128,128]{1,0:T(8,128)S(1)}, u32[]{:S(2)}) copy-start(f32[128,128]{1,0:T(8,128)S(1)} %get-tuple-element.24.value_ref.source_ref) | copy-start | bytes 196612
  20.3 31.4 %all-to-all-start = ((f32[128,1,768]{2,1,0:T(1,128)}), f32[128,1,768]{2,1,0:T(1,128)S(1)}, u32[]{:S(2)}, u32[]{:S(2)}) async-start(f32[128,1,768]{2,1,0:T(1,128)} %bitcast.4), calls=%async_computation | async-start | bytes 786432 | tf_op jit(solution)/shard_map/all_to_all | solution.py:426
  31.8 13.0 %copy-start.22 = (f32[8,1280]{1,0:T(8,128)S(1)}, f32[8,1280]{1,0:T(8,128)}, u32[]{:S(2)}) copy-start(f32[8,1280]{1,0:T(8,128)} %param.17) | copy-start | bytes 122884
  31.9 2.2 %copy-start = (bf16[16384,128]{1,0:T(8,128)(2,1)S(1)}, bf16[16384,128]{1,0:T(8,128)(2,1)}, u32[]{:S(2)}) copy-start(bf16[16384,128]{1,0:T(8,128)(2,1)} %jac_ref.9) | copy-start | bytes 12582916
  39.2 22.4 %copy-start.11 = (f32[128]{0:T(128)S(1)}, f32[128]{0:T(128)}, u32[]{:S(2)}) copy-start(f32[128]{0:T(128)} %param.16) | copy-start | bytes 1540
  39.2 9.2 %collective-permute-start = (f32[2,64,128]{2,1,0:T(8,128)S(1)}, f32[2,64,128]{2,1,0:T(8,128)S(1)}, u32[]{:S(2)}, u32[]{:S(2)}) collective-permute-start(f32[2,64,128]{2,1,0:T(8,128)S(1)} %get-tuple-element.50), channel_id=1, source_target_pairs={{0,4},{4,8},{8,12},{12,16},{16,20},{20,24},{24,28},{28,32},{32,36}... | collective-permute-start | bytes 196616 | tf_op jit(solution)/shard_map/ppermute | solution.py:435
  42.8 5.6 %collective-permute-start.1 = (f32[2,64,128]{2,1,0:T(8,128)S(1)}, f32[2,64,128]{2,1,0:T(8,128)S(1)}, u32[]{:S(2)}, u32[]{:S(2)}) collective-permute-start(f32[2,64,128]{2,1,0:T(8,128)S(1)} %get-tuple-element.49), channel_id=1, source_target_pairs={{4,0},{8,4},{12,8},{16,12},{20,16},{24,20},{28,24},{32,28},{36,32}... | collective-permute-start | bytes 196616 | tf_op jit(solution)/shard_map/ppermute | solution.py:436
  48.4 13.2 %collective-permute-start.2 = (f32[36,2,128]{2,1,0:T(2,128)S(1)}, f32[36,2,128]{2,1,0:T(2,128)S(1)}, u32[]{:S(2)}, u32[]{:S(2)}) collective-permute-start(f32[36,2,128]{2,1,0:T(2,128)S(1)} %pad_maximum_fusion), channel_id=1, source_target_pairs={{0,1},{1,2},{2,3},{3,0},{4,5},{5,6},{6,7},{7,4},{8,9},{9,10},{10,1... | collective-permute-start | bytes 110600 | tf_op jit(solution)/shard_map/ppermute | solution.py:444
  49.8 11.7 %collective-permute-start.3 = (f32[36,2,128]{2,1,0:T(2,128)S(1)}, f32[36,2,128]{2,1,0:T(2,128)S(1)}, u32[]{:S(2)}, u32[]{:S(2)}) collective-permute-start(f32[36,2,128]{2,1,0:T(2,128)S(1)} %pad_maximum_fusion.1), channel_id=1, source_target_pairs={{1,0},{2,1},{3,2},{0,3},{5,4},{6,5},{7,6},{4,7},{9,8},{10,9},{11,1... | collective-permute-start | bytes 110600 | tf_op jit(solution)/shard_map/ppermute | solution.py:445
  51.7 21.7 %copy-start.6 = (f32[8,16384]{1,0:T(8,128)S(1)}, f32[8,16384]{1,0:T(8,128)}, u32[]{:S(2)}) copy-start(f32[8,16384]{1,0:T(8,128)} %pred_ref.5) | copy-start | bytes 1572868
  52.4 21.0 %copy-start.10 = (s32[16384]{0:T(1024)S(1)}, s32[16384]{0:T(1024)}, u32[]{:S(2)}) copy-start(s32[16384]{0:T(1024)} %param.14) | copy-start | bytes 196612
  52.4 21.0 %copy-start.19 = (f32[128,128]{1,0:T(8,128)S(1)}, f32[128,128]{1,0:T(8,128)}, u32[]{:S(2)}) copy-start(f32[128,128]{1,0:T(8,128)} %copy-done.18) | copy-start | bytes 196612
  52.4 21.0 %all-to-all-start.1 = ((f32[128,1,384]{2,1,0:T(1,128)}), f32[128,1,384]{2,1,0:T(1,128)S(1)}, u32[]{:S(2)}, u32[]{:S(2)}) async-start(f32[128,1,384]{2,1,0:T(1,128)} %bitcast.9), calls=%async_computation.1 | async-start | bytes 393216 | tf_op jit(solution)/shard_map/all_to_all | solution.py:426
  61.6 2.2 %copy-start.1 = (bf16[16384,128]{1,0:T(8,128)(2,1)S(1)}, bf16[16384,128]{1,0:T(8,128)(2,1)}, u32[]{:S(2)}) copy-start(bf16[16384,128]{1,0:T(8,128)(2,1)} %jac_ref.9) | copy-start | bytes 12582916
  73.4 15.1 %copy-start.2 = (bf16[16384,128]{1,0:T(8,128)(2,1)S(1)}, bf16[16384,128]{1,0:T(8,128)(2,1)}, u32[]{:S(2)}) copy-start(bf16[16384,128]{1,0:T(8,128)(2,1)} %jac_ref.9) | copy-start | bytes 12582916
  88.5 28.9 %copy-start.16 = (f32[128,128]{1,0:T(8,128)}, f32[128,128]{1,0:T(8,128)S(1)}, u32[]{:S(2)}) copy-start(f32[128,128]{1,0:T(8,128)S(1)} %get-tuple-element.29.value_ref.image1_ref) | copy-start | bytes 196612
  94.2 15.6 %collective-permute-start.5 = (f32[2,64,128]{2,1,0:T(8,128)}, f32[2,64,128]{2,1,0:T(8,128)S(1)}, u32[]{:S(2)}, u32[]{:S(2)}) collective-permute-start(f32[2,64,128]{2,1,0:T(8,128)} %get-tuple-element.45), channel_id=1, source_target_pairs={{4,0},{8,4},{12,8},{16,12},{20,16},{24,20},{28,24},{32,28},{36,32}... | collective-permute-start | bytes 196616 | tf_op jit(solution)/shard_map/ppermute | solution.py:436
  97.3 19.5 %all-to-all-start.2 = ((f32[128,1,384]{2,1,0:T(1,128)}), f32[128,1,384]{2,1,0:T(1,128)S(1)}, u32[]{:S(2)}, u32[]{:S(2)}) async-start(f32[128,1,384]{2,1,0:T(1,128)} %bitcast.15), calls=%async_computation.2 | async-start | bytes 393216 | tf_op jit(solution)/shard_map/all_to_all | solution.py:426
  106.3 5.2 %collective-permute-start.4 = (f32[2,64,128]{2,1,0:T(8,128)}, f32[2,64,128]{2,1,0:T(8,128)S(1)}, u32[]{:S(2)}, u32[]{:S(2)}) collective-permute-start(f32[2,64,128]{2,1,0:T(8,128)} %get-tuple-element.46), channel_id=1, source_target_pairs={{0,4},{4,8},{8,12},{12,16},{16,20},{20,24},{24,28},{28,32},{32,36}... | collective-permute-start | bytes 196616 | tf_op jit(solution)/shard_map/ppermute | solution.py:435
  111.5 13.8 %collective-permute-start.6 = (f32[36,2,128]{2,1,0:T(2,128)S(1)}, f32[36,2,128]{2,1,0:T(2,128)S(1)}, u32[]{:S(2)}, u32[]{:S(2)}) collective-permute-start(f32[36,2,128]{2,1,0:T(2,128)S(1)} %pad_maximum_fusion.2), channel_id=1, source_target_pairs={{0,1},{1,2},{2,3},{3,0},{4,5},{5,6},{6,7},{7,4},{8,9},{9,10},{10,1... | collective-permute-start | bytes 110600 | tf_op jit(solution)/shard_map/ppermute | solution.py:444
  113.5 11.8 %collective-permute-start.7 = (f32[36,2,128]{2,1,0:T(2,128)}, f32[36,2,128]{2,1,0:T(2,128)S(1)}, u32[]{:S(2)}, u32[]{:S(2)}) collective-permute-start(f32[36,2,128]{2,1,0:T(2,128)} %pad_maximum_fusion.3), channel_id=1, source_target_pairs={{1,0},{2,1},{3,2},{0,3},{5,4},{6,5},{7,6},{4,7},{9,8},{10,9},{11,1... | collective-permute-start | bytes 110600 | tf_op jit(solution)/shard_map/ppermute | solution.py:445
  117.5 20.6 %all-to-all-start.3 = ((f32[128,1,384]{2,1,0:T(1,128)}), f32[128,1,384]{2,1,0:T(1,128)S(1)}, u32[]{:S(2)}, u32[]{:S(2)}) async-start(f32[128,1,384]{2,1,0:T(1,128)} %bitcast.17), calls=%async_computation.3 | async-start | bytes 393216 | tf_op jit(solution)/shard_map/all_to_all | solution.py:426
  125.3 2.2 %copy-start.3 = (bf16[16384,128]{1,0:T(8,128)(2,1)S(1)}, bf16[16384,128]{1,0:T(8,128)(2,1)}, u32[]{:S(2)}) copy-start(bf16[16384,128]{1,0:T(8,128)(2,1)} %jac_ref.9) | copy-start | bytes 12582916
  137.1 1.0 copy-start.12
  138.1 0.8 copy-start.20
  154.1 27.0 %copy-start.15 = (f32[128,128]{1,0:T(8,128)S(1)}, f32[128,128]{1,0:T(8,128)}, u32[]{:S(2)}) copy-start(f32[128,128]{1,0:T(8,128)} %copy-done.14) | copy-start | bytes 196612
  154.1 27.0 %copy-start.17 = (f32[128,128]{1,0:T(8,128)S(1)}, f32[128,128]{1,0:T(8,128)}, u32[]{:S(2)}) copy-start(f32[128,128]{1,0:T(8,128)} %copy-done.16) | copy-start | bytes 196612
  154.1 27.8 %all-to-all-start.4 = ((f32[128,1,384]{2,1,0:T(1,128)}), f32[128,1,384]{2,1,0:T(1,128)S(1)}, u32[]{:S(2)}, u32[]{:S(2)}) async-start(f32[128,1,384]{2,1,0:T(1,128)} %bitcast.19), calls=%async_computation.4 | async-start | bytes 393216 | tf_op jit(solution)/shard_map/all_to_all | solution.py:426
  163.8 2.2 %copy-start.4 = (bf16[16384,128]{1,0:T(8,128)(2,1)S(1)}, bf16[16384,128]{1,0:T(8,128)(2,1)}, u32[]{:S(2)}) copy-start(bf16[16384,128]{1,0:T(8,128)(2,1)} %jac_ref.9) | copy-start | bytes 12582916
  171.1 32.0 %copy-start.13 = (f32[32,64,128]{2,1,0:T(8,128)S(1)}, f32[32,64,128]{2,1,0:T(8,128)}, u32[]{:S(2)}) copy-start(f32[32,64,128]{2,1,0:T(8,128)} %copy-done.12) | copy-start | bytes 3145732
  171.1 10.0 %collective-permute-start.8 = (f32[1,64,128]{2,1,0:T(8,128)S(1)}, f32[1,64,128]{2,1,0:T(8,128)S(1)}, u32[]{:S(2)}, u32[]{:S(2)}) collective-permute-start(f32[1,64,128]{2,1,0:T(8,128)S(1)} %get-tuple-element.42), channel_id=1, source_target_pairs={{0,4},{4,8},{8,12},{12,16},{16,20},{20,24},{24,28},{28,32},{32,36}... | collective-permute-start | bytes 98312 | tf_op jit(solution)/shard_map/ppermute | solution.py:435
  174.8 6.3 %collective-permute-start.9 = (f32[1,64,128]{2,1,0:T(8,128)S(1)}, f32[1,64,128]{2,1,0:T(8,128)S(1)}, u32[]{:S(2)}, u32[]{:S(2)}) collective-permute-start(f32[1,64,128]{2,1,0:T(8,128)S(1)} %get-tuple-element.41), channel_id=1, source_target_pairs={{4,0},{8,4},{12,8},{16,12},{20,16},{24,20},{28,24},{32,28},{36,32}... | collective-permute-start | bytes 98312 | tf_op jit(solution)/shard_map/ppermute | solution.py:436
  176.8 4.3 %collective-permute-start.10 = (f32[32,1,128]{2,1,0:T(1,128)S(1)}, f32[32,1,128]{2,1,0:T(1,128)S(1)}, u32[]{:S(2)}, u32[]{:S(2)}) collective-permute-start(f32[32,1,128]{2,1,0:T(1,128)S(1)} %get-tuple-element.40), channel_id=1, source_target_pairs={{0,1},{1,2},{2,3},{3,0},{4,5},{5,6},{6,7},{7,4},{8,9},{9,10},{10,1... | collective-permute-start | bytes 49160 | tf_op jit(solution)/shard_map/ppermute | solution.py:444
  178.2 2.9 %collective-permute-start.11 = (f32[32,1,128]{2,1,0:T(1,128)S(1)}, f32[32,1,128]{2,1,0:T(1,128)S(1)}, u32[]{:S(2)}, u32[]{:S(2)}) collective-permute-start(f32[32,1,128]{2,1,0:T(1,128)S(1)} %get-tuple-element.39), channel_id=1, source_target_pairs={{1,0},{2,1},{3,2},{0,3},{5,4},{6,5},{7,6},{4,7},{9,8},{10,9},{11,1... | collective-permute-start | bytes 49160 | tf_op jit(solution)/shard_map/ppermute | solution.py:445
  182.6 20.4 %all-to-all-start.5 = ((f32[128,1,128]{2,1,0:T(1,128)}), f32[128,1,128]{2,1,0:T(1,128)S(1)}, u32[]{:S(2)}, u32[]{:S(2)}) async-start(f32[128,1,128]{2,1,0:T(1,128)} %bitcast.22), calls=%async_computation.5 | async-start | bytes 131072 | tf_op jit(solution)/shard_map/all_to_all | solution.py:426
where the time goes:
time: 206 us; the launch traced here: 205 us
  starting transfers between devices  85.2 us (41%)
  Pallas kernels  83.6 us (41%)
  waiting for transfers between devices  17.4 us (8%)
  local copies, waits for them, and re-layouts  16.2 us (8%)
    pallas_call x13, Pallas kernels, call(): pl.pallas_call(kernel, out_shape=out_shape, in_specs=in_specs, out_specs=...  83.6 us
    all_to_all x6, starting transfers between devices, exchange(): lax.all_to_all(array.reshape(DEVICES, 1, width), OWNERS, split_axis=0, co...  57.9 us
    unnamed x46, local copies, waits for them, and re-layouts  14.8 us
    all_to_all x6, waiting for transfers between devices, exchange(): lax.all_to_all(array.reshape(DEVICES, 1, width), OWNERS, split_axis=0, co...  11.1 us
    ppermute x3, starting transfers between devices, halo(): lax.ppermute(field[LAT_DEV - width:], SWATH, [(i, i + 1) for i in range(b...  10.8 us
    ppermute x3, starting transfers between devices, halo(): lax.ppermute(field[:width], SWATH, [(i + 1, i) for i in range(bands - 1)])  6.8 us
    ppermute x3, starting transfers between devices, halo(): lax.ppermute(columns(lambda f: f[:, :width]), 'chan', [(b, a) for a, b in...  5.43 us
    ppermute x3, starting transfers between devices, halo(): west = lax.ppermute(columns(lambda f: f[:, LON_DEV - width:]), 'chan', ring)  4.29 us
  transfers between devices with their start and end apart: 18, of which 5 were waited for; matrix products, arithmetic and copies ran while one was open for 1% of the time, Pallas kernels for 15%

commit v1 on v0

v1 whole, which is shorter than its diff:
```python
import functools

import jax
import jax.numpy as jnp
from jax import lax
from jax.experimental import pallas as pl
from jax.experimental.pallas import tpu as pltpu
from jax.sharding import Mesh
from jax.sharding import PartitionSpec as P

LEV = 128
NPRED = 8
LINE = 128
LAT_DEV = 32
LON_DEV = 64
SLOTS = 16384
LINES = SLOTS // LINE
GROUP = 8
KSLOT = GROUP * LINE
SUBS = 8
UNROLL = 32
STAGES = LINES // UNROLL
LOW = 256
HIGH = 20
CHAN_HIGH = 5
N_BLOCK = 4
ROWS = 3
DEVICES = 128
TABLE = DEVICES * ROWS
SWATH = ("swath_0", "swath_1", "swath_2")
SWATH_CHAN = ("swath_0", "swath_1", "swath_2", "chan")
F32 = jnp.float32
BF16 = jnp.bfloat16

VMEM = pl.BlockSpec(memory_space=pltpu.VMEM)
SMEM = pl.BlockSpec(memory_space=pltpu.SMEM)
HBM = pl.BlockSpec(memory_space=pltpu.HBM)


def call(kernel, out_shape, in_specs, args, scratch=(), flops=10**9, limit=40, name=None, outs=None):
    return pl.pallas_call(
        kernel,
        out_shape=out_shape,
        in_specs=in_specs,
        out_specs=outs or jax.tree.map(lambda _: VMEM, out_shape),
        scratch_shapes=list(scratch),
        compiler_params=pltpu.CompilerParams(vmem_limit_bytes=int(limit * 2**20)),
        cost_estimate=pl.CostEstimate(flops=flops, bytes_accessed=4 * 2**20, transcendentals=0),
        name=name,
    )(*args)


def split(x):
    high = x.astype(BF16)
    return high, (x - high.astype(F32)).astype(BF16)


def table_tiles():
    for high in range(HIGH):
        for half in range(2):
            tile = high % CHAN_HIGH * 2 + half
            yield high, half, high // CHAN_HIGH, tile


def tile_rows(block, tile, rows, offset=0):
    start = N_BLOCK * rows * 8 * (tile % 4) + rows * block + tile // 4 + offset
    return pl.ds(start, 8, stride=N_BLOCK * rows)


def one_hot_low(low8, hot_ref):
    ids = lax.broadcasted_iota(jnp.int32, (LOW, LINE), 0).astype(F32).astype(BF16)
    low = low8.astype(F32)
    for j in range(GROUP):
        row = jnp.broadcast_to(low[j : j + 1], (LOW, LINE)).astype(BF16)
        hot_ref[:, j * LINE : (j + 1) * LINE] = jnp.where(
            ids == row, jnp.ones((), BF16), jnp.zeros((), BF16)
        )


def joined(ref, part, high, cols):
    at = 8 * HIGH * part + 8 * high
    return ref[at : at + 8, cols] + ref[at + 8 * HIGH : at + 8 * HIGH + 8, cols]


def spread_high(values, high_row, spread_ref, cols):
    offset = (lax.broadcasted_iota(jnp.int32, (16, LINE), 0) // 8).astype(F32)
    base = (jnp.broadcast_to(high_row, (16, LINE)) - offset).astype(BF16)
    pieces = []
    for value in values:
        for half in split(value):
            pieces.append(jnp.concatenate([half, half], axis=0))
    for m in range(HIGH // 2):
        mask = base == jnp.array(2 * m, BF16)
        for i, piece in enumerate(pieces):
            at = 8 * HIGH * i + 16 * m
            spread_ref[at : at + 16, cols] = jnp.where(mask, piece, jnp.zeros((), BF16))


def dot_rows(left, right):
    return lax.dot_general(left, right, (((1,), (1,)), ((), ())), preferred_element_type=F32)


def live_weights(count, g, lines, prec):
    slot = (
        g * lines * LINE
        + lax.broadcasted_iota(jnp.int32, (lines, LINE), 0) * LINE
        + lax.broadcasted_iota(jnp.int32, (lines, LINE), 1)
    )
    return jnp.where(slot < count, prec, 0.0)


def table_start_kernel(
    count_ref, innov_hbm, prec_hbm, pred_hbm, chan_hbm,
    table_ref,
    innov_ref, prec_ref, pred_ref, chan_ref, sems,
    hot_ref, spread_ref, acc_ref,
):
    small = [
        pltpu.make_async_copy(source, target, sems.at[i])
        for i, (source, target) in enumerate(
            [(chan_hbm, chan_ref), (innov_hbm, innov_ref), (prec_hbm, prec_ref)]
        )
    ]

    def large(i):
        at = pl.ds(pl.multiple_of(i * SUBS * KSLOT, SUBS * KSLOT), SUBS * KSLOT)
        return pltpu.make_async_copy(pred_hbm.at[:, at], pred_ref.at[:, at], sems.at[3 + i])

    steps = LINES // GROUP // SUBS
    for copy in small + [large(i) for i in range(steps)]:
        copy.start()
    count = count_ref[0, 0]
    acc_ref[...] = jnp.zeros_like(acc_ref)
    table_ref[...] = jnp.zeros_like(table_ref)
    for copy in small:
        copy.wait()

    def prepare(g, sub):
        rows = pl.ds(pl.multiple_of(g * GROUP, GROUP), GROUP)
        weight = live_weights(count, g, GROUP, prec_ref[rows, :])
        source = weight * innov_ref[rows, :]
        chan = chan_ref[rows, :]
        one_hot_low(chan & (LOW - 1), hot_ref.at[sub])
        high = (chan >> 8).astype(F32)
        for j in range(GROUP):
            pred = pred_ref[:, pl.ds(pl.multiple_of(g * KSLOT + j * LINE, LINE), LINE)]
            spread_high(
                [pred * source[j : j + 1], pred * pred * weight[j : j + 1]],
                high[j : j + 1],
                spread_ref.at[sub],
                slice(j * LINE, (j + 1) * LINE),
            )

    def step(i, _):
        large(i).wait()
        for sub in range(SUBS):
            prepare(i * SUBS + sub, sub)
        acc = dot_rows(spread_ref[0], hot_ref[0])
        for sub in range(1, SUBS):
            acc = acc + dot_rows(spread_ref[sub], hot_ref[sub])
        acc_ref[...] += acc
        return 0

    lax.fori_loop(0, steps, step, 0)
    for high, half, block, tile in table_tiles():
        cols = slice(half * 128, half * 128 + 128)
        for part in range(2):
            table_ref[tile_rows(block, tile, 2 * ROWS, ROWS * part), :] = joined(
                acc_ref, 2 * part, high, cols
            )


def image_kernel(
    count_ref, coef_ref, prec_ref, state_ref, pred_ref, chan_ref,
    table_ref, image_ref,
    hot_ref, got_ref, coef_split, spread_ref, acc_ref,
):
    for high, half, block, tile in table_tiles():
        acc_ref[high * 8 : high * 8 + 8, half * 128 : half * 128 + 128] = coef_ref[
            tile_rows(block, tile, ROWS), :
        ]
    high_part, low_part = split(acc_ref[0 : 8 * HIGH, :])
    coef_split[0 : 8 * HIGH, :] = high_part
    coef_split[8 * HIGH :, :] = low_part
    acc_ref[...] = jnp.zeros_like(acc_ref)

    def one_hots(g, sub):
        rows = pl.ds(pl.multiple_of(g * GROUP, GROUP), GROUP)
        one_hot_low(chan_ref[rows, :] & (LOW - 1), hot_ref.at[sub])

    def lookups(g, sub):
        got_ref[sub] = jnp.dot(coef_split[...], hot_ref[sub], preferred_element_type=F32)

    def images(g, sub):
        rows = pl.ds(pl.multiple_of(g * GROUP, GROUP), GROUP)
        high_id = chan_ref[rows, :] >> 8
        got = got_ref.at[sub]
        looked = []
        preds = []
        for j in range(GROUP):
            cols = slice(j * LINE, (j + 1) * LINE)
            pred = pred_ref[:, pl.ds(pl.multiple_of(g * KSLOT + j * LINE, LINE), LINE)]
            ids = jnp.broadcast_to(high_id[j : j + 1], (8, LINE))
            coef = [got[at : at + 8, cols] for at in (0, 8 * HIGH)]
            for high in range(1, HIGH):
                mask = ids == high
                coef = [
                    jnp.where(mask, got[at + 8 * high : at + 8 * high + 8, cols], old)
                    for at, old in zip((0, 8 * HIGH), coef)
                ]
            looked.append(jnp.sum(pred * (coef[0] + coef[1]), axis=0, keepdims=True))
            preds.append(pred)
        weight = live_weights(count_ref[0, 0], g, GROUP, prec_ref[rows, :])
        image = weight * (state_ref[rows, :] + jnp.concatenate(looked, axis=0))
        image_ref[rows, :] = image
        high_f = high_id.astype(F32)
        for j in range(GROUP):
            cols = slice(j * LINE, (j + 1) * LINE)
            spread_high(
                [preds[j] * image[j : j + 1]], high_f[j : j + 1], spread_ref.at[sub], cols
            )

    def step(i, _):
        for work in (one_hots, lookups, images):
            for sub in range(SUBS):
                work(i * SUBS + sub, sub)
        acc = dot_rows(spread_ref[0], hot_ref[0])
        for sub in range(1, SUBS):
            acc = acc + dot_rows(spread_ref[sub], hot_ref[sub])
        acc_ref[...] += acc
        return 0

    lax.fori_loop(0, LINES // GROUP // SUBS, step, 0)
    table_ref[...] = jnp.zeros_like(table_ref)
    for high, half, block, tile in table_tiles():
        table_ref[tile_rows(block, tile, ROWS), :] = joined(
            acc_ref, 0, high, slice(half * 128, half * 128 + 128)
        )


def jac_copy(jac_hbm, jac_ref, sems, i):
    at = pl.ds(pl.multiple_of(i * UNROLL * LINE, UNROLL * LINE), UNROLL * LINE)
    return pltpu.make_async_copy(jac_hbm.at[at], jac_ref.at[at], sems.at[i])


def start_jac(*refs):
    for i in range(STAGES):
        jac_copy(*refs, i).start()


def adjoint_kernel(first, *refs):
    if first:
        row_ref, count_ref, col_ref, innov_ref, prec_ref, jac_hbm, field_ref, jac_ref, sems = refs
    else:
        row_ref, col_ref, value_ref, jac_hbm, field_ref, jac_ref, sems = refs
    start_jac(jac_hbm, jac_ref, sems)
    field_ref[...] = jnp.zeros_like(field_ref)
    ids = lax.broadcasted_iota(jnp.int32, (LON_DEV, LINE), 0).astype(F32).astype(BF16)

    def step(g, _):
        jac_copy(jac_hbm, jac_ref, sems, g).wait()
        rows = pl.ds(pl.multiple_of(g * UNROLL, UNROLL), UNROLL)
        col = col_ref[rows, :].astype(F32)
        if first:
            weight = live_weights(count_ref[0, 0], g, UNROLL, prec_ref[rows, :])
            value = weight * innov_ref[rows, :]
        else:
            value = value_ref[rows, :]
        high = value.astype(BF16).astype(F32)
        low = value - high
        for j in range(UNROLL):
            mask = ids == jnp.broadcast_to(col[j : j + 1], (LON_DEV, LINE)).astype(BF16)
            hot = jnp.concatenate(
                [
                    jnp.where(
                        mask,
                        jnp.broadcast_to(part[j : j + 1], (LON_DEV, LINE)).astype(BF16),
                        jnp.zeros((), BF16),
                    )
                    for part in (high, low)
                ],
                axis=0,
            )
            jac = jac_ref[pl.ds(pl.multiple_of(g * UNROLL * LINE + j * LINE, LINE), LINE), :]
            add = jnp.dot(hot, jac, preferred_element_type=F32)
            add = add[:LON_DEV] + add[LON_DEV:]
            at = row_ref[g * UNROLL + j]
            field_ref[at] += add
        return 0

    lax.fori_loop(0, STAGES, step, 0)


def smoothed_row(mid, above, below, smoothing, size):
    left = pltpu.roll(mid, 1, 0)
    right = pltpu.roll(mid, size - 1, 0)
    return mid + smoothing * (above + below + left + right - 4.0 * mid)


WIDE = LON_DEV + 16


def forward_kernel(
    row_ref, edge_ref, field_ref, north_ref, south_ref, west_ref, east_ref, smooth_ref, col_ref, jac_hbm,
    out_hbm, seen_ref,
    jac_ref, sems, out_ref, out_sem, ext_ref, mid_ref, parts_ref,
):
    start_jac(jac_hbm, jac_ref, sems)
    ext_ref[...] = jnp.zeros_like(ext_ref)
    ext_ref[2 : LAT_DEV + 2, 8 : 8 + LON_DEV] = field_ref[...]
    ext_ref[0:2, 8 : 8 + LON_DEV] = north_ref[...]
    ext_ref[LAT_DEV + 2 : LAT_DEV + 4, 8 : 8 + LON_DEV] = south_ref[...]
    ext_ref[:, 6:8] = west_ref[...]
    ext_ref[:, 8 + LON_DEV : 10 + LON_DEV] = east_ref[...]
    smoothing = smooth_ref[...]

    def first(r, _):
        mid_ref[r] = smoothed_row(ext_ref[r + 1], ext_ref[r], ext_ref[r + 2], smoothing, WIDE)
        return 0

    lax.fori_loop(0, LAT_DEV + 2, first, 0, unroll=2)
    mid_ref[0] = mid_ref[0] * jnp.where(edge_ref[0] > 0, 1.0, 0.0)
    mid_ref[LAT_DEV + 1] = mid_ref[LAT_DEV + 1] * jnp.where(edge_ref[1] > 0, 1.0, 0.0)

    def second(r, _):
        mid = mid_ref[r + 1]
        twice = smoothed_row(mid, mid_ref[r], mid_ref[r + 2], smoothing, WIDE)
        out_ref[r] = mid[8 : 8 + LON_DEV]
        high, low = split(twice[8 : 8 + LON_DEV])
        parts_ref[r, 0:LON_DEV, :] = high
        parts_ref[r, LON_DEV:, :] = low
        return 0

    lax.fori_loop(0, LAT_DEV, second, 0, unroll=4)
    out_copy = pltpu.make_async_copy(out_ref, out_hbm, out_sem.at[0])
    out_copy.start()
    ids = lax.broadcasted_iota(jnp.int32, (LON_DEV, LINE), 0)

    def step(g, _):
        jac_copy(jac_hbm, jac_ref, sems, g).wait()
        rows = pl.ds(pl.multiple_of(g * UNROLL, UNROLL), UNROLL)
        col = col_ref[rows, :]
        seen = []
        for j in range(UNROLL):
            jac = jac_ref[pl.ds(pl.multiple_of(g * UNROLL * LINE + j * LINE, LINE), LINE), :]
            at = row_ref[g * UNROLL + j]
            grid = dot_rows(parts_ref[at], jac)
            grid = grid[:LON_DEV] + grid[LON_DEV:]
            mask = ids == jnp.broadcast_to(col[j : j + 1], (LON_DEV, LINE))
            seen.append(jnp.sum(jnp.where(mask, grid, 0.0), axis=0, keepdims=True))
        seen_ref[rows, :] = jnp.concatenate(seen, axis=0)
        return 0

    lax.fori_loop(0, STAGES, step, 0)
    out_copy.wait()


def lanes_of(values):
    lane = lax.broadcasted_iota(jnp.int32, (1, 128), 1)
    row = jnp.zeros((1, 128), F32)
    for i, value in enumerate(values):
        row = jnp.where(lane == i, value, row)
    return row


def total(x):
    return jnp.sum(jnp.sum(x, axis=0, keepdims=True), axis=1, keepdims=True)


def state_sums_kernel(
    field_ref, north_ref, south_ref, west_ref, east_ref, smooth_ref,
    count_ref, innov_ref, prec_ref, image1_ref, image2_ref, seen1_ref, seen2_ref,
    sums_ref,
    ext_ref,
):
    ext_ref[...] = jnp.zeros_like(ext_ref)
    ext_ref[1 : LAT_DEV + 1, 8 : 8 + LON_DEV] = field_ref[...]
    ext_ref[0:1, 8 : 8 + LON_DEV] = north_ref[...]
    ext_ref[LAT_DEV + 1 : LAT_DEV + 2, 8 : 8 + LON_DEV] = south_ref[...]
    ext_ref[1 : LAT_DEV + 1, 7:8] = west_ref[...]
    ext_ref[1 : LAT_DEV + 1, 8 + LON_DEV : 9 + LON_DEV] = east_ref[...]
    smoothing = smooth_ref[...]

    def first(r, acc):
        row = smoothed_row(ext_ref[r + 1], ext_ref[r], ext_ref[r + 2], smoothing, WIDE)
        row = row[8 : 8 + LON_DEV]
        return acc + row * row

    acc = lax.fori_loop(0, LAT_DEV, first, jnp.zeros((LON_DEV, LEV), F32))
    source = live_weights(count_ref[0, 0], 0, LINES, prec_ref[...]) * innov_ref[...]
    image1, image2 = (image1_ref[...], image2_ref[...])
    seen1, seen2 = (seen1_ref[...], seen2_ref[...])
    sums_ref[...] = lanes_of(
        [
            total(seen1 * source),
            total(seen1 * image1),
            total(seen2 * image1),
            total(seen1 * image2),
            total(seen2 * image2),
            total(acc),
        ]
    )


def arrived_sum(ref, rows):
    acc = ref[0:24, :]
    for g in range(1, ref.shape[0] // 24):
        acc = acc + ref[24 * g : 24 * g + 24, :]
    out = acc[0:rows]
    for s in range(1, 24 // rows):
        out = out + acc[rows * s : rows * s + rows]
    return out


def to_everyone(rows, ref):
    tile = jnp.concatenate([rows] * (24 // rows.shape[0]), axis=0)
    for g in range(ref.shape[0] // 24):
        ref[24 * g : 24 * g + 24, :] = tile


def owner_start_kernel(arrived_ref, prior_ref, out_ref, own_ref):
    both = arrived_sum(arrived_ref, 2 * ROWS)
    res = both[:ROWS]
    diag = both[ROWS:] + prior_ref[...]
    pre = res / diag
    own_ref[0:3] = res
    own_ref[3:6] = pre
    own_ref[6:9] = diag
    to_everyone(pre, out_ref)


def owner_next_kernel(arrived_ref, prior_ref, own_ref, out_ref, next_ref):
    image = arrived_sum(arrived_ref, ROWS) + prior_ref[...] * own_ref[3:6]
    pre = image / own_ref[6:9]
    next_ref[0:3] = image
    next_ref[3:6] = pre
    to_everyone(pre, out_ref)


def owner_last_kernel(arrived_ref, prior_ref, own_ref, next_ref, sums_ref, out_ref):
    res, pre = (own_ref[0:3], own_ref[3:6])
    image, image_pre = (next_ref[0:3], next_ref[3:6])
    last = arrived_sum(arrived_ref, ROWS) + prior_ref[...] * image_pre
    row = lanes_of(
        [jnp.zeros((1, 1), F32)] * 6
        + [
            total(res * pre),
            total(res * res),
            total(pre * image),
            total(image * image_pre),
            total(res * image),
            total(image * image),
            total(image_pre * last),
            total(res * last),
            total(image * last),
            total(last * last),
        ]
    )
    out_ref[...] = jnp.broadcast_to(row + sums_ref[...], out_ref.shape)


def finish_kernel(chan_ref, arrived_ref, a_ref, b_ref, pre_ref, image_pre_ref, x_ref, bias_ref, norm_ref):
    sums = jnp.sum(arrived_ref[...], axis=0, keepdims=True)
    lane = lax.broadcasted_iota(jnp.int32, (1, 128), 1)
    pick = [
        jnp.sum(jnp.where(lane == i, sums, 0.0), axis=1, keepdims=True) for i in range(16)
    ]
    aa, ab, bb, ac, bc, cc = pick[:6]
    rz_b, rr_b, zq_b, qw_b, rq_b, qq_b, wt_b, rt_b, qt_b, tt_b = pick[6:]
    state_qq = aa + 2.0 * ab + bb
    state_qc = ac + bc
    rz0 = aa + rz_b
    rr0 = aa + rr_b
    zq = aa + ab + zq_b
    qw = state_qq + qw_b
    rq = aa + ab + rq_b
    qq = state_qq + qq_b
    wt = state_qq + state_qc + wt_b
    rt = aa + ab + ac + rt_b
    qt = state_qq + state_qc + qt_b
    tt = state_qq + 2.0 * state_qc + cc + tt_b
    alpha0 = rz0 / zq
    rz1 = rz0 - 2.0 * alpha0 * zq + alpha0 * alpha0 * qw
    rr1 = rr0 - 2.0 * alpha0 * rq + alpha0 * alpha0 * qq
    beta = rz1 / rz0
    grow = 1.0 + beta
    pq = grow * grow * zq - 2.0 * alpha0 * grow * qw + alpha0 * alpha0 * wt
    alpha1 = rz1 / pq
    along = alpha0 + alpha1 * grow
    back = alpha0 * alpha1
    rr2 = (
        rr0
        - 2.0 * along * rq
        + 2.0 * back * rt
        + along * along * qq
        - 2.0 * along * back * qt
        + back * back * tt
    )
    for i, value in enumerate((rr0, rr1, rr2)):
        norm_ref[i] = jnp.sqrt(jnp.maximum(value, 0.0))[0, 0]
    coef_a = along - back
    x_ref[...] = coef_a[None] * a_ref[...] - back[None] * b_ref[...]
    block = chan_ref[0]
    for i in range(2 * CHAN_HIGH):
        rows = tile_rows(block, i, ROWS)
        bias_ref[:, 128 * i : 128 * i + 128] = along * pre_ref[rows, :] - back * image_pre_ref[rows, :]


def exchange(array, width):
    moved = lax.all_to_all(
        array.reshape(DEVICES, 1, width), SWATH_CHAN, split_axis=0, concat_axis=0, tiled=True
    )
    return moved.reshape(array.shape)


def halo(field, width):
    bands = lax.axis_size(SWATH)
    sectors = lax.axis_size("chan")
    north = lax.ppermute(field[LAT_DEV - width :], SWATH, [(i, i + 1) for i in range(bands - 1)])
    south = lax.ppermute(field[:width], SWATH, [(i + 1, i) for i in range(bands - 1)])

    def columns(part):
        if width == 1:
            return part(field)
        return jnp.concatenate([part(north), part(field), part(south)], axis=0)

    ring = [(i, (i + 1) % sectors) for i in range(sectors)]
    west = lax.ppermute(columns(lambda f: f[:, LON_DEV - width :]), "chan", ring)
    east = lax.ppermute(columns(lambda f: f[:, :width]), "chan", [(b, a) for a, b in ring])
    return north, south, west, east


def shape(*dims):
    return jax.ShapeDtypeStruct(dims, F32)


FIELD = shape(LAT_DEV, LON_DEV, LEV)
SQUARE = shape(LINES, LINE)


def run_table_start(count, innov, prec, pred, chan):
    return call(
        table_start_kernel,
        shape(2 * TABLE, 128),
        [SMEM] + [HBM] * 4,
        (count, innov, prec, pred, chan),
        [
            pltpu.VMEM((LINES, LINE), F32),
            pltpu.VMEM((LINES, LINE), F32),
            pltpu.VMEM((NPRED, SLOTS), F32),
            pltpu.VMEM((LINES, LINE), jnp.int32),
            pltpu.SemaphoreType.DMA((3 + LINES // GROUP // SUBS,)),
            pltpu.VMEM((SUBS, LOW, KSLOT), BF16),
            pltpu.VMEM((SUBS, 32 * HIGH, KSLOT), BF16),
            pltpu.VMEM((32 * HIGH, LOW), F32),
        ],
        flops=4 * 10**9,
        limit=24,
        name="table_start",
    )


JAC_STAGES = [pltpu.VMEM((SLOTS, LEV), BF16), pltpu.SemaphoreType.DMA((STAGES,))]


def run_adjoint(line_row, col, values, jac):
    first = len(values) > 1
    return call(
        functools.partial(adjoint_kernel, first),
        FIELD,
        [SMEM, SMEM] + [VMEM] * 3 + [HBM] if first else [SMEM, VMEM, VMEM, HBM],
        (line_row, values[0], col, *values[1:], jac) if first else (line_row, col, *values, jac),
        JAC_STAGES,
        flops=2 * 10**9,
        limit=14,
        name="adjoint",
    )


def run_forward(line_row, edges, field, halos, smooth, col, jac):
    return call(
        forward_kernel,
        (pltpu.HBM((LAT_DEV, LON_DEV, LEV), F32), SQUARE),
        [SMEM, SMEM] + [VMEM] * 7 + [HBM],
        (line_row, edges, field, *halos, smooth, col, jac),
        JAC_STAGES
        + [
            pltpu.VMEM((LAT_DEV, LON_DEV, LEV), F32),
            pltpu.SemaphoreType.DMA((1,)),
            pltpu.VMEM((LAT_DEV + 4, WIDE, LEV), F32),
            pltpu.VMEM((LAT_DEV + 2, WIDE, LEV), F32),
            pltpu.VMEM((LAT_DEV, 2 * LON_DEV, LEV), BF16),
        ],
        flops=2 * 10**9,
        limit=14,
        outs=(HBM, VMEM),
        name="forward",
    )


def run_image(count, coefs, prec, state, pred, chan):
    return call(
        image_kernel,
        (shape(TABLE, 128), SQUARE),
        [SMEM] + [VMEM] * 5,
        (count, coefs, prec, state, pred, chan),
        [
            pltpu.VMEM((SUBS, LOW, KSLOT), BF16),
            pltpu.VMEM((SUBS, 16 * HIGH, KSLOT), F32),
            pltpu.VMEM((16 * HIGH, LOW), BF16),
            pltpu.VMEM((SUBS, 16 * HIGH, KSLOT), BF16),
            pltpu.VMEM((16 * HIGH, LOW), F32),
        ],
        flops=4 * 10**9,
        limit=16,
        name="image",
    )


def body(
    innovations,
    obs_precision,
    jacobian,
    predictors,
    obs_column,
    obs_channel,
    obs_count,
    smoothing,
    bias_precision,
):
    band = lax.axis_index(SWATH)
    sector = lax.axis_index("chan")
    square = (LINES, LINE)
    chan = obs_channel.reshape(square)
    col_all = obs_column.reshape(square)
    line_row = col_all[:, 0] // LON_DEV
    col = col_all % LON_DEV
    smooth = smoothing.reshape(1, LEV)
    edges = jnp.stack([band > 0, band < lax.axis_size(SWATH) - 1]).astype(jnp.int32)
    prior = bias_precision.reshape(NPRED, 2 * CHAN_HIGH, 128).transpose(1, 0, 2).reshape(-1, 128)
    prior = jnp.pad(prior, ((0, 16), (0, 0)), constant_values=1.0)
    prior = lax.dynamic_index_in_dim(prior.reshape(ROWS, -1, 128), band, axis=1, keepdims=False)
    innov = innovations.reshape(square)
    prec = obs_precision.reshape(square)
    jacobian = pltpu.with_memory_space_constraint(jacobian, pltpu.HBM)
    table0 = run_table_start(
        obs_count, *(pltpu.with_memory_space_constraint(x, pltpu.HBM) for x in (innov, prec, predictors, chan))
    )

    def adjoint(*values):
        return run_adjoint(line_row, col, values, jacobian)

    def forward(field):
        return run_forward(line_row, edges, field, halo(field, 2), smooth, col, jacobian)

    def image_of(coefs, state):
        return run_image(obs_count, coefs, prec, state, predictors, chan)

    arrived0 = exchange(table0, 2 * ROWS * 128)
    send0, own = call(
        owner_start_kernel, (shape(TABLE, 128), shape(9, 128)), [VMEM] * 2, (arrived0, prior), limit=3, name="owner_start"
    )
    pre = exchange(send0, ROWS * 128)
    a_field, seen1 = forward(adjoint(obs_count, innov, prec))
    table1, image1 = image_of(pre, seen1)
    arrived1 = exchange(table1, ROWS * 128)
    send1, own_next = call(
        owner_next_kernel, (shape(TABLE, 128), shape(6, 128)), [VMEM] * 3, (arrived1, prior, own), limit=3, name="owner_next"
    )
    image_pre = exchange(send1, ROWS * 128)
    b_field, seen2 = forward(adjoint(image1))
    table2, image2 = image_of(image_pre, seen1 + seen2)
    arrived2 = exchange(table2, ROWS * 128)
    last = adjoint(image2)
    sums = call(
        state_sums_kernel,
        shape(1, 128),
        [VMEM] * 6 + [SMEM] + [VMEM] * 6,
        (last, *halo(last, 1), smooth, obs_count, innov, prec, image1, image2, seen1, seen2),
        [pltpu.VMEM((LAT_DEV + 2, WIDE, LEV), F32)],
        limit=5, name="state_sums",
    )
    send2 = call(
        owner_last_kernel,
        shape(DEVICES, 128),
        [VMEM] * 5,
        (arrived2, prior, own, own_next, sums),
        limit=3, name="owner_last",
    )
    send2, sector = lax.optimization_barrier((send2, sector.reshape(1)))
    arrived3 = exchange(send2, 128)
    state, bias, norms = call(
        finish_kernel,
        (FIELD, shape(NPRED, 2 * CHAN_HIGH * 128), shape(3)),
        [SMEM] + [VMEM] * 5,
        (sector, arrived3, a_field, b_field, pre, image_pre),
        outs=(VMEM, VMEM, SMEM),
        limit=6, name="finish",
    )
    return state, bias, norms


def solution(mesh):
    torus = Mesh(
        mesh.devices.reshape(4, 4, 2, mesh.shape["chan"]), ("swath_0", "swath_1", "swath_2", "chan")
    )
    placed = (
        P(SWATH_CHAN),
        P(SWATH_CHAN),
        P(SWATH_CHAN, None),
        P(None, SWATH_CHAN),
        P(SWATH_CHAN),
        P(SWATH_CHAN),
        P(SWATH, "chan"),
        P(),
        P(None, "chan"),
    )
    return jax.shard_map(
        body,
        mesh=torus,
        in_specs=placed,
        out_specs=(P(SWATH, "chan", None), P(None, "chan"), P()),
        check_vma=False,
    )
```

time: 206 us -> 159 us (0.77)
  Pallas kernels: 83.6 us -> 51.2 us
  starting transfers between devices: 85.2 us -> 63.6 us
  blocking collectives: 0 us -> 20.3 us
  local copies, waits for them, and re-layouts: 16.2 us -> 2.73 us
    pallas_call x13, Pallas kernels: 83.6 us -> 51.2 us  [call(): pl.pallas_call(kernel, out_shape=out_shape, in_specs=in_specs, out_specs=...]
    all_to_all x6 -> x5, starting transfers between devices: 57.9 us -> 37 us  [exchange(): lax.all_to_all(array.reshape(DEVICES, 1, width), SWATH_CHAN, split_axis=0...]
    all_to_all x0 -> x1, blocking collectives: none -> 20.3 us  [exchange(): lax.all_to_all(array.reshape(DEVICES, 1, width), SWATH_CHAN, split_axis=0...]
    unnamed x46 -> x19, local copies, waits for them, and re-layouts: 14.8 us -> 2.48 us
    all_to_all x6 -> x5, waiting for transfers between devices: 11.1 us -> 12.4 us  [exchange(): lax.all_to_all(array.reshape(DEVICES, 1, width), SWATH_CHAN, split_axis=0...]
  transfers between devices with their start and end apart: 18 -> 17, of which waited for: 5 -> 6; matrix products, arithmetic and copies ran while one was open for 1% -> 0% of each run, Pallas kernels for 15% -> 13%
where the time goes in v1:
time: 159 us; the launch traced here: 158 us
  starting transfers between devices  63.6 us (40%)
  Pallas kernels  51.2 us (32%)
  blocking collectives  20.3 us (13%)
  waiting for transfers between devices  18.3 us (12%)
  local copies, waits for them, and re-layouts  2.73 us (2%)
  between operations  1.85 us (1%)
    pallas_call x13, Pallas kernels, call(): pl.pallas_call(kernel, out_shape=out_shape, in_specs=in_specs, out_specs=...  51.2 us
    all_to_all x5, starting transfers between devices, exchange(): lax.all_to_all(array.reshape(DEVICES, 1, width), SWATH_CHAN, split_axis=0...  37 us
    all_to_all x1, blocking collectives, exchange(): lax.all_to_all(array.reshape(DEVICES, 1, width), SWATH_CHAN, split_axis=0...  20.3 us
    all_to_all x5, waiting for transfers between devices, exchange(): lax.all_to_all(array.reshape(DEVICES, 1, width), SWATH_CHAN, split_axis=0...  12.4 us
    ppermute x3, starting transfers between devices, halo(): lax.ppermute(field[LAT_DEV - width:], SWATH, [(i, i + 1) for i in range(b...  10.6 us
    ppermute x3, starting transfers between devices, halo(): lax.ppermute(field[:width], SWATH, [(i + 1, i) for i in range(bands - 1)])  6.12 us
    ppermute x3, starting transfers between devices, halo(): lax.ppermute(columns(lambda f: f[:, :width]), 'chan', [(b, a) for a, b in...  5.49 us
    ppermute x3, starting transfers between devices, halo(): west = lax.ppermute(columns(lambda f: f[:, LON_DEV - width:]), 'chan', ring)  4.29 us
  transfers between devices with their start and end apart: 17, of which 6 were waited for; matrix products, arithmetic and copies ran while one was open for 0% of the time, Pallas kernels for 13%

profile of v1, /device:TPU:1, one launch (start us, length us, event | category | flops | bytes accessed | tf_op | source)
XLA Modules:
  0.0 158.2 jit_solution(1305919399013573536)
XLA Ops:
  1.3 8.6 %table_start.1 = f32[768,128]{1,0:T(8,128)} custom-call(s32[1,1]{1,0:T(1,128)S(6)} %copy.21.count_ref.refs_1_, f32[128,128]{1,0:T(8,128)} %bitcast.47, f32[128,128]{1,0:T(8,128)} %bitcast.50, f32[8,16384]{1,0:T(8,128)} %pred_ref.3, s32[128,128]{1,0:T(8,128)} %bitcast.44), custom_call_target="tpu_custom_call" | custom-call | flops 4000000000 | bytes 4194304 | tf_op jit(solution)/shard_map/table_start/pallas_call | solution.py:41
  9.9 11.5 %all-to-all-start = ((f32[128,1,768]{2,1,0:T(1,128)}), f32[128,1,768]{2,1,0:T(1,128)S(1)}, u32[]{:S(2)}, u32[]{:S(2)}) async-start(f32[128,1,768]{2,1,0:T(1,128)} %bitcast.3), calls=%async_computation | async-start | bytes 786432 | tf_op jit(solution)/shard_map/all_to_all | solution.py:510
  21.4 0.0 copy-start.8
  21.5 0.1 slice_reduce_fusion
  21.6 3.6 %adjoint.3.field_ref = f32[32,64,128]{2,1,0:T(8,128)S(1)} custom-call(s32[128]{0:T(128)S(1)} %and_select_fusion.refs_0_.row_ref, s32[1,1]{1,0:T(1,128)S(6)} %copy.21.count_ref.refs_1_, s32[128,128]{1,0:T(8,128)S(1)} %add_select_fusion.refs_2_.col_ref.refs_1_, f32[128,128]{1,0:T(8,128)S(1)} %bitcast.48, f32[128,128]{1,0:T(8,128)S(1)} %bitcast.51, ...), custom_call_target="tpu_custom_call" | custom-call | flops 2000000000 | bytes 4194304 | tf_op jit(solution)/shard_map/adjoint/pallas_call | solution.py:41
  25.3 0.0 copy-start.4
  25.3 3.5 %collective-permute-start = (f32[2,64,128]{2,1,0:T(8,128)S(1)}, f32[2,64,128]{2,1,0:T(8,128)S(1)}, u32[]{:S(2)}, u32[]{:S(2)}) collective-permute-start(f32[2,64,128]{2,1,0:T(8,128)S(1)} %get-tuple-element.42), channel_id=1, source_target_pairs={{0,4},{4,8},{8,12},{12,16},{16,20},{20,24},{24,28},{28,32},{32,36}... | collective-permute-start | bytes 196616 | tf_op jit(solution)/shard_map/ppermute | solution.py:519
  28.8 1.9 %collective-permute-start.1 = (f32[2,64,128]{2,1,0:T(8,128)S(1)}, f32[2,64,128]{2,1,0:T(8,128)S(1)}, u32[]{:S(2)}, u32[]{:S(2)}) collective-permute-start(f32[2,64,128]{2,1,0:T(8,128)S(1)} %get-tuple-element.41), channel_id=1, source_target_pairs={{4,0},{8,4},{12,8},{16,12},{20,16},{24,20},{28,24},{32,28},{36,32}... | collective-permute-start | bytes 196616 | tf_op jit(solution)/shard_map/ppermute | solution.py:520
  30.9 3.5 %collective-permute-done.1.south_ref = f32[2,64,128]{2,1,0:T(8,128)S(1)} collective-permute-done((f32[2,64,128]{2,1,0:T(8,128)S(1)}, f32[2,64,128]{2,1,0:T(8,128)S(1)}, u32[]{:S(2)}, u32[]{:S(2)}) %collective-permute-start.1) | collective-permute-done | bytes 65568 | tf_op jit(solution)/shard_map/ppermute | solution.py:520
  34.4 0.0 collective-permute-done.north_ref
  34.5 1.4 collective-permute-start.2
  35.9 1.8 %collective-permute-start.3 = (f32[36,2,128]{2,1,0:T(2,128)S(1)}, f32[36,2,128]{2,1,0:T(2,128)S(1)}, u32[]{:S(2)}, u32[]{:S(2)}) collective-permute-start(f32[36,2,128]{2,1,0:T(2,128)S(1)} %pad_maximum_fusion.1), channel_id=1, source_target_pairs={{1,0},{2,1},{3,2},{0,3},{5,4},{6,5},{7,6},{4,7},{9,8},{10,9},{11,1... | collective-permute-start | bytes 110600 | tf_op jit(solution)/shard_map/ppermute | solution.py:529
  37.8 0.7 owner_start.1
  38.5 9.0 %all-to-all-start.1 = ((f32[128,1,384]{2,1,0:T(1,128)}), f32[128,1,384]{2,1,0:T(1,128)S(1)}, u32[]{:S(2)}, u32[]{:S(2)}) async-start(f32[128,1,384]{2,1,0:T(1,128)} %bitcast.9), calls=%async_computation.1 | async-start | bytes 393216 | tf_op jit(solution)/shard_map/all_to_all | solution.py:510
  47.6 0.1 add_convert_fusion.edge_ref
  47.7 5.3 %forward.2 = (f32[32,64,128]{2,1,0:T(8,128)}, f32[128,128]{1,0:T(8,128)S(1)}) custom-call(s32[128]{0:T(128)S(1)} %and_select_fusion.refs_0_.row_ref, s32[2]{0:T(128)S(1)} %add_convert_fusion.edge_ref, f32[32,64,128]{2,1,0:T(8,128)S(1)} %adjoint.3.field_ref, f32[2,64,128]{2,1,0:T(8,128)S(1)} %collective-permute-done.north_ref, ...), custom_call_target="tpu_custom_call" | custom-call | flops 2000000000 | bytes 4194304 | tf_op jit(solution)/shard_map/forward/pallas_call | solution.py:41
  52.9 5.1 %all-to-all-done.1 = f32[128,1,384]{2,1,0:T(1,128)S(1)} async-done(((f32[128,1,384]{2,1,0:T(1,128)}), f32[128,1,384]{2,1,0:T(1,128)S(1)}, u32[]{:S(2)}, u32[]{:S(2)}) %all-to-all-start.1) | async-done | bytes 196640 | tf_op jit(solution)/shard_map/all_to_all | solution.py:510
  58.0 8.8 %image.2 = (f32[384,128]{1,0:T(8,128)}, f32[128,128]{1,0:T(8,128)S(1)}) custom-call(s32[1,1]{1,0:T(1,128)S(6)} %copy.21.count_ref.refs_1_, f32[384,128]{1,0:T(8,128)S(1)} %bitcast.33, f32[128,128]{1,0:T(8,128)S(1)} %bitcast.52, f32[128,128]{1,0:T(8,128)S(1)} %get-tuple-element.18.state_ref.seen1_ref, f32[8,16384]{1,0:T(8,128)S(1)} %copy-done, ...), custom_call_target="tpu_custom_call" | custom-call | flops 4000000000 | bytes 4194304 | tf_op jit(solution)/shard_map/image/pallas_call | solution.py:41
  66.8 3.5 %adjoint.4.field_ref = f32[32,64,128]{2,1,0:T(8,128)S(1)} custom-call(s32[128]{0:T(128)S(1)} %and_select_fusion.refs_0_.row_ref, s32[128,128]{1,0:T(8,128)S(1)} %add_select_fusion.refs_2_.col_ref.refs_1_, f32[128,128]{1,0:T(8,128)S(1)} %get-tuple-element.22.refs_2_.image1_ref, bf16[16384,128]{1,0:T(8,128)(2,1)} %refs_3_.3), custom_call_target="tpu_custom_call" | custom-call | flops 2000000000 | bytes 4194304 | tf_op jit(solution)/shard_map/adjoint/pallas_call | solution.py:41
  70.4 2.3 %collective-permute-start.5 = (f32[2,64,128]{2,1,0:T(8,128)S(1)}, f32[2,64,128]{2,1,0:T(8,128)S(1)}, u32[]{:S(2)}, u32[]{:S(2)}) collective-permute-start(f32[2,64,128]{2,1,0:T(8,128)S(1)} %get-tuple-element.37), channel_id=1, source_target_pairs={{4,0},{8,4},{12,8},{16,12},{20,16},{24,20},{28,24},{32,28},{36,32}... | collective-permute-start | bytes 196616 | tf_op jit(solution)/shard_map/ppermute | solution.py:520
  72.7 4.7 %all-to-all-start.2 = ((f32[128,1,384]{2,1,0:T(1,128)}), f32[128,1,384]{2,1,0:T(1,128)S(1)}, u32[]{:S(2)}, u32[]{:S(2)}) async-start(f32[128,1,384]{2,1,0:T(1,128)} %bitcast.15), calls=%async_computation.2 | async-start | bytes 393216 | tf_op jit(solution)/shard_map/all_to_all | solution.py:510
  77.4 3.5 %collective-permute-start.4 = (f32[2,64,128]{2,1,0:T(8,128)S(1)}, f32[2,64,128]{2,1,0:T(8,128)S(1)}, u32[]{:S(2)}, u32[]{:S(2)}) collective-permute-start(f32[2,64,128]{2,1,0:T(8,128)S(1)} %get-tuple-element.38), channel_id=1, source_target_pairs={{0,4},{4,8},{8,12},{12,16},{16,20},{20,24},{24,28},{28,32},{32,36}... | collective-permute-start | bytes 196616 | tf_op jit(solution)/shard_map/ppermute | solution.py:519
  81.0 1.3 collective-permute-done.4.north_ref
  82.3 1.4 collective-permute-start.6
  83.8 1.8 %collective-permute-start.7 = (f32[36,2,128]{2,1,0:T(2,128)S(1)}, f32[36,2,128]{2,1,0:T(2,128)S(1)}, u32[]{:S(2)}, u32[]{:S(2)}) collective-permute-start(f32[36,2,128]{2,1,0:T(2,128)S(1)} %pad_maximum_fusion.3), channel_id=1, source_target_pairs={{1,0},{2,1},{3,2},{0,3},{5,4},{6,5},{7,6},{4,7},{9,8},{10,9},{11,1... | collective-permute-start | bytes 110600 | tf_op jit(solution)/shard_map/ppermute | solution.py:529
  85.6 2.2 %all-to-all-done.2 = f32[128,1,384]{2,1,0:T(1,128)S(1)} async-done(((f32[128,1,384]{2,1,0:T(1,128)}), f32[128,1,384]{2,1,0:T(1,128)S(1)}, u32[]{:S(2)}, u32[]{:S(2)}) %all-to-all-start.2) | async-done | bytes 196640 | tf_op jit(solution)/shard_map/all_to_all | solution.py:510
  87.8 0.7 owner_next.1
  88.5 7.1 %all-to-all-start.3 = ((f32[128,1,384]{2,1,0:T(1,128)}), f32[128,1,384]{2,1,0:T(1,128)S(1)}, u32[]{:S(2)}, u32[]{:S(2)}) async-start(f32[128,1,384]{2,1,0:T(1,128)} %bitcast.17), calls=%async_computation.3 | async-start | bytes 393216 | tf_op jit(solution)/shard_map/all_to_all | solution.py:510
  95.7 0.0 collective-permute-done.6.west_ref
  95.7 0.0 collective-permute-done.7.east_ref
  95.7 5.3 %forward.3 = (f32[32,64,128]{2,1,0:T(8,128)}, f32[128,128]{1,0:T(8,128)S(1)}) custom-call(s32[128]{0:T(128)S(1)} %and_select_fusion.refs_0_.row_ref, s32[2]{0:T(128)S(1)} %add_convert_fusion.edge_ref, f32[32,64,128]{2,1,0:T(8,128)S(1)} %adjoint.4.field_ref, f32[2,64,128]{2,1,0:T(8,128)S(1)} %collective-permute-done.4.north_ref, ...), custom_call_target="tpu_custom_call" | custom-call | flops 2000000000 | bytes 4194304 | tf_op jit(solution)/shard_map/forward/pallas_call | solution.py:41
  101.0 5.1 %all-to-all-done.3 = f32[128,1,384]{2,1,0:T(1,128)S(1)} async-done(((f32[128,1,384]{2,1,0:T(1,128)}), f32[128,1,384]{2,1,0:T(1,128)S(1)}, u32[]{:S(2)}, u32[]{:S(2)}) %all-to-all-start.3) | async-done | bytes 196640 | tf_op jit(solution)/shard_map/all_to_all | solution.py:510
  106.1 8.8 %image.3 = (f32[384,128]{1,0:T(8,128)}, f32[128,128]{1,0:T(8,128)S(1)}) custom-call(s32[1,1]{1,0:T(1,128)S(6)} %copy.21.count_ref.refs_1_, f32[384,128]{1,0:T(8,128)S(1)} %bitcast.35, f32[128,128]{1,0:T(8,128)S(1)} %bitcast.53, f32[128,128]{1,0:T(8,128)S(1)} %add.26.state_ref, f32[8,16384]{1,0:T(8,128)S(1)} %copy-done, s32[128,128]{1,0:T(8,128)S(1)} %bitcast.46), custom_call_target="tpu_custom_call" | custom-call | flops 4000000000 | bytes 4194304 | tf_op jit(solution)/shard_map/image/pallas_call | solution.py:41
  114.9 4.7 %all-to-all-start.4 = ((f32[128,1,384]{2,1,0:T(1,128)}), f32[128,1,384]{2,1,0:T(1,128)S(1)}, u32[]{:S(2)}, u32[]{:S(2)}) async-start(f32[128,1,384]{2,1,0:T(1,128)} %bitcast.19), calls=%async_computation.4 | async-start | bytes 393216 | tf_op jit(solution)/shard_map/all_to_all | solution.py:510
  119.6 3.6 %adjoint.5.field_ref = f32[32,64,128]{2,1,0:T(8,128)S(1)} custom-call(s32[128]{0:T(128)S(1)} %and_select_fusion.refs_0_.row_ref, s32[128,128]{1,0:T(8,128)S(1)} %add_select_fusion.refs_2_.col_ref.refs_1_, f32[128,128]{1,0:T(8,128)S(1)} %get-tuple-element.26.refs_2_.image2_ref, bf16[16384,128]{1,0:T(8,128)(2,1)} %refs_3_.3), custom_call_target="tpu_custom_call" | custom-call | flops 2000000000 | bytes 4194304 | tf_op jit(solution)/shard_map/adjoint/pallas_call | solution.py:41
  123.1 3.5 %collective-permute-start.8 = (f32[1,64,128]{2,1,0:T(8,128)S(1)}, f32[1,64,128]{2,1,0:T(8,128)S(1)}, u32[]{:S(2)}, u32[]{:S(2)}) collective-permute-start(f32[1,64,128]{2,1,0:T(8,128)S(1)} %get-tuple-element.34), channel_id=1, source_target_pairs={{0,4},{4,8},{8,12},{12,16},{16,20},{20,24},{24,28},{28,32},{32,36}... | collective-permute-start | bytes 98312 | tf_op jit(solution)/shard_map/ppermute | solution.py:519
  126.7 1.9 %collective-permute-start.9 = (f32[1,64,128]{2,1,0:T(8,128)S(1)}, f32[1,64,128]{2,1,0:T(8,128)S(1)}, u32[]{:S(2)}, u32[]{:S(2)}) collective-permute-start(f32[1,64,128]{2,1,0:T(8,128)S(1)} %get-tuple-element.33), channel_id=1, source_target_pairs={{4,0},{8,4},{12,8},{16,12},{20,16},{24,20},{28,24},{32,28},{36,32}... | collective-permute-start | bytes 98312 | tf_op jit(solution)/shard_map/ppermute | solution.py:520
  128.6 1.4 collective-permute-start.10
  130.1 1.8 %collective-permute-start.11 = (f32[32,1,128]{2,1,0:T(1,128)S(1)}, f32[32,1,128]{2,1,0:T(1,128)S(1)}, u32[]{:S(2)}, u32[]{:S(2)}) collective-permute-start(f32[32,1,128]{2,1,0:T(1,128)S(1)} %get-tuple-element.31), channel_id=1, source_target_pairs={{1,0},{2,1},{3,2},{0,3},{5,4},{6,5},{7,6},{4,7},{9,8},{10,9},{11,1... | collective-permute-start | bytes 49160 | tf_op jit(solution)/shard_map/ppermute | solution.py:529
  131.9 1.0 collective-permute-done.10.west_ref
  133.0 0.0 collective-permute-done.8.north_ref
  133.0 0.0 collective-permute-done.9.south_ref
  133.0 0.8 state_sums.1.sums_ref
  133.8 0.1 owner_last.1
  134.0 20.3 %all_to_all.30 = f32[128,1,128]{2,1,0:T(1,128)S(1)} all-to-all(f32[128,1,128]{2,1,0:T(1,128)S(1)} %bitcast.40), channel_id=1, replica_groups=mesh['swath_0'=4,'swath_1'=4,'swath_2'=2,'chan'=4] {'swath_0','swath_1',..., dimensions={0} | all-to-all | bytes 131072 | tf_op jit(solution)/shard_map/all_to_all | solution.py:510
  154.3 1.2 copy-done.5
  155.5 1.2 copy-done.6
  156.7 1.3 finish.1
  (40 shorter events, 0.3 us)
Async XLA Ops:
  1.3 20.1 %copy-start.7 = (s32[16384]{0:T(1024)S(1)}, s32[16384]{0:T(1024)}, u32[]{:S(2)}) copy-start(s32[16384]{0:T(1024)} %param.13) | copy-start | bytes 196612
  1.3 20.3 %copy-start.2 = (f32[16384]{0:T(1024)S(1)}, f32[16384]{0:T(1024)}, u32[]{:S(2)}) copy-start(f32[16384]{0:T(1024)} %param.9) | copy-start | bytes 196612
  1.3 20.3 %copy-start.3 = (f32[16384]{0:T(1024)S(1)}, f32[16384]{0:T(1024)}, u32[]{:S(2)}) copy-start(f32[16384]{0:T(1024)} %param.10) | copy-start | bytes 196612
  9.9 27.9 %all-to-all-start = ((f32[128,1,768]{2,1,0:T(1,128)}), f32[128,1,768]{2,1,0:T(1,128)S(1)}, u32[]{:S(2)}, u32[]{:S(2)}) async-start(f32[128,1,768]{2,1,0:T(1,128)} %bitcast.3), calls=%async_computation | async-start | bytes 786432 | tf_op jit(solution)/shard_map/all_to_all | solution.py:510
  21.4 9.4 %copy-start.8 = (f32[8,1280]{1,0:T(8,128)S(1)}, f32[8,1280]{1,0:T(8,128)}, u32[]{:S(2)}) copy-start(f32[8,1280]{1,0:T(8,128)} %param.17) | copy-start | bytes 122884
  25.3 22.4 %copy-start.4 = (f32[128]{0:T(128)S(1)}, f32[128]{0:T(128)}, u32[]{:S(2)}) copy-start(f32[128]{0:T(128)} %param.16) | copy-start | bytes 1540
  25.3 9.1 %collective-permute-start = (f32[2,64,128]{2,1,0:T(8,128)S(1)}, f32[2,64,128]{2,1,0:T(8,128)S(1)}, u32[]{:S(2)}, u32[]{:S(2)}) collective-permute-start(f32[2,64,128]{2,1,0:T(8,128)S(1)} %get-tuple-element.42), channel_id=1, source_target_pairs={{0,4},{4,8},{8,12},{12,16},{16,20},{20,24},{24,28},{28,32},{32,36}... | collective-permute-start | bytes 196616 | tf_op jit(solution)/shard_map/ppermute | solution.py:519
  28.8 5.6 %collective-permute-start.1 = (f32[2,64,128]{2,1,0:T(8,128)S(1)}, f32[2,64,128]{2,1,0:T(8,128)S(1)}, u32[]{:S(2)}, u32[]{:S(2)}) collective-permute-start(f32[2,64,128]{2,1,0:T(8,128)S(1)} %get-tuple-element.41), channel_id=1, source_target_pairs={{4,0},{8,4},{12,8},{16,12},{20,16},{24,20},{28,24},{32,28},{36,32}... | collective-permute-start | bytes 196616 | tf_op jit(solution)/shard_map/ppermute | solution.py:520
  34.5 13.2 %collective-permute-start.2 = (f32[36,2,128]{2,1,0:T(2,128)S(1)}, f32[36,2,128]{2,1,0:T(2,128)S(1)}, u32[]{:S(2)}, u32[]{:S(2)}) collective-permute-start(f32[36,2,128]{2,1,0:T(2,128)S(1)} %pad_maximum_fusion), channel_id=1, source_target_pairs={{0,1},{1,2},{2,3},{3,0},{4,5},{5,6},{6,7},{7,4},{8,9},{9,10},{10,1... | collective-permute-start | bytes 110600 | tf_op jit(solution)/shard_map/ppermute | solution.py:528
  35.9 11.7 %collective-permute-start.3 = (f32[36,2,128]{2,1,0:T(2,128)S(1)}, f32[36,2,128]{2,1,0:T(2,128)S(1)}, u32[]{:S(2)}, u32[]{:S(2)}) collective-permute-start(f32[36,2,128]{2,1,0:T(2,128)S(1)} %pad_maximum_fusion.1), channel_id=1, source_target_pairs={{1,0},{2,1},{3,2},{0,3},{5,4},{6,5},{7,6},{4,7},{9,8},{10,9},{11,1... | collective-permute-start | bytes 110600 | tf_op jit(solution)/shard_map/ppermute | solution.py:529
  38.5 19.5 %copy-start = (f32[8,16384]{1,0:T(8,128)S(1)}, f32[8,16384]{1,0:T(8,128)}, u32[]{:S(2)}) copy-start(f32[8,16384]{1,0:T(8,128)} %pred_ref.3) | copy-start | bytes 1572868
  38.5 19.5 %copy-start.1 = (s32[16384]{0:T(1024)S(1)}, s32[16384]{0:T(1024)}, u32[]{:S(2)}) copy-start(s32[16384]{0:T(1024)} %param.14) | copy-start | bytes 196612
  38.5 19.5 %all-to-all-start.1 = ((f32[128,1,384]{2,1,0:T(1,128)}), f32[128,1,384]{2,1,0:T(1,128)S(1)}, u32[]{:S(2)}, u32[]{:S(2)}) async-start(f32[128,1,384]{2,1,0:T(1,128)} %bitcast.9), calls=%async_computation.1 | async-start | bytes 393216 | tf_op jit(solution)/shard_map/all_to_all | solution.py:510
  70.4 10.6 %collective-permute-start.5 = (f32[2,64,128]{2,1,0:T(8,128)S(1)}, f32[2,64,128]{2,1,0:T(8,128)S(1)}, u32[]{:S(2)}, u32[]{:S(2)}) collective-permute-start(f32[2,64,128]{2,1,0:T(8,128)S(1)} %get-tuple-element.37), channel_id=1, source_target_pairs={{4,0},{8,4},{12,8},{16,12},{20,16},{24,20},{28,24},{32,28},{36,32}... | collective-permute-start | bytes 196616 | tf_op jit(solution)/shard_map/ppermute | solution.py:520
  72.7 15.1 %all-to-all-start.2 = ((f32[128,1,384]{2,1,0:T(1,128)}), f32[128,1,384]{2,1,0:T(1,128)S(1)}, u32[]{:S(2)}, u32[]{:S(2)}) async-start(f32[128,1,384]{2,1,0:T(1,128)} %bitcast.15), calls=%async_computation.2 | async-start | bytes 393216 | tf_op jit(solution)/shard_map/all_to_all | solution.py:510
  77.4 4.9 %collective-permute-start.4 = (f32[2,64,128]{2,1,0:T(8,128)S(1)}, f32[2,64,128]{2,1,0:T(8,128)S(1)}, u32[]{:S(2)}, u32[]{:S(2)}) collective-permute-start(f32[2,64,128]{2,1,0:T(8,128)S(1)} %get-tuple-element.38), channel_id=1, source_target_pairs={{0,4},{4,8},{8,12},{12,16},{16,20},{20,24},{24,28},{28,32},{32,36}... | collective-permute-start | bytes 196616 | tf_op jit(solution)/shard_map/ppermute | solution.py:519
  82.3 13.4 %collective-permute-start.6 = (f32[36,2,128]{2,1,0:T(2,128)S(1)}, f32[36,2,128]{2,1,0:T(2,128)S(1)}, u32[]{:S(2)}, u32[]{:S(2)}) collective-permute-start(f32[36,2,128]{2,1,0:T(2,128)S(1)} %pad_maximum_fusion.2), channel_id=1, source_target_pairs={{0,1},{1,2},{2,3},{3,0},{4,5},{5,6},{6,7},{7,4},{8,9},{9,10},{10,1... | collective-permute-start | bytes 110600 | tf_op jit(solution)/shard_map/ppermute | solution.py:528
  83.8 11.9 %collective-permute-start.7 = (f32[36,2,128]{2,1,0:T(2,128)S(1)}, f32[36,2,128]{2,1,0:T(2,128)S(1)}, u32[]{:S(2)}, u32[]{:S(2)}) collective-permute-start(f32[36,2,128]{2,1,0:T(2,128)S(1)} %pad_maximum_fusion.3), channel_id=1, source_target_pairs={{1,0},{2,1},{3,2},{0,3},{5,4},{6,5},{7,6},{4,7},{9,8},{10,9},{11,1... | collective-permute-start | bytes 110600 | tf_op jit(solution)/shard_map/ppermute | solution.py:529
  88.5 17.6 %all-to-all-start.3 = ((f32[128,1,384]{2,1,0:T(1,128)}), f32[128,1,384]{2,1,0:T(1,128)S(1)}, u32[]{:S(2)}, u32[]{:S(2)}) async-start(f32[128,1,384]{2,1,0:T(1,128)} %bitcast.17), calls=%async_computation.3 | async-start | bytes 393216 | tf_op jit(solution)/shard_map/all_to_all | solution.py:510
  114.9 18.9 %all-to-all-start.4 = ((f32[128,1,384]{2,1,0:T(1,128)}), f32[128,1,384]{2,1,0:T(1,128)S(1)}, u32[]{:S(2)}, u32[]{:S(2)}) async-start(f32[128,1,384]{2,1,0:T(1,128)} %bitcast.19), calls=%async_computation.4 | async-start | bytes 393216 | tf_op jit(solution)/shard_map/all_to_all | solution.py:510
  123.1 9.8 %collective-permute-start.8 = (f32[1,64,128]{2,1,0:T(8,128)S(1)}, f32[1,64,128]{2,1,0:T(8,128)S(1)}, u32[]{:S(2)}, u32[]{:S(2)}) collective-permute-start(f32[1,64,128]{2,1,0:T(8,128)S(1)} %get-tuple-element.34), channel_id=1, source_target_pairs={{0,4},{4,8},{8,12},{12,16},{16,20},{20,24},{24,28},{28,32},{32,36}... | collective-permute-start | bytes 98312 | tf_op jit(solution)/shard_map/ppermute | solution.py:519
  126.7 6.3 %collective-permute-start.9 = (f32[1,64,128]{2,1,0:T(8,128)S(1)}, f32[1,64,128]{2,1,0:T(8,128)S(1)}, u32[]{:S(2)}, u32[]{:S(2)}) collective-permute-start(f32[1,64,128]{2,1,0:T(8,128)S(1)} %get-tuple-element.33), channel_id=1, source_target_pairs={{4,0},{8,4},{12,8},{16,12},{20,16},{24,20},{28,24},{32,28},{36,32}... | collective-permute-start | bytes 98312 | tf_op jit(solution)/shard_map/ppermute | solution.py:520
  128.6 4.3 %collective-permute-start.10 = (f32[32,1,128]{2,1,0:T(1,128)S(1)}, f32[32,1,128]{2,1,0:T(1,128)S(1)}, u32[]{:S(2)}, u32[]{:S(2)}) collective-permute-start(f32[32,1,128]{2,1,0:T(1,128)S(1)} %get-tuple-element.32), channel_id=1, source_target_pairs={{0,1},{1,2},{2,3},{3,0},{4,5},{5,6},{6,7},{7,4},{8,9},{9,10},{10,1... | collective-permute-start | bytes 49160 | tf_op jit(solution)/shard_map/ppermute | solution.py:528
  130.1 2.9 %collective-permute-start.11 = (f32[32,1,128]{2,1,0:T(1,128)S(1)}, f32[32,1,128]{2,1,0:T(1,128)S(1)}, u32[]{:S(2)}, u32[]{:S(2)}) collective-permute-start(f32[32,1,128]{2,1,0:T(1,128)S(1)} %get-tuple-element.31), channel_id=1, source_target_pairs={{1,0},{2,1},{3,2},{0,3},{5,4},{6,5},{7,6},{4,7},{9,8},{10,9},{11,1... | collective-permute-start | bytes 49160 | tf_op jit(solution)/shard_map/ppermute | solution.py:529
  154.3 1.2 copy-start.5
  155.5 1.2 copy-start.6

commit v2 on v1

--- a/solution.py
+++ b/solution.py
@@ -24,6 +24,7 @@
 HIGH = 20
 CHAN_HIGH = 5
 N_BLOCK = 4
+OUT_PARTS = 4
 ROWS = 3
 DEVICES = 128
 TABLE = DEVICES * ROWS
@@ -109,26 +110,88 @@
     return jnp.where(slot < count, prec, 0.0)
 
 
+def jac_copy(jac_hbm, jac_ref, sems, i):
+    at = pl.ds(pl.multiple_of(i * UNROLL * LINE, UNROLL * LINE), UNROLL * LINE)
+    return pltpu.make_async_copy(jac_hbm.at[at], jac_ref.at[at], sems.at[i])
+
+
+def start_jac(*refs):
+    for i in range(STAGES):
+        jac_copy(*refs, i).start()
+
+
+def add_adjoint(row_ref, col_ref, value_of, jac_hbm, jac_ref, sems, field_ref):
+    field_ref[...] = jnp.zeros_like(field_ref)
+    ids = lax.broadcasted_iota(jnp.int32, (LON_DEV, LINE), 0).astype(F32).astype(BF16)
+
+    def step(g, _):
+        jac_copy(jac_hbm, jac_ref, sems, g).wait()
+        rows = pl.ds(pl.multiple_of(g * UNROLL, UNROLL), UNROLL)
+        col = col_ref[rows, :].astype(F32)
+        value = value_of(g, rows)
+        high = value.astype(BF16).astype(F32)
+        low = value - high
+        for j in range(UNROLL):
+            mask = ids == jnp.broadcast_to(col[j : j + 1], (LON_DEV, LINE)).astype(BF16)
+            hot = jnp.concatenate(
+                [
+                    jnp.where(
+                        mask,
+                        jnp.broadcast_to(part[j : j + 1], (LON_DEV, LINE)).astype(BF16),
+                        jnp.zeros((), BF16),
+                    )
+                    for part in (high, low)
+                ],
+                axis=0,
+            )
+            jac = jac_ref[pl.ds(pl.multiple_of(g * UNROLL * LINE + j * LINE, LINE), LINE), :]
+            add = jnp.dot(hot, jac, preferred_element_type=F32)
+            add = add[:LON_DEV] + add[LON_DEV:]
+            at = row_ref[g * UNROLL + j]
+            field_ref[at] += add
+        return 0
+
+    lax.fori_loop(0, STAGES, step, 0)
+
+
+def even_band():
+    return 1 - lax.axis_index("swath_2")
+
+
+def store_edges(field_ref, even, pair_ref, next_ref):
+    width = pair_ref.shape[0]
+    far = (LAT_DEV - width) * even
+    pair_ref[...] = field_ref[pl.ds(far, width)]
+    next_ref[...] = field_ref[pl.ds(LAT_DEV - width - far, width)]
+
+
 def table_start_kernel(
-    count_ref, innov_hbm, prec_hbm, pred_hbm, chan_hbm,
-    table_ref,
-    innov_ref, prec_ref, pred_ref, chan_ref, sems,
-    hot_ref, spread_ref, acc_ref,
+    count_ref, innov_hbm, prec_hbm, pred_hbm, chan_hbm, column_hbm, jac_hbm,
+    table_hbm, field_ref, pair_ref, next_ref, row_ref, col_ref,
+    innov_ref, prec_ref, pred_ref, chan_ref, column_ref, column_smem, sems,
+    hot_ref, spread_ref, acc_ref, table_ref, table_sem, jac_ref, jac_sems,
 ):
     small = [
         pltpu.make_async_copy(source, target, sems.at[i])
         for i, (source, target) in enumerate(
-            [(chan_hbm, chan_ref), (innov_hbm, innov_ref), (prec_hbm, prec_ref)]
+            [
+                (chan_hbm, chan_ref),
+                (innov_hbm, innov_ref),
+                (prec_hbm, prec_ref),
+                (column_hbm, column_ref),
+                (column_hbm, column_smem),
+            ]
         )
     ]
 
     def large(i):
         at = pl.ds(pl.multiple_of(i * SUBS * KSLOT, SUBS * KSLOT), SUBS * KSLOT)
-        return pltpu.make_async_copy(pred_hbm.at[:, at], pred_ref.at[:, at], sems.at[3 + i])
+        return pltpu.make_async_copy(pred_hbm.at[:, at], pred_ref.at[:, at], sems.at[5 + i])
 
     steps = LINES // GROUP // SUBS
     for copy in small + [large(i) for i in range(steps)]:
         copy.start()
+    start_jac(jac_hbm, jac_ref, jac_sems)
     count = count_ref[0, 0]
     acc_ref[...] = jnp.zeros_like(acc_ref)
     table_ref[...] = jnp.zeros_like(table_ref)
@@ -168,13 +231,31 @@
             table_ref[tile_rows(block, tile, 2 * ROWS, ROWS * part), :] = joined(
                 acc_ref, 2 * part, high, cols
             )
+    written = pltpu.make_async_copy(table_ref, table_hbm, table_sem.at[0])
+    written.start()
+
+    col_ref[...] = column_ref[...] & (LON_DEV - 1)
+
+    def rows_of(i, _):
+        row_ref[i] = column_smem[i, 0] >> 6
+        return 0
+
+    lax.fori_loop(0, LINES, rows_of, 0, unroll=16)
+
+    def value_of(g, rows):
+        return live_weights(count, g, UNROLL, prec_ref[rows, :]) * innov_ref[rows, :]
+
+    add_adjoint(row_ref, col_ref, value_of, jac_hbm, jac_ref, jac_sems, field_ref)
+    store_edges(field_ref, even_band(), pair_ref, next_ref)
+    written.wait()
 
 
 def image_kernel(
-    count_ref, coef_ref, prec_ref, state_ref, pred_ref, chan_ref,
-    table_ref, image_ref,
-    hot_ref, got_ref, coef_split, spread_ref, acc_ref,
+    count_ref, row_ref, coef_ref, prec_ref, state_ref, pred_ref, chan_ref, col_ref, jac_hbm,
+    table_hbm, image_ref, field_ref, pair_ref, next_ref,
+    hot_ref, got_ref, coef_split, spread_ref, acc_ref, table_ref, table_sem, jac_ref, jac_sems,
 ):
+    start_jac(jac_hbm, jac_ref, jac_sems)
     for high, half, block, tile in table_tiles():
         acc_ref[high * 8 : high * 8 + 8, half * 128 : half * 128 + 128] = coef_ref[
             tile_rows(block, tile, ROWS), :
@@ -236,59 +317,13 @@
         table_ref[tile_rows(block, tile, ROWS), :] = joined(
             acc_ref, 0, high, slice(half * 128, half * 128 + 128)
         )
-
-
-def jac_copy(jac_hbm, jac_ref, sems, i):
-    at = pl.ds(pl.multiple_of(i * UNROLL * LINE, UNROLL * LINE), UNROLL * LINE)
-    return pltpu.make_async_copy(jac_hbm.at[at], jac_ref.at[at], sems.at[i])
-
-
-def start_jac(*refs):
-    for i in range(STAGES):
-        jac_copy(*refs, i).start()
-
-
-def adjoint_kernel(first, *refs):
-    if first:
-        row_ref, count_ref, col_ref, innov_ref, prec_ref, jac_hbm, field_ref, jac_ref, sems = refs
-    else:
-        row_ref, col_ref, value_ref, jac_hbm, field_ref, jac_ref, sems = refs
-    start_jac(jac_hbm, jac_ref, sems)
-    field_ref[...] = jnp.zeros_like(field_ref)
-    ids = lax.broadcasted_iota(jnp.int32, (LON_DEV, LINE), 0).astype(F32).astype(BF16)
-
-    def step(g, _):
-        jac_copy(jac_hbm, jac_ref, sems, g).wait()
-        rows = pl.ds(pl.multiple_of(g * UNROLL, UNROLL), UNROLL)
-        col = col_ref[rows, :].astype(F32)
-        if first:
-            weight = live_weights(count_ref[0, 0], g, UNROLL, prec_ref[rows, :])
-            value = weight * innov_ref[rows, :]
-        else:
-            value = value_ref[rows, :]
-        high = value.astype(BF16).astype(F32)
-        low = value - high
-        for j in range(UNROLL):
-            mask = ids == jnp.broadcast_to(col[j : j + 1], (LON_DEV, LINE)).astype(BF16)
-            hot = jnp.concatenate(
-                [
-                    jnp.where(
-                        mask,
-                        jnp.broadcast_to(part[j : j + 1], (LON_DEV, LINE)).astype(BF16),
-                        jnp.zeros((), BF16),
-                    )
-                    for part in (high, low)
-                ],
-                axis=0,
-            )
-            jac = jac_ref[pl.ds(pl.multiple_of(g * UNROLL * LINE + j * LINE, LINE), LINE), :]
-            add = jnp.dot(hot, jac, preferred_element_type=F32)
-            add = add[:LON_DEV] + add[LON_DEV:]
-            at = row_ref[g * UNROLL + j]
-            field_ref[at] += add
-        return 0
-
-    lax.fori_loop(0, STAGES, step, 0)
+    written = pltpu.make_async_copy(table_ref, table_hbm, table_sem.at[0])
+    written.start()
+    add_adjoint(
+        row_ref, col_ref, lambda g, rows: image_ref[rows, :], jac_hbm, jac_ref, jac_sems, field_ref
+    )
+    store_edges(field_ref, even_band(), pair_ref, next_ref)
+    written.wait()
 
 
 def smoothed_row(mid, above, below, smoothing, size):
@@ -300,18 +335,35 @@
 WIDE = LON_DEV + 16
 
 
+def fill_extended(ext_ref, even, field_ref, pair_ref, next_ref, west_ref, east_ref):
+    width = pair_ref.shape[0]
+    ext_ref[...] = jnp.zeros_like(ext_ref)
+    pair_at = (LAT_DEV + width) * even
+    next_at = LAT_DEV + width - pair_at
+    parts = [
+        (pair_ref, pl.ds(pair_at, width), slice(0, width)),
+        (field_ref, slice(width, LAT_DEV + width), slice(width, LAT_DEV + width)),
+        (next_ref, pl.ds(next_at, width), slice(LAT_DEV + width, LAT_DEV + 2 * width)),
+    ]
+    corners = west_ref.shape[0] > LAT_DEV
+    for ref, rows, side in parts:
+        ext_ref[rows, 8 : 8 + LON_DEV] = ref[...]
+        if not corners:
+            if ref is not field_ref:
+                continue
+            side = slice(0, LAT_DEV)
+        ext_ref[rows, 8 - width : 8] = west_ref[side]
+        ext_ref[rows, 8 + LON_DEV : 8 + LON_DEV + width] = east_ref[side]
+
+
 def forward_kernel(
-    row_ref, edge_ref, field_ref, north_ref, south_ref, west_ref, east_ref, smooth_ref, col_ref, jac_hbm,
+    bands,
+    row_ref, field_ref, pair_ref, next_ref, west_ref, east_ref, smooth_ref, col_ref, jac_hbm,
     out_hbm, seen_ref,
     jac_ref, sems, out_ref, out_sem, ext_ref, mid_ref, parts_ref,
 ):
     start_jac(jac_hbm, jac_ref, sems)
-    ext_ref[...] = jnp.zeros_like(ext_ref)
-    ext_ref[2 : LAT_DEV + 2, 8 : 8 + LON_DEV] = field_ref[...]
-    ext_ref[0:2, 8 : 8 + LON_DEV] = north_ref[...]
-    ext_ref[LAT_DEV + 2 : LAT_DEV + 4, 8 : 8 + LON_DEV] = south_ref[...]
-    ext_ref[:, 6:8] = west_ref[...]
-    ext_ref[:, 8 + LON_DEV : 10 + LON_DEV] = east_ref[...]
+    fill_extended(ext_ref, even_band(), field_ref, pair_ref, next_ref, west_ref, east_ref)
     smoothing = smooth_ref[...]
 
     def first(r, _):
@@ -319,8 +371,9 @@
         return 0
 
     lax.fori_loop(0, LAT_DEV + 2, first, 0, unroll=2)
-    mid_ref[0] = mid_ref[0] * jnp.where(edge_ref[0] > 0, 1.0, 0.0)
-    mid_ref[LAT_DEV + 1] = mid_ref[LAT_DEV + 1] * jnp.where(edge_ref[1] > 0, 1.0, 0.0)
+    band = lax.axis_index(SWATH)
+    mid_ref[0] = mid_ref[0] * jnp.where(band > 0, 1.0, 0.0)
+    mid_ref[LAT_DEV + 1] = mid_ref[LAT_DEV + 1] * jnp.where(band < bands - 1, 1.0, 0.0)
 
     def second(r, _):
         mid = mid_ref[r + 1]
@@ -368,17 +421,12 @@
 
 
 def state_sums_kernel(
-    field_ref, north_ref, south_ref, west_ref, east_ref, smooth_ref,
+    field_ref, pair_ref, next_ref, west_ref, east_ref, smooth_ref,
     count_ref, innov_ref, prec_ref, image1_ref, image2_ref, seen1_ref, seen2_ref,
     sums_ref,
     ext_ref,
 ):
-    ext_ref[...] = jnp.zeros_like(ext_ref)
-    ext_ref[1 : LAT_DEV + 1, 8 : 8 + LON_DEV] = field_ref[...]
-    ext_ref[0:1, 8 : 8 + LON_DEV] = north_ref[...]
-    ext_ref[LAT_DEV + 1 : LAT_DEV + 2, 8 : 8 + LON_DEV] = south_ref[...]
-    ext_ref[1 : LAT_DEV + 1, 7:8] = west_ref[...]
-    ext_ref[1 : LAT_DEV + 1, 8 + LON_DEV : 9 + LON_DEV] = east_ref[...]
+    fill_extended(ext_ref, even_band(), field_ref, pair_ref, next_ref, west_ref, east_ref)
     smoothing = smooth_ref[...]
 
     def first(r, acc):
@@ -459,7 +507,26 @@
     out_ref[...] = jnp.broadcast_to(row + sums_ref[...], out_ref.shape)
 
 
-def finish_kernel(chan_ref, arrived_ref, a_ref, b_ref, pre_ref, image_pre_ref, x_ref, bias_ref, norm_ref):
+def finish_kernel(
+    chan_ref, arrived_ref, a_hbm, b_hbm, pre_ref, image_pre_ref,
+    x_hbm, bias_ref, norm_ref,
+    a_ref, b_ref, in_sems, out_sems,
+):
+    rows_in = LAT_DEV // OUT_PARTS
+    sources = ((a_hbm, a_ref), (b_hbm, b_ref))
+
+    def fetch(i, which):
+        at = pl.ds(i * rows_in, rows_in)
+        source, target = sources[which]
+        return pltpu.make_async_copy(source.at[at], target.at[at], in_sems.at[which, i])
+
+    def write(i):
+        at = pl.ds(i * rows_in, rows_in)
+        return pltpu.make_async_copy(a_ref.at[at], x_hbm.at[at], out_sems.at[i])
+
+    for i in range(OUT_PARTS):
+        for which in range(2):
+            fetch(i, which).start()
     sums = jnp.sum(arrived_ref[...], axis=0, keepdims=True)
     lane = lax.broadcasted_iota(jnp.int32, (1, 128), 1)
     pick = [
@@ -499,11 +566,18 @@
     for i, value in enumerate((rr0, rr1, rr2)):
         norm_ref[i] = jnp.sqrt(jnp.maximum(value, 0.0))[0, 0]
     coef_a = along - back
-    x_ref[...] = coef_a[None] * a_ref[...] - back[None] * b_ref[...]
+    for i in range(OUT_PARTS):
+        for which in range(2):
+            fetch(i, which).wait()
+        at = slice(i * rows_in, (i + 1) * rows_in)
+        a_ref[at] = coef_a[None] * a_ref[at] - back[None] * b_ref[at]
+        write(i).start()
     block = chan_ref[0]
     for i in range(2 * CHAN_HIGH):
         rows = tile_rows(block, i, ROWS)
         bias_ref[:, 128 * i : 128 * i + 128] = along * pre_ref[rows, :] - back * image_pre_ref[rows, :]
+    for i in range(OUT_PARTS):
+        write(i).wait()
 
 
 def exchange(array, width):
@@ -513,21 +587,24 @@
     return moved.reshape(array.shape)
 
 
-def halo(field, width):
+def halo(field, pair, following):
+    width = pair.shape[0]
     bands = lax.axis_size(SWATH)
     sectors = lax.axis_size("chan")
-    north = lax.ppermute(field[LAT_DEV - width :], SWATH, [(i, i + 1) for i in range(bands - 1)])
-    south = lax.ppermute(field[:width], SWATH, [(i + 1, i) for i in range(bands - 1)])
+    same = [(i, i ^ 1) for i in range(bands)]
+    other = [(i, i + 1) for i in range(1, bands - 1, 2)]
+    pair = lax.ppermute(pair, SWATH, same)
+    following = lax.ppermute(following, SWATH, other + [(b, a) for a, b in other])
 
     def columns(part):
         if width == 1:
             return part(field)
-        return jnp.concatenate([part(north), part(field), part(south)], axis=0)
+        return jnp.concatenate([part(pair), part(field), part(following)], axis=0)
 
     ring = [(i, (i + 1) % sectors) for i in range(sectors)]
     west = lax.ppermute(columns(lambda f: f[:, LON_DEV - width :]), "chan", ring)
     east = lax.ppermute(columns(lambda f: f[:, :width]), "chan", [(b, a) for a, b in ring])
-    return north, south, west, east
+    return pair, following, west, east
 
 
 def shape(*dims):
@@ -538,51 +615,55 @@
 SQUARE = shape(LINES, LINE)
 
 
-def run_table_start(count, innov, prec, pred, chan):
+JAC_STAGES = [pltpu.VMEM((SLOTS, LEV), BF16), pltpu.SemaphoreType.DMA((STAGES,))]
+
+
+def edges_of(width):
+    return (shape(width, LON_DEV, LEV),) * 2
+
+
+def run_table_start(count, innov, prec, pred, chan, column, jac):
+    square = pltpu.VMEM((LINES, LINE), F32)
+    whole = pltpu.VMEM((LINES, LINE), jnp.int32)
     return call(
         table_start_kernel,
-        shape(2 * TABLE, 128),
-        [SMEM] + [HBM] * 4,
-        (count, innov, prec, pred, chan),
+        (
+            pltpu.HBM((2 * TABLE, 128), F32),
+            FIELD,
+            *edges_of(2),
+            jax.ShapeDtypeStruct((LINES,), jnp.int32),
+            jax.ShapeDtypeStruct((LINES, LINE), jnp.int32),
+        ),
+        [SMEM] + [HBM] * 6,
+        (count, innov, prec, pred, chan, column, jac),
         [
-            pltpu.VMEM((LINES, LINE), F32),
-            pltpu.VMEM((LINES, LINE), F32),
+            square,
+            square,
             pltpu.VMEM((NPRED, SLOTS), F32),
-            pltpu.VMEM((LINES, LINE), jnp.int32),
-            pltpu.SemaphoreType.DMA((3 + LINES // GROUP // SUBS,)),
+            whole,
+            whole,
+            pltpu.SMEM((LINES, LINE), jnp.int32),
+            pltpu.SemaphoreType.DMA((5 + LINES // GROUP // SUBS,)),
             pltpu.VMEM((SUBS, LOW, KSLOT), BF16),
             pltpu.VMEM((SUBS, 32 * HIGH, KSLOT), BF16),
             pltpu.VMEM((32 * HIGH, LOW), F32),
-        ],
-        flops=4 * 10**9,
-        limit=24,
+            pltpu.VMEM((2 * TABLE, 128), F32),
+            pltpu.SemaphoreType.DMA((1,)),
+        ]
+        + JAC_STAGES,
+        flops=6 * 10**9,
+        limit=32,
+        outs=(HBM, VMEM, VMEM, VMEM, SMEM, VMEM),
         name="table_start",
     )
 
 
-JAC_STAGES = [pltpu.VMEM((SLOTS, LEV), BF16), pltpu.SemaphoreType.DMA((STAGES,))]
-
-
-def run_adjoint(line_row, col, values, jac):
-    first = len(values) > 1
+def run_forward(line_row, field, halos, smooth, col, jac):
     return call(
-        functools.partial(adjoint_kernel, first),
-        FIELD,
-        [SMEM, SMEM] + [VMEM] * 3 + [HBM] if first else [SMEM, VMEM, VMEM, HBM],
-        (line_row, values[0], col, *values[1:], jac) if first else (line_row, col, *values, jac),
-        JAC_STAGES,
-        flops=2 * 10**9,
-        limit=14,
-        name="adjoint",
-    )
-
-
-def run_forward(line_row, edges, field, halos, smooth, col, jac):
-    return call(
-        forward_kernel,
+        functools.partial(forward_kernel, lax.axis_size(SWATH)),
         (pltpu.HBM((LAT_DEV, LON_DEV, LEV), F32), SQUARE),
-        [SMEM, SMEM] + [VMEM] * 7 + [HBM],
-        (line_row, edges, field, *halos, smooth, col, jac),
+        [SMEM] + [VMEM] * 7 + [HBM],
+        (line_row, field, *halos, smooth, col, jac),
         JAC_STAGES
         + [
             pltpu.VMEM((LAT_DEV, LON_DEV, LEV), F32),
@@ -598,21 +679,25 @@
     )
 
 
-def run_image(count, coefs, prec, state, pred, chan):
+def run_image(count, line_row, coefs, prec, state, pred, chan, col, jac, width):
     return call(
         image_kernel,
-        (shape(TABLE, 128), SQUARE),
-        [SMEM] + [VMEM] * 5,
-        (count, coefs, prec, state, pred, chan),
+        (pltpu.HBM((TABLE, 128), F32), SQUARE, FIELD, *edges_of(width)),
+        [SMEM] * 2 + [VMEM] * 6 + [HBM],
+        (count, line_row, coefs, prec, state, pred, chan, col, jac),
         [
             pltpu.VMEM((SUBS, LOW, KSLOT), BF16),
             pltpu.VMEM((SUBS, 16 * HIGH, KSLOT), F32),
             pltpu.VMEM((16 * HIGH, LOW), BF16),
             pltpu.VMEM((SUBS, 16 * HIGH, KSLOT), BF16),
             pltpu.VMEM((16 * HIGH, LOW), F32),
-        ],
-        flops=4 * 10**9,
-        limit=16,
+            pltpu.VMEM((TABLE, 128), F32),
+            pltpu.SemaphoreType.DMA((1,)),
+        ]
+        + JAC_STAGES,
+        flops=6 * 10**9,
+        limit=36,
+        outs=(HBM, VMEM, VMEM, VMEM, VMEM),
         name="image",
     )
 
@@ -632,53 +717,50 @@
     sector = lax.axis_index("chan")
     square = (LINES, LINE)
     chan = obs_channel.reshape(square)
-    col_all = obs_column.reshape(square)
-    line_row = col_all[:, 0] // LON_DEV
-    col = col_all % LON_DEV
     smooth = smoothing.reshape(1, LEV)
-    edges = jnp.stack([band > 0, band < lax.axis_size(SWATH) - 1]).astype(jnp.int32)
     prior = bias_precision.reshape(NPRED, 2 * CHAN_HIGH, 128).transpose(1, 0, 2).reshape(-1, 128)
     prior = jnp.pad(prior, ((0, 16), (0, 0)), constant_values=1.0)
     prior = lax.dynamic_index_in_dim(prior.reshape(ROWS, -1, 128), band, axis=1, keepdims=False)
     innov = innovations.reshape(square)
     prec = obs_precision.reshape(square)
     jacobian = pltpu.with_memory_space_constraint(jacobian, pltpu.HBM)
-    table0 = run_table_start(
-        obs_count, *(pltpu.with_memory_space_constraint(x, pltpu.HBM) for x in (innov, prec, predictors, chan))
-    )
-
-    def adjoint(*values):
-        return run_adjoint(line_row, col, values, jacobian)
-
-    def forward(field):
-        return run_forward(line_row, edges, field, halo(field, 2), smooth, col, jacobian)
-
-    def image_of(coefs, state):
-        return run_image(obs_count, coefs, prec, state, predictors, chan)
+    in_hbm = [
+        pltpu.with_memory_space_constraint(x, pltpu.HBM)
+        for x in (innov, prec, predictors, chan, obs_column.reshape(square))
+    ]
+    table0, *start, line_row, col = run_table_start(obs_count, *in_hbm, jacobian)
+
+    def forward(field, *edges):
+        return run_forward(line_row, field, halo(field, *edges), smooth, col, jacobian)
+
+    def image_of(coefs, state, width):
+        return run_image(
+            obs_count, line_row, coefs, prec, state, predictors, chan, col, jacobian, width
+        )
 
     arrived0 = exchange(table0, 2 * ROWS * 128)
     send0, own = call(
         owner_start_kernel, (shape(TABLE, 128), shape(9, 128)), [VMEM] * 2, (arrived0, prior), limit=3, name="owner_start"
     )
     pre = exchange(send0, ROWS * 128)
-    a_field, seen1 = forward(adjoint(obs_count, innov, prec))
-    table1, image1 = image_of(pre, seen1)
+    a_field, seen1 = forward(*start)
+    table1, image1, *first = image_of(pre, seen1, 2)
     arrived1 = exchange(table1, ROWS * 128)
     send1, own_next = call(
         owner_next_kernel, (shape(TABLE, 128), shape(6, 128)), [VMEM] * 3, (arrived1, prior, own), limit=3, name="owner_next"
     )
     image_pre = exchange(send1, ROWS * 128)
-    b_field, seen2 = forward(adjoint(image1))
-    table2, image2 = image_of(image_pre, seen1 + seen2)
+    b_field, seen2 = forward(*first)
+    table2, image2, *last = image_of(image_pre, seen1 + seen2, 1)
     arrived2 = exchange(table2, ROWS * 128)
-    last = adjoint(image2)
     sums = call(
         state_sums_kernel,
         shape(1, 128),
         [VMEM] * 6 + [SMEM] + [VMEM] * 6,
-        (last, *halo(last, 1), smooth, obs_count, innov, prec, image1, image2, seen1, seen2),
+        (last[0], *halo(*last), smooth, obs_count, innov, prec, image1, image2, seen1, seen2),
         [pltpu.VMEM((LAT_DEV + 2, WIDE, LEV), F32)],
-        limit=5, name="state_sums",
+        limit=5,
+        name="state_sums",
     )
     send2 = call(
         owner_last_kernel,
@@ -692,10 +774,24 @@
     state, bias, norms = call(
         finish_kernel,
         (FIELD, shape(NPRED, 2 * CHAN_HIGH * 128), shape(3)),
-        [SMEM] + [VMEM] * 5,
-        (sector, arrived3, a_field, b_field, pre, image_pre),
-        outs=(VMEM, VMEM, SMEM),
-        limit=6, name="finish",
+        [SMEM, VMEM, HBM, HBM, VMEM, VMEM],
+        (
+            sector,
+            arrived3,
+            pltpu.with_memory_space_constraint(a_field, pltpu.HBM),
+            pltpu.with_memory_space_constraint(b_field, pltpu.HBM),
+            pre,
+            image_pre,
+        ),
+        [
+            pltpu.VMEM((LAT_DEV, LON_DEV, LEV), F32),
+            pltpu.VMEM((LAT_DEV, LON_DEV, LEV), F32),
+            pltpu.SemaphoreType.DMA((2, OUT_PARTS)),
+            pltpu.SemaphoreType.DMA((OUT_PARTS,)),
+        ],
+        outs=(HBM, VMEM, SMEM),
+        limit=6,
+        name="finish",
     )
     return state, bias, norms
 

time: 159 us -> 148 us (0.931)
  waiting for transfers between devices: 18.3 us -> 32.2 us
  starting transfers between devices: 63.6 us -> 50.3 us
  blocking collectives: 20.3 us -> 15 us
  Pallas kernels: 51.2 us -> 48.3 us
  local copies, waits for them, and re-layouts: 2.73 us -> 0.15 us
    all_to_all x5, waiting for transfers between devices: 12.4 us -> 30.8 us  [exchange(): lax.all_to_all(array.reshape(DEVICES, 1, width), SWATH_CHAN, split_axis=0...]
    all_to_all x5, starting transfers between devices: 37 us -> 30.1 us  [exchange(): lax.all_to_all(array.reshape(DEVICES, 1, width), SWATH_CHAN, split_axis=0...]
    ppermute x6, starting transfers between devices: 16.8 us -> 10 us  [the longest x3 7.7 us: halo(): lax.ppermute(following, SWATH, other + [(b, a) for a, b in other])]
    all_to_all x1, blocking collectives: 20.3 us -> 15 us  [exchange(): lax.all_to_all(array.reshape(DEVICES, 1, width), SWATH_CHAN, split_axis=0...]
    ppermute x6, waiting for transfers between devices: 4.87 us -> 0.02 us  [the longest x3 0.01 us: halo(): lax.ppermute(following, SWATH, other + [(b, a) for a, b in other])]
    ppermute x3, starting transfers between devices: 5.49 us -> 8.43 us  [halo(): lax.ppermute(columns(lambda f: f[:, :width]), 'chan', [(b, a) for a, b in...]
    pallas_call x13 -> x10, Pallas kernels: 51.2 us -> 48.3 us  [call(): pl.pallas_call(kernel, out_shape=out_shape, in_specs=in_specs, out_specs=...]
    ppermute x3, starting transfers between devices: 4.29 us -> 1.7 us  [halo(): west = lax.ppermute(columns(lambda f: f[:, LON_DEV - width:]), 'chan', ring)]
  transfers between devices with their start and end apart: 17 -> 17, of which waited for: 6 -> 6; matrix products, arithmetic and copies ran while one was open for 0% -> 0% of each run, Pallas kernels for 13% -> 9%
where the time goes in v2:
time: 148 us
  starting transfers between devices  50.3 us (34%)
  Pallas kernels  48.3 us (33%)
  waiting for transfers between devices  32.2 us (22%)
  blocking collectives  15 us (10%)
  between operations  1.8 us (1%)
    pallas_call x10, Pallas kernels, call(): pl.pallas_call(kernel, out_shape=out_shape, in_specs=in_specs, out_specs=...  48.3 us
    all_to_all x5, waiting for transfers between devices, exchange(): lax.all_to_all(array.reshape(DEVICES, 1, width), SWATH_CHAN, split_axis=0...  30.8 us
    all_to_all x5, starting transfers between devices, exchange(): lax.all_to_all(array.reshape(DEVICES, 1, width), SWATH_CHAN, split_axis=0...  30.1 us
    all_to_all x1, blocking collectives, exchange(): lax.all_to_all(array.reshape(DEVICES, 1, width), SWATH_CHAN, split_axis=0...  15 us
    ppermute x3, starting transfers between devices, halo(): lax.ppermute(columns(lambda f: f[:, :width]), 'chan', [(b, a) for a, b in...  8.43 us
    ppermute x3, starting transfers between devices, halo(): lax.ppermute(following, SWATH, other + [(b, a) for a, b in other])  7.7 us
  transfers between devices with their start and end apart: 17, of which 6 were waited for; matrix products, arithmetic and copies ran while one was open for 0% of the time, Pallas kernels for 9%

profile of v2, /device:TPU:1, one launch (start us, length us, event | category | flops | bytes accessed | tf_op | source)
XLA Modules:
  0.0 147.9 jit_solution(18423479078739529922)
XLA Ops:
  1.3 0.0 copy-start.5
  1.3 11.3 %table_start.1 = (f32[768,128]{1,0:T(8,128)}, f32[32,64,128]{2,1,0:T(8,128)S(1)}, f32[2,64,128]{2,1,0:T(8,128)S(1)}, f32[2,64,128]{2,1,0:T(8,128)S(1)}, s32[128]{0:T(128)S(1)}, /*index=5*/s32[128,128]{1,0:T(8,128)S(1)}) custom-call(s32[1,1]{1,0:T(1,128)S(6)} %copy.21.count_ref, f32[128,128]{1,0:T(8,128)} %bitcast.44, f32[128,128]{1,0:T(8,128)} %bitcast.46, ...), custom_call_target="tpu_custom_call" | custom-call | flops 6000000000 | bytes 4194304 | tf_op jit(solution)/shard_map/table_start/pallas_call | solution.py:42
  12.6 0.0 copy-start.4
  12.6 1.5 collective-permute-start
  14.1 3.2 %collective-permute-start.1 = (f32[2,64,128]{2,1,0:T(8,128)S(1)}, f32[2,64,128]{2,1,0:T(8,128)S(1)}, u32[]{:S(2)}, u32[]{:S(2)}) collective-permute-start(f32[2,64,128]{2,1,0:T(8,128)S(1)} %get-tuple-element.34), channel_id=1, source_target_pairs={{4,8},{12,16},{20,24},{28,32},{36,40},{44,48},{52,56},{60,64},{68,... | collective-permute-start | bytes 196616 | tf_op jit(solution)/shard_map/ppermute | solution.py:597
  17.3 9.8 %all-to-all-start = ((f32[128,1,768]{2,1,0:T(1,128)}), f32[128,1,768]{2,1,0:T(1,128)S(1)}, u32[]{:S(2)}, u32[]{:S(2)}) async-start(f32[128,1,768]{2,1,0:T(1,128)} %bitcast.53), calls=%async_computation | async-start | bytes 786432 | tf_op jit(solution)/shard_map/all_to_all | solution.py:584
  27.2 0.0 collective-permute-done.pair_ref
  27.3 0.0 collective-permute-done.1.next_ref
  27.3 3.3 %collective-permute-start.3 = (f32[36,2,128]{2,1,0:T(2,128)S(1)}, f32[36,2,128]{2,1,0:T(2,128)S(1)}, u32[]{:S(2)}, u32[]{:S(2)}) collective-permute-start(f32[36,2,128]{2,1,0:T(2,128)S(1)} %pad_maximum_fusion.1), channel_id=1, source_target_pairs={{1,0},{2,1},{3,2},{0,3},{5,4},{6,5},{7,6},{4,7},{9,8},{10,9},{11,1... | collective-permute-start | bytes 110600 | tf_op jit(solution)/shard_map/ppermute | solution.py:606
  30.6 0.1 collective-permute-start.2
  30.7 8.9 %all-to-all-done = f32[128,1,768]{2,1,0:T(1,128)S(1)} async-done(((f32[128,1,768]{2,1,0:T(1,128)}), f32[128,1,768]{2,1,0:T(1,128)S(1)}, u32[]{:S(2)}, u32[]{:S(2)}) %all-to-all-start) | async-done | bytes 393248 | tf_op jit(solution)/shard_map/all_to_all | solution.py:584
  39.7 0.7 owner_start.1
  40.4 4.2 %all-to-all-start.1 = ((f32[128,1,384]{2,1,0:T(1,128)}), f32[128,1,384]{2,1,0:T(1,128)S(1)}, u32[]{:S(2)}, u32[]{:S(2)}) async-start(f32[128,1,384]{2,1,0:T(1,128)} %bitcast.10), calls=%async_computation.1 | async-start | bytes 393216 | tf_op jit(solution)/shard_map/all_to_all | solution.py:584
  44.6 0.0 collective-permute-done.3.east_ref
  44.6 0.0 collective-permute-done.2.west_ref
  44.6 5.3 %forward.2 = (f32[32,64,128]{2,1,0:T(8,128)}, f32[128,128]{1,0:T(8,128)S(1)}) custom-call(s32[128]{0:T(128)S(1)} %get-tuple-element.29.row_ref, f32[32,64,128]{2,1,0:T(8,128)S(1)} %get-tuple-element.32.field_ref, f32[2,64,128]{2,1,0:T(8,128)S(1)} %collective-permute-done.pair_ref, f32[2,64,128]{2,1,0:T(8,128)S(1)} %collective-permute-done.1.next_ref, ...), custom_call_target="tpu_custom_call" | custom-call | flops 2000000000 | bytes 4194304 | tf_op jit(solution)/shard_map/forward/pallas_call | solution.py:42
  49.9 5.1 %all-to-all-done.1 = f32[128,1,384]{2,1,0:T(1,128)S(1)} async-done(((f32[128,1,384]{2,1,0:T(1,128)}), f32[128,1,384]{2,1,0:T(1,128)S(1)}, u32[]{:S(2)}, u32[]{:S(2)}) %all-to-all-start.1) | async-done | bytes 196640 | tf_op jit(solution)/shard_map/all_to_all | solution.py:584
  55.0 10.5 %image.2 = (f32[384,128]{1,0:T(8,128)}, f32[128,128]{1,0:T(8,128)S(1)}, f32[32,64,128]{2,1,0:T(8,128)S(1)}, f32[2,64,128]{2,1,0:T(8,128)S(1)}, f32[2,64,128]{2,1,0:T(8,128)S(1)}) custom-call(s32[1,1]{1,0:T(1,128)S(6)} %copy.21.count_ref, s32[128]{0:T(128)S(1)} %get-tuple-element.29.row_ref, f32[384,128]{1,0:T(8,128)S(1)} %bitcast.30, ...), custom_call_target="tpu_custom_call" | custom-call | flops 6000000000 | bytes 4194304 | tf_op jit(solution)/shard_map/image/pallas_call | solution.py:42
  65.6 0.4 collective-permute-start.4
  66.0 2.2 %collective-permute-start.5 = (f32[2,64,128]{2,1,0:T(8,128)S(1)}, f32[2,64,128]{2,1,0:T(8,128)S(1)}, u32[]{:S(2)}, u32[]{:S(2)}) collective-permute-start(f32[2,64,128]{2,1,0:T(8,128)S(1)} %get-tuple-element.42), channel_id=1, source_target_pairs={{4,8},{12,16},{20,24},{28,32},{36,40},{44,48},{52,56},{60,64},{68,... | collective-permute-start | bytes 196616 | tf_op jit(solution)/shard_map/ppermute | solution.py:597
  68.3 5.9 %all-to-all-start.2 = ((f32[128,1,384]{2,1,0:T(1,128)}), f32[128,1,384]{2,1,0:T(1,128)S(1)}, u32[]{:S(2)}, u32[]{:S(2)}) async-start(f32[128,1,384]{2,1,0:T(1,128)} %bitcast.55), calls=%async_computation.2 | async-start | bytes 393216 | tf_op jit(solution)/shard_map/all_to_all | solution.py:584
  74.2 0.0 collective-permute-done.4.pair_ref
  74.2 0.0 collective-permute-done.5.next_ref
  74.3 3.3 %collective-permute-start.7 = (f32[36,2,128]{2,1,0:T(2,128)S(1)}, f32[36,2,128]{2,1,0:T(2,128)S(1)}, u32[]{:S(2)}, u32[]{:S(2)}) collective-permute-start(f32[36,2,128]{2,1,0:T(2,128)S(1)} %pad_maximum_fusion.3), channel_id=1, source_target_pairs={{1,0},{2,1},{3,2},{0,3},{5,4},{6,5},{7,6},{4,7},{9,8},{10,9},{11,1... | collective-permute-start | bytes 110600 | tf_op jit(solution)/shard_map/ppermute | solution.py:606
  77.6 0.1 collective-permute-start.6
  77.7 6.9 %all-to-all-done.2 = f32[128,1,384]{2,1,0:T(1,128)S(1)} async-done(((f32[128,1,384]{2,1,0:T(1,128)}), f32[128,1,384]{2,1,0:T(1,128)S(1)}, u32[]{:S(2)}, u32[]{:S(2)}) %all-to-all-start.2) | async-done | bytes 196640 | tf_op jit(solution)/shard_map/all_to_all | solution.py:584
  84.6 0.7 owner_next.1
  85.4 4.2 %all-to-all-start.3 = ((f32[128,1,384]{2,1,0:T(1,128)}), f32[128,1,384]{2,1,0:T(1,128)S(1)}, u32[]{:S(2)}, u32[]{:S(2)}) async-start(f32[128,1,384]{2,1,0:T(1,128)} %bitcast.15), calls=%async_computation.3 | async-start | bytes 393216 | tf_op jit(solution)/shard_map/all_to_all | solution.py:584
  89.6 0.0 collective-permute-done.7.east_ref
  89.6 0.0 collective-permute-done.6.west_ref
  89.6 5.3 %forward.3 = (f32[32,64,128]{2,1,0:T(8,128)}, f32[128,128]{1,0:T(8,128)S(1)}) custom-call(s32[128]{0:T(128)S(1)} %get-tuple-element.29.row_ref, f32[32,64,128]{2,1,0:T(8,128)S(1)} %get-tuple-element.40.field_ref, f32[2,64,128]{2,1,0:T(8,128)S(1)} %collective-permute-done.4.pair_ref, f32[2,64,128]{2,1,0:T(8,128)S(1)} %collective-permute-done.5.next_ref, ...), custom_call_target="tpu_custom_call" | custom-call | flops 2000000000 | bytes 4194304 | tf_op jit(solution)/shard_map/forward/pallas_call | solution.py:42
  94.9 5.1 %all-to-all-done.3 = f32[128,1,384]{2,1,0:T(1,128)S(1)} async-done(((f32[128,1,384]{2,1,0:T(1,128)}), f32[128,1,384]{2,1,0:T(1,128)S(1)}, u32[]{:S(2)}, u32[]{:S(2)}) %all-to-all-start.3) | async-done | bytes 196640 | tf_op jit(solution)/shard_map/all_to_all | solution.py:584
  100.0 10.5 %image.3 = (f32[384,128]{1,0:T(8,128)}, f32[128,128]{1,0:T(8,128)S(1)}, f32[32,64,128]{2,1,0:T(8,128)S(1)}, f32[1,64,128]{2,1,0:T(8,128)S(1)}, f32[1,64,128]{2,1,0:T(8,128)S(1)}) custom-call(s32[1,1]{1,0:T(1,128)S(6)} %copy.21.count_ref, s32[128]{0:T(128)S(1)} %get-tuple-element.29.row_ref, f32[384,128]{1,0:T(8,128)S(1)} %bitcast.32, ...), custom_call_target="tpu_custom_call" | custom-call | flops 6000000000 | bytes 4194304 | tf_op jit(solution)/shard_map/image/pallas_call | solution.py:42
  110.6 0.4 collective-permute-start.8
  111.0 2.2 %collective-permute-start.9 = (f32[1,64,128]{2,1,0:T(8,128)S(1)}, f32[1,64,128]{2,1,0:T(8,128)S(1)}, u32[]{:S(2)}, u32[]{:S(2)}) collective-permute-start(f32[1,64,128]{2,1,0:T(8,128)S(1)} %get-tuple-element.48), channel_id=1, source_target_pairs={{4,8},{12,16},{20,24},{28,32},{36,40},{44,48},{52,56},{60,64},{68,... | collective-permute-start | bytes 98312 | tf_op jit(solution)/shard_map/ppermute | solution.py:597
  113.2 5.9 %all-to-all-start.4 = ((f32[128,1,384]{2,1,0:T(1,128)}), f32[128,1,384]{2,1,0:T(1,128)S(1)}, u32[]{:S(2)}, u32[]{:S(2)}) async-start(f32[128,1,384]{2,1,0:T(1,128)} %bitcast.54), calls=%async_computation.4 | async-start | bytes 393216 | tf_op jit(solution)/shard_map/all_to_all | solution.py:584
  119.2 1.6 %collective-permute-start.10 = (f32[32,1,128]{2,1,0:T(1,128)S(1)}, f32[32,1,128]{2,1,0:T(1,128)S(1)}, u32[]{:S(2)}, u32[]{:S(2)}) collective-permute-start(f32[32,1,128]{2,1,0:T(1,128)S(1)} %get-tuple-element.56), channel_id=1, source_target_pairs={{0,1},{1,2},{2,3},{3,0},{4,5},{5,6},{6,7},{7,4},{8,9},{9,10},{10,1... | collective-permute-start | bytes 49160 | tf_op jit(solution)/shard_map/ppermute | solution.py:605
  120.8 1.8 %collective-permute-start.11 = (f32[32,1,128]{2,1,0:T(1,128)S(1)}, f32[32,1,128]{2,1,0:T(1,128)S(1)}, u32[]{:S(2)}, u32[]{:S(2)}) collective-permute-start(f32[32,1,128]{2,1,0:T(1,128)S(1)} %get-tuple-element.55), channel_id=1, source_target_pairs={{1,0},{2,1},{3,2},{0,3},{5,4},{6,5},{7,6},{4,7},{9,8},{10,9},{11,1... | collective-permute-start | bytes 49160 | tf_op jit(solution)/shard_map/ppermute | solution.py:606
  122.6 1.4 collective-permute-done.10.west_ref
  124.0 0.0 collective-permute-done.11.east_ref
  124.0 0.0 collective-permute-done.8.pair_ref
  124.0 0.0 collective-permute-done.9.next_ref
  124.0 0.0 copy-done.2
  124.0 0.8 state_sums.1.sums_ref
  124.8 4.8 %all-to-all-done.4 = f32[128,1,384]{2,1,0:T(1,128)S(1)} async-done(((f32[128,1,384]{2,1,0:T(1,128)}), f32[128,1,384]{2,1,0:T(1,128)S(1)}, u32[]{:S(2)}, u32[]{:S(2)}) %all-to-all-start.4) | async-done | bytes 196640 | tf_op jit(solution)/shard_map/all_to_all | solution.py:584
  129.6 0.1 owner_last.1
  129.7 15.0 %all_to_all.30 = f32[128,1,128]{2,1,0:T(1,128)S(1)} all-to-all(f32[128,1,128]{2,1,0:T(1,128)S(1)} %bitcast.37), channel_id=1, replica_groups=mesh['swath_0'=4,'swath_1'=4,'swath_2'=2,'chan'=4] {'swath_0','swath_1',..., dimensions={0} | all-to-all | bytes 131072 | tf_op jit(solution)/shard_map/all_to_all | solution.py:584
  144.8 3.0 %finish.1 = (f32[32,64,128]{2,1,0:T(8,128)}, f32[8,1280]{1,0:T(8,128)}, f32[3]{0:T(128)}) custom-call(s32[1]{0:T(128)} %bitcast.19.chan_ref, f32[128,128]{1,0:T(8,128)S(1)} %bitcast.36, f32[32,64,128]{2,1,0:T(8,128)} %get-tuple-element.53.a_hbm, f32[32,64,128]{2,1,0:T(8,128)} %get-tuple-element.54.b_hbm, f32[384,128]{1,0:T(8,128)S(1)} %bitcast.31, ...), custom_call_target="tpu_custom_call" | custom-call | flops 1000000000 | bytes 4194304 | tf_op jit(solution)/shard_map/finish/pallas_call | solution.py:42
  (24 shorter events, 0.2 us)
Async XLA Ops:
  1.3 25.9 %copy-start.5 = (f32[8,1280]{1,0:T(8,128)S(1)}, f32[8,1280]{1,0:T(8,128)}, u32[]{:S(2)}) copy-start(f32[8,1280]{1,0:T(8,128)} %param.17) | copy-start | bytes 122884
  12.6 32.0 %copy-start.4 = (f32[128]{0:T(128)S(1)}, f32[128]{0:T(128)}, u32[]{:S(2)}) copy-start(f32[128]{0:T(128)} %param.16) | copy-start | bytes 1540
  12.6 14.6 %collective-permute-start = (f32[2,64,128]{2,1,0:T(8,128)S(1)}, f32[2,64,128]{2,1,0:T(8,128)S(1)}, u32[]{:S(2)}, u32[]{:S(2)}) collective-permute-start(f32[2,64,128]{2,1,0:T(8,128)S(1)} %get-tuple-element.33), channel_id=1, source_target_pairs={{0,4},{4,0},{8,12},{12,8},{16,20},{20,16},{24,28},{28,24},{32,36},... | collective-permute-start | bytes 196616 | tf_op jit(solution)/shard_map/ppermute | solution.py:596
  14.1 13.2 %collective-permute-start.1 = (f32[2,64,128]{2,1,0:T(8,128)S(1)}, f32[2,64,128]{2,1,0:T(8,128)S(1)}, u32[]{:S(2)}, u32[]{:S(2)}) collective-permute-start(f32[2,64,128]{2,1,0:T(8,128)S(1)} %get-tuple-element.34), channel_id=1, source_target_pairs={{4,8},{12,16},{20,24},{28,32},{36,40},{44,48},{52,56},{60,64},{68,... | collective-permute-start | bytes 196616 | tf_op jit(solution)/shard_map/ppermute | solution.py:597
  17.3 22.3 %all-to-all-start = ((f32[128,1,768]{2,1,0:T(1,128)}), f32[128,1,768]{2,1,0:T(1,128)S(1)}, u32[]{:S(2)}, u32[]{:S(2)}) async-start(f32[128,1,768]{2,1,0:T(1,128)} %bitcast.53), calls=%async_computation | async-start | bytes 786432 | tf_op jit(solution)/shard_map/all_to_all | solution.py:584
  27.3 17.3 %collective-permute-start.3 = (f32[36,2,128]{2,1,0:T(2,128)S(1)}, f32[36,2,128]{2,1,0:T(2,128)S(1)}, u32[]{:S(2)}, u32[]{:S(2)}) collective-permute-start(f32[36,2,128]{2,1,0:T(2,128)S(1)} %pad_maximum_fusion.1), channel_id=1, source_target_pairs={{1,0},{2,1},{3,2},{0,3},{5,4},{6,5},{7,6},{4,7},{9,8},{10,9},{11,1... | collective-permute-start | bytes 110600 | tf_op jit(solution)/shard_map/ppermute | solution.py:606
  30.6 14.0 %collective-permute-start.2 = (f32[36,2,128]{2,1,0:T(2,128)S(1)}, f32[36,2,128]{2,1,0:T(2,128)S(1)}, u32[]{:S(2)}, u32[]{:S(2)}) collective-permute-start(f32[36,2,128]{2,1,0:T(2,128)S(1)} %pad_maximum_fusion), channel_id=1, source_target_pairs={{0,1},{1,2},{2,3},{3,0},{4,5},{5,6},{6,7},{7,4},{8,9},{9,10},{10,1... | collective-permute-start | bytes 110600 | tf_op jit(solution)/shard_map/ppermute | solution.py:605
  40.4 14.6 %copy-start = (f32[8,16384]{1,0:T(8,128)S(1)}, f32[8,16384]{1,0:T(8,128)}, u32[]{:S(2)}) copy-start(f32[8,16384]{1,0:T(8,128)} %pred_ref.3) | copy-start | bytes 1572868
  40.4 14.6 %copy-start.1 = (s32[16384]{0:T(1024)S(1)}, s32[16384]{0:T(1024)}, u32[]{:S(2)}) copy-start(s32[16384]{0:T(1024)} %param.14) | copy-start | bytes 196612
  40.4 14.6 %copy-start.3 = (f32[16384]{0:T(1024)S(1)}, f32[16384]{0:T(1024)}, u32[]{:S(2)}) copy-start(f32[16384]{0:T(1024)} %param.10) | copy-start | bytes 196612
  40.4 14.6 %all-to-all-start.1 = ((f32[128,1,384]{2,1,0:T(1,128)}), f32[128,1,384]{2,1,0:T(1,128)S(1)}, u32[]{:S(2)}, u32[]{:S(2)}) async-start(f32[128,1,384]{2,1,0:T(1,128)} %bitcast.10), calls=%async_computation.1 | async-start | bytes 393216 | tf_op jit(solution)/shard_map/all_to_all | solution.py:584
  65.6 8.7 %collective-permute-start.4 = (f32[2,64,128]{2,1,0:T(8,128)S(1)}, f32[2,64,128]{2,1,0:T(8,128)S(1)}, u32[]{:S(2)}, u32[]{:S(2)}) collective-permute-start(f32[2,64,128]{2,1,0:T(8,128)S(1)} %get-tuple-element.41), channel_id=1, source_target_pairs={{0,4},{4,0},{8,12},{12,8},{16,20},{20,16},{24,28},{28,24},{32,36},... | collective-permute-start | bytes 196616 | tf_op jit(solution)/shard_map/ppermute | solution.py:596
  66.0 8.3 %collective-permute-start.5 = (f32[2,64,128]{2,1,0:T(8,128)S(1)}, f32[2,64,128]{2,1,0:T(8,128)S(1)}, u32[]{:S(2)}, u32[]{:S(2)}) collective-permute-start(f32[2,64,128]{2,1,0:T(8,128)S(1)} %get-tuple-element.42), channel_id=1, source_target_pairs={{4,8},{12,16},{20,24},{28,32},{36,40},{44,48},{52,56},{60,64},{68,... | collective-permute-start | bytes 196616 | tf_op jit(solution)/shard_map/ppermute | solution.py:597
  68.3 16.3 %all-to-all-start.2 = ((f32[128,1,384]{2,1,0:T(1,128)}), f32[128,1,384]{2,1,0:T(1,128)S(1)}, u32[]{:S(2)}, u32[]{:S(2)}) async-start(f32[128,1,384]{2,1,0:T(1,128)} %bitcast.55), calls=%async_computation.2 | async-start | bytes 393216 | tf_op jit(solution)/shard_map/all_to_all | solution.py:584
  74.3 15.3 %collective-permute-start.7 = (f32[36,2,128]{2,1,0:T(2,128)S(1)}, f32[36,2,128]{2,1,0:T(2,128)S(1)}, u32[]{:S(2)}, u32[]{:S(2)}) collective-permute-start(f32[36,2,128]{2,1,0:T(2,128)S(1)} %pad_maximum_fusion.3), channel_id=1, source_target_pairs={{1,0},{2,1},{3,2},{0,3},{5,4},{6,5},{7,6},{4,7},{9,8},{10,9},{11,1... | collective-permute-start | bytes 110600 | tf_op jit(solution)/shard_map/ppermute | solution.py:606
  77.6 12.0 %collective-permute-start.6 = (f32[36,2,128]{2,1,0:T(2,128)S(1)}, f32[36,2,128]{2,1,0:T(2,128)S(1)}, u32[]{:S(2)}, u32[]{:S(2)}) collective-permute-start(f32[36,2,128]{2,1,0:T(2,128)S(1)} %pad_maximum_fusion.2), channel_id=1, source_target_pairs={{0,1},{1,2},{2,3},{3,0},{4,5},{5,6},{6,7},{7,4},{8,9},{9,10},{10,1... | collective-permute-start | bytes 110600 | tf_op jit(solution)/shard_map/ppermute | solution.py:605
  85.4 14.7 %all-to-all-start.3 = ((f32[128,1,384]{2,1,0:T(1,128)}), f32[128,1,384]{2,1,0:T(1,128)S(1)}, u32[]{:S(2)}, u32[]{:S(2)}) async-start(f32[128,1,384]{2,1,0:T(1,128)} %bitcast.15), calls=%async_computation.3 | async-start | bytes 393216 | tf_op jit(solution)/shard_map/all_to_all | solution.py:584
  100.0 24.0 %copy-start.2 = (f32[16384]{0:T(1024)S(1)}, f32[16384]{0:T(1024)}, u32[]{:S(2)}) copy-start(f32[16384]{0:T(1024)} %param.9) | copy-start | bytes 196612
  110.6 13.4 %collective-permute-start.8 = (f32[1,64,128]{2,1,0:T(8,128)S(1)}, f32[1,64,128]{2,1,0:T(8,128)S(1)}, u32[]{:S(2)}, u32[]{:S(2)}) collective-permute-start(f32[1,64,128]{2,1,0:T(8,128)S(1)} %get-tuple-element.47), channel_id=1, source_target_pairs={{0,4},{4,0},{8,12},{12,8},{16,20},{20,16},{24,28},{28,24},{32,36},... | collective-permute-start | bytes 98312 | tf_op jit(solution)/shard_map/ppermute | solution.py:596
  111.0 13.0 %collective-permute-start.9 = (f32[1,64,128]{2,1,0:T(8,128)S(1)}, f32[1,64,128]{2,1,0:T(8,128)S(1)}, u32[]{:S(2)}, u32[]{:S(2)}) collective-permute-start(f32[1,64,128]{2,1,0:T(8,128)S(1)} %get-tuple-element.48), channel_id=1, source_target_pairs={{4,8},{12,16},{20,24},{28,32},{36,40},{44,48},{52,56},{60,64},{68,... | collective-permute-start | bytes 98312 | tf_op jit(solution)/shard_map/ppermute | solution.py:597
  113.2 16.4 %all-to-all-start.4 = ((f32[128,1,384]{2,1,0:T(1,128)}), f32[128,1,384]{2,1,0:T(1,128)S(1)}, u32[]{:S(2)}, u32[]{:S(2)}) async-start(f32[128,1,384]{2,1,0:T(1,128)} %bitcast.54), calls=%async_computation.4 | async-start | bytes 393216 | tf_op jit(solution)/shard_map/all_to_all | solution.py:584
  119.2 4.7 %collective-permute-start.10 = (f32[32,1,128]{2,1,0:T(1,128)S(1)}, f32[32,1,128]{2,1,0:T(1,128)S(1)}, u32[]{:S(2)}, u32[]{:S(2)}) collective-permute-start(f32[32,1,128]{2,1,0:T(1,128)S(1)} %get-tuple-element.56), channel_id=1, source_target_pairs={{0,1},{1,2},{2,3},{3,0},{4,5},{5,6},{6,7},{7,4},{8,9},{9,10},{10,1... | collective-permute-start | bytes 49160 | tf_op jit(solution)/shard_map/ppermute | solution.py:605
  120.8 3.2 %collective-permute-start.11 = (f32[32,1,128]{2,1,0:T(1,128)S(1)}, f32[32,1,128]{2,1,0:T(1,128)S(1)}, u32[]{:S(2)}, u32[]{:S(2)}) collective-permute-start(f32[32,1,128]{2,1,0:T(1,128)S(1)} %get-tuple-element.55), channel_id=1, source_target_pairs={{1,0},{2,1},{3,2},{0,3},{5,4},{6,5},{7,6},{4,7},{9,8},{10,9},{11,1... | collective-permute-start | bytes 49160 | tf_op jit(solution)/shard_map/ppermute | solution.py:606

commit v3 on v2

--- a/solution.py
+++ b/solution.py
@@ -18,7 +18,7 @@
 GROUP = 8
 KSLOT = GROUP * LINE
 SUBS = 8
-UNROLL = 32
+UNROLL = 64
 STAGES = LINES // UNROLL
 LOW = 256
 HIGH = 20

time: 148 us -> 148 us (level)
  no operation moved by 1% of the time
where the time goes in v3:
time: 148 us; the launch traced here: 147 us
  starting transfers between devices  50.3 us (34%)
  Pallas kernels  47.6 us (32%)
  waiting for transfers between devices  32.2 us (22%)
  blocking collectives  15 us (10%)
  between operations  1.82 us (1%)
    pallas_call x10, Pallas kernels, call(): pl.pallas_call(kernel, out_shape=out_shape, in_specs=in_specs, out_specs=...  47.6 us
    all_to_all x5, waiting for transfers between devices, exchange(): lax.all_to_all(array.reshape(DEVICES, 1, width), SWATH_CHAN, split_axis=0...  30.8 us
    all_to_all x5, starting transfers between devices, exchange(): lax.all_to_all(array.reshape(DEVICES, 1, width), SWATH_CHAN, split_axis=0...  30.1 us
    all_to_all x1, blocking collectives, exchange(): lax.all_to_all(array.reshape(DEVICES, 1, width), SWATH_CHAN, split_axis=0...  15 us
    ppermute x3, starting transfers between devices, halo(): lax.ppermute(columns(lambda f: f[:, :width]), 'chan', [(b, a) for a, b in...  8.43 us
    ppermute x3, starting transfers between devices, halo(): lax.ppermute(following, SWATH, other + [(b, a) for a, b in other])  7.7 us
  transfers between devices with their start and end apart: 17, of which 6 were waited for; matrix products, arithmetic and copies ran while one was open for 0% of the time, Pallas kernels for 9%

profile of v3, /device:TPU:1, one launch (start us, length us, event | category | flops | bytes accessed | tf_op | source)
XLA Modules:
  0.0 147.2 jit_solution(12845109550401090264)
XLA Ops:
  1.3 11.1 %table_start.1 = (f32[768,128]{1,0:T(8,128)}, f32[32,64,128]{2,1,0:T(8,128)S(1)}, f32[2,64,128]{2,1,0:T(8,128)S(1)}, f32[2,64,128]{2,1,0:T(8,128)S(1)}, s32[128]{0:T(128)S(1)}, /*index=5*/s32[128,128]{1,0:T(8,128)S(1)}) custom-call(s32[1,1]{1,0:T(1,128)S(6)} %copy.21.count_ref, f32[128,128]{1,0:T(8,128)} %bitcast.44, f32[128,128]{1,0:T(8,128)} %bitcast.46, ...), custom_call_target="tpu_custom_call" | custom-call | flops 6000000000 | bytes 4194304 | tf_op jit(solution)/shard_map/table_start/pallas_call | solution.py:42
  12.4 0.0 copy-start.4
  12.4 1.5 collective-permute-start
  13.8 3.2 %collective-permute-start.1 = (f32[2,64,128]{2,1,0:T(8,128)S(1)}, f32[2,64,128]{2,1,0:T(8,128)S(1)}, u32[]{:S(2)}, u32[]{:S(2)}) collective-permute-start(f32[2,64,128]{2,1,0:T(8,128)S(1)} %get-tuple-element.34), channel_id=1, source_target_pairs={{4,8},{12,16},{20,24},{28,32},{36,40},{44,48},{52,56},{60,64},{68,... | collective-permute-start | bytes 196616 | tf_op jit(solution)/shard_map/ppermute | solution.py:597
  17.0 9.8 %all-to-all-start = ((f32[128,1,768]{2,1,0:T(1,128)}), f32[128,1,768]{2,1,0:T(1,128)S(1)}, u32[]{:S(2)}, u32[]{:S(2)}) async-start(f32[128,1,768]{2,1,0:T(1,128)} %bitcast.53), calls=%async_computation | async-start | bytes 786432 | tf_op jit(solution)/shard_map/all_to_all | solution.py:584
  27.0 0.0 collective-permute-done.pair_ref
  27.0 0.0 collective-permute-done.1.next_ref
  27.1 3.3 %collective-permute-start.3 = (f32[36,2,128]{2,1,0:T(2,128)S(1)}, f32[36,2,128]{2,1,0:T(2,128)S(1)}, u32[]{:S(2)}, u32[]{:S(2)}) collective-permute-start(f32[36,2,128]{2,1,0:T(2,128)S(1)} %pad_maximum_fusion.1), channel_id=1, source_target_pairs={{1,0},{2,1},{3,2},{0,3},{5,4},{6,5},{7,6},{4,7},{9,8},{10,9},{11,1... | collective-permute-start | bytes 110600 | tf_op jit(solution)/shard_map/ppermute | solution.py:606
  30.4 0.1 collective-permute-start.2
  30.5 8.9 %all-to-all-done = f32[128,1,768]{2,1,0:T(1,128)S(1)} async-done(((f32[128,1,768]{2,1,0:T(1,128)}), f32[128,1,768]{2,1,0:T(1,128)S(1)}, u32[]{:S(2)}, u32[]{:S(2)}) %all-to-all-start) | async-done | bytes 393248 | tf_op jit(solution)/shard_map/all_to_all | solution.py:584
  39.4 0.7 owner_start.1
  40.1 4.2 %all-to-all-start.1 = ((f32[128,1,384]{2,1,0:T(1,128)}), f32[128,1,384]{2,1,0:T(1,128)S(1)}, u32[]{:S(2)}, u32[]{:S(2)}) async-start(f32[128,1,384]{2,1,0:T(1,128)} %bitcast.10), calls=%async_computation.1 | async-start | bytes 393216 | tf_op jit(solution)/shard_map/all_to_all | solution.py:584
  44.3 0.0 collective-permute-done.3.east_ref
  44.3 0.0 collective-permute-done.2.west_ref
  44.3 0.0 copy-done.4
  44.3 5.2 %forward.2 = (f32[32,64,128]{2,1,0:T(8,128)}, f32[128,128]{1,0:T(8,128)S(1)}) custom-call(s32[128]{0:T(128)S(1)} %get-tuple-element.29.row_ref, f32[32,64,128]{2,1,0:T(8,128)S(1)} %get-tuple-element.32.field_ref, f32[2,64,128]{2,1,0:T(8,128)S(1)} %collective-permute-done.pair_ref, f32[2,64,128]{2,1,0:T(8,128)S(1)} %collective-permute-done.1.next_ref, ...), custom_call_target="tpu_custom_call" | custom-call | flops 2000000000 | bytes 4194304 | tf_op jit(solution)/shard_map/forward/pallas_call | solution.py:42
  49.6 5.1 %all-to-all-done.1 = f32[128,1,384]{2,1,0:T(1,128)S(1)} async-done(((f32[128,1,384]{2,1,0:T(1,128)}), f32[128,1,384]{2,1,0:T(1,128)S(1)}, u32[]{:S(2)}, u32[]{:S(2)}) %all-to-all-start.1) | async-done | bytes 196640 | tf_op jit(solution)/shard_map/all_to_all | solution.py:584
  54.7 0.0 copy-done
  54.7 10.3 %image.2 = (f32[384,128]{1,0:T(8,128)}, f32[128,128]{1,0:T(8,128)S(1)}, f32[32,64,128]{2,1,0:T(8,128)S(1)}, f32[2,64,128]{2,1,0:T(8,128)S(1)}, f32[2,64,128]{2,1,0:T(8,128)S(1)}) custom-call(s32[1,1]{1,0:T(1,128)S(6)} %copy.21.count_ref, s32[128]{0:T(128)S(1)} %get-tuple-element.29.row_ref, f32[384,128]{1,0:T(8,128)S(1)} %bitcast.30, ...), custom_call_target="tpu_custom_call" | custom-call | flops 6000000000 | bytes 4194304 | tf_op jit(solution)/shard_map/image/pallas_call | solution.py:42
  65.1 0.4 collective-permute-start.4
  65.5 2.2 %collective-permute-start.5 = (f32[2,64,128]{2,1,0:T(8,128)S(1)}, f32[2,64,128]{2,1,0:T(8,128)S(1)}, u32[]{:S(2)}, u32[]{:S(2)}) collective-permute-start(f32[2,64,128]{2,1,0:T(8,128)S(1)} %get-tuple-element.42), channel_id=1, source_target_pairs={{4,8},{12,16},{20,24},{28,32},{36,40},{44,48},{52,56},{60,64},{68,... | collective-permute-start | bytes 196616 | tf_op jit(solution)/shard_map/ppermute | solution.py:597
  67.8 5.9 %all-to-all-start.2 = ((f32[128,1,384]{2,1,0:T(1,128)}), f32[128,1,384]{2,1,0:T(1,128)S(1)}, u32[]{:S(2)}, u32[]{:S(2)}) async-start(f32[128,1,384]{2,1,0:T(1,128)} %bitcast.55), calls=%async_computation.2 | async-start | bytes 393216 | tf_op jit(solution)/shard_map/all_to_all | solution.py:584
  73.7 0.0 collective-permute-done.4.pair_ref
  73.7 0.0 collective-permute-done.5.next_ref
  73.8 3.3 %collective-permute-start.7 = (f32[36,2,128]{2,1,0:T(2,128)S(1)}, f32[36,2,128]{2,1,0:T(2,128)S(1)}, u32[]{:S(2)}, u32[]{:S(2)}) collective-permute-start(f32[36,2,128]{2,1,0:T(2,128)S(1)} %pad_maximum_fusion.3), channel_id=1, source_target_pairs={{1,0},{2,1},{3,2},{0,3},{5,4},{6,5},{7,6},{4,7},{9,8},{10,9},{11,1... | collective-permute-start | bytes 110600 | tf_op jit(solution)/shard_map/ppermute | solution.py:606
  77.1 0.1 collective-permute-start.6
  77.2 6.9 %all-to-all-done.2 = f32[128,1,384]{2,1,0:T(1,128)S(1)} async-done(((f32[128,1,384]{2,1,0:T(1,128)}), f32[128,1,384]{2,1,0:T(1,128)S(1)}, u32[]{:S(2)}, u32[]{:S(2)}) %all-to-all-start.2) | async-done | bytes 196640 | tf_op jit(solution)/shard_map/all_to_all | solution.py:584
  84.1 0.7 owner_next.1
  84.9 4.3 %all-to-all-start.3 = ((f32[128,1,384]{2,1,0:T(1,128)}), f32[128,1,384]{2,1,0:T(1,128)S(1)}, u32[]{:S(2)}, u32[]{:S(2)}) async-start(f32[128,1,384]{2,1,0:T(1,128)} %bitcast.15), calls=%async_computation.3 | async-start | bytes 393216 | tf_op jit(solution)/shard_map/all_to_all | solution.py:584
  89.1 0.0 collective-permute-done.7.east_ref
  89.1 0.0 collective-permute-done.6.west_ref
  89.1 5.2 %forward.3 = (f32[32,64,128]{2,1,0:T(8,128)}, f32[128,128]{1,0:T(8,128)S(1)}) custom-call(s32[128]{0:T(128)S(1)} %get-tuple-element.29.row_ref, f32[32,64,128]{2,1,0:T(8,128)S(1)} %get-tuple-element.40.field_ref, f32[2,64,128]{2,1,0:T(8,128)S(1)} %collective-permute-done.4.pair_ref, f32[2,64,128]{2,1,0:T(8,128)S(1)} %collective-permute-done.5.next_ref, ...), custom_call_target="tpu_custom_call" | custom-call | flops 2000000000 | bytes 4194304 | tf_op jit(solution)/shard_map/forward/pallas_call | solution.py:42
  94.4 5.1 %all-to-all-done.3 = f32[128,1,384]{2,1,0:T(1,128)S(1)} async-done(((f32[128,1,384]{2,1,0:T(1,128)}), f32[128,1,384]{2,1,0:T(1,128)S(1)}, u32[]{:S(2)}, u32[]{:S(2)}) %all-to-all-start.3) | async-done | bytes 196640 | tf_op jit(solution)/shard_map/all_to_all | solution.py:584
  99.5 10.3 %image.3 = (f32[384,128]{1,0:T(8,128)}, f32[128,128]{1,0:T(8,128)S(1)}, f32[32,64,128]{2,1,0:T(8,128)S(1)}, f32[1,64,128]{2,1,0:T(8,128)S(1)}, f32[1,64,128]{2,1,0:T(8,128)S(1)}) custom-call(s32[1,1]{1,0:T(1,128)S(6)} %copy.21.count_ref, s32[128]{0:T(128)S(1)} %get-tuple-element.29.row_ref, f32[384,128]{1,0:T(8,128)S(1)} %bitcast.32, ...), custom_call_target="tpu_custom_call" | custom-call | flops 6000000000 | bytes 4194304 | tf_op jit(solution)/shard_map/image/pallas_call | solution.py:42
  109.8 0.4 collective-permute-start.8
  110.3 2.2 %collective-permute-start.9 = (f32[1,64,128]{2,1,0:T(8,128)S(1)}, f32[1,64,128]{2,1,0:T(8,128)S(1)}, u32[]{:S(2)}, u32[]{:S(2)}) collective-permute-start(f32[1,64,128]{2,1,0:T(8,128)S(1)} %get-tuple-element.48), channel_id=1, source_target_pairs={{4,8},{12,16},{20,24},{28,32},{36,40},{44,48},{52,56},{60,64},{68,... | collective-permute-start | bytes 98312 | tf_op jit(solution)/shard_map/ppermute | solution.py:597
  112.5 5.9 %all-to-all-start.4 = ((f32[128,1,384]{2,1,0:T(1,128)}), f32[128,1,384]{2,1,0:T(1,128)S(1)}, u32[]{:S(2)}, u32[]{:S(2)}) async-start(f32[128,1,384]{2,1,0:T(1,128)} %bitcast.54), calls=%async_computation.4 | async-start | bytes 393216 | tf_op jit(solution)/shard_map/all_to_all | solution.py:584
  118.5 1.6 %collective-permute-start.10 = (f32[32,1,128]{2,1,0:T(1,128)S(1)}, f32[32,1,128]{2,1,0:T(1,128)S(1)}, u32[]{:S(2)}, u32[]{:S(2)}) collective-permute-start(f32[32,1,128]{2,1,0:T(1,128)S(1)} %get-tuple-element.56), channel_id=1, source_target_pairs={{0,1},{1,2},{2,3},{3,0},{4,5},{5,6},{6,7},{7,4},{8,9},{9,10},{10,1... | collective-permute-start | bytes 49160 | tf_op jit(solution)/shard_map/ppermute | solution.py:605
  120.1 1.8 %collective-permute-start.11 = (f32[32,1,128]{2,1,0:T(1,128)S(1)}, f32[32,1,128]{2,1,0:T(1,128)S(1)}, u32[]{:S(2)}, u32[]{:S(2)}) collective-permute-start(f32[32,1,128]{2,1,0:T(1,128)S(1)} %get-tuple-element.55), channel_id=1, source_target_pairs={{1,0},{2,1},{3,2},{0,3},{5,4},{6,5},{7,6},{4,7},{9,8},{10,9},{11,1... | collective-permute-start | bytes 49160 | tf_op jit(solution)/shard_map/ppermute | solution.py:606
  121.9 1.4 collective-permute-done.10.west_ref
  123.2 0.0 collective-permute-done.11.east_ref
  123.2 0.0 collective-permute-done.8.pair_ref
  123.2 0.0 collective-permute-done.9.next_ref
  123.3 0.8 state_sums.1.sums_ref
  124.1 4.8 %all-to-all-done.4 = f32[128,1,384]{2,1,0:T(1,128)S(1)} async-done(((f32[128,1,384]{2,1,0:T(1,128)}), f32[128,1,384]{2,1,0:T(1,128)S(1)}, u32[]{:S(2)}, u32[]{:S(2)}) %all-to-all-start.4) | async-done | bytes 196640 | tf_op jit(solution)/shard_map/all_to_all | solution.py:584
  128.9 0.1 owner_last.1
  129.0 15.0 %all_to_all.30 = f32[128,1,128]{2,1,0:T(1,128)S(1)} all-to-all(f32[128,1,128]{2,1,0:T(1,128)S(1)} %bitcast.37), channel_id=1, replica_groups=mesh['swath_0'=4,'swath_1'=4,'swath_2'=2,'chan'=4] {'swath_0','swath_1',..., dimensions={0} | all-to-all | bytes 131072 | tf_op jit(solution)/shard_map/all_to_all | solution.py:584
  144.0 3.0 %finish.1 = (f32[32,64,128]{2,1,0:T(8,128)}, f32[8,1280]{1,0:T(8,128)}, f32[3]{0:T(128)}) custom-call(s32[1]{0:T(128)} %bitcast.19.chan_ref, f32[128,128]{1,0:T(8,128)S(1)} %bitcast.36, f32[32,64,128]{2,1,0:T(8,128)} %get-tuple-element.53.a_hbm, f32[32,64,128]{2,1,0:T(8,128)} %get-tuple-element.54.b_hbm, f32[384,128]{1,0:T(8,128)S(1)} %bitcast.31, ...), custom_call_target="tpu_custom_call" | custom-call | flops 1000000000 | bytes 4194304 | tf_op jit(solution)/shard_map/finish/pallas_call | solution.py:42
  (24 shorter events, 0.2 us)
Async XLA Ops:
  1.3 25.6 %copy-start.5 = (f32[8,1280]{1,0:T(8,128)S(1)}, f32[8,1280]{1,0:T(8,128)}, u32[]{:S(2)}) copy-start(f32[8,1280]{1,0:T(8,128)} %param.17) | copy-start | bytes 122884
  12.4 32.0 %copy-start.4 = (f32[128]{0:T(128)S(1)}, f32[128]{0:T(128)}, u32[]{:S(2)}) copy-start(f32[128]{0:T(128)} %param.16) | copy-start | bytes 1540
  12.4 14.6 %collective-permute-start = (f32[2,64,128]{2,1,0:T(8,128)S(1)}, f32[2,64,128]{2,1,0:T(8,128)S(1)}, u32[]{:S(2)}, u32[]{:S(2)}) collective-permute-start(f32[2,64,128]{2,1,0:T(8,128)S(1)} %get-tuple-element.33), channel_id=1, source_target_pairs={{0,4},{4,0},{8,12},{12,8},{16,20},{20,16},{24,28},{28,24},{32,36},... | collective-permute-start | bytes 196616 | tf_op jit(solution)/shard_map/ppermute | solution.py:596
  13.8 13.2 %collective-permute-start.1 = (f32[2,64,128]{2,1,0:T(8,128)S(1)}, f32[2,64,128]{2,1,0:T(8,128)S(1)}, u32[]{:S(2)}, u32[]{:S(2)}) collective-permute-start(f32[2,64,128]{2,1,0:T(8,128)S(1)} %get-tuple-element.34), channel_id=1, source_target_pairs={{4,8},{12,16},{20,24},{28,32},{36,40},{44,48},{52,56},{60,64},{68,... | collective-permute-start | bytes 196616 | tf_op jit(solution)/shard_map/ppermute | solution.py:597
  17.0 22.3 %all-to-all-start = ((f32[128,1,768]{2,1,0:T(1,128)}), f32[128,1,768]{2,1,0:T(1,128)S(1)}, u32[]{:S(2)}, u32[]{:S(2)}) async-start(f32[128,1,768]{2,1,0:T(1,128)} %bitcast.53), calls=%async_computation | async-start | bytes 786432 | tf_op jit(solution)/shard_map/all_to_all | solution.py:584
  27.1 17.3 %collective-permute-start.3 = (f32[36,2,128]{2,1,0:T(2,128)S(1)}, f32[36,2,128]{2,1,0:T(2,128)S(1)}, u32[]{:S(2)}, u32[]{:S(2)}) collective-permute-start(f32[36,2,128]{2,1,0:T(2,128)S(1)} %pad_maximum_fusion.1), channel_id=1, source_target_pairs={{1,0},{2,1},{3,2},{0,3},{5,4},{6,5},{7,6},{4,7},{9,8},{10,9},{11,1... | collective-permute-start | bytes 110600 | tf_op jit(solution)/shard_map/ppermute | solution.py:606
  30.4 14.0 %collective-permute-start.2 = (f32[36,2,128]{2,1,0:T(2,128)S(1)}, f32[36,2,128]{2,1,0:T(2,128)S(1)}, u32[]{:S(2)}, u32[]{:S(2)}) collective-permute-start(f32[36,2,128]{2,1,0:T(2,128)S(1)} %pad_maximum_fusion), channel_id=1, source_target_pairs={{0,1},{1,2},{2,3},{3,0},{4,5},{5,6},{6,7},{7,4},{8,9},{9,10},{10,1... | collective-permute-start | bytes 110600 | tf_op jit(solution)/shard_map/ppermute | solution.py:605
  40.1 14.6 %copy-start = (f32[8,16384]{1,0:T(8,128)S(1)}, f32[8,16384]{1,0:T(8,128)}, u32[]{:S(2)}) copy-start(f32[8,16384]{1,0:T(8,128)} %pred_ref.3) | copy-start | bytes 1572868
  40.1 14.6 %copy-start.1 = (s32[16384]{0:T(1024)S(1)}, s32[16384]{0:T(1024)}, u32[]{:S(2)}) copy-start(s32[16384]{0:T(1024)} %param.14) | copy-start | bytes 196612
  40.1 14.6 %copy-start.3 = (f32[16384]{0:T(1024)S(1)}, f32[16384]{0:T(1024)}, u32[]{:S(2)}) copy-start(f32[16384]{0:T(1024)} %param.10) | copy-start | bytes 196612
  40.1 14.6 %all-to-all-start.1 = ((f32[128,1,384]{2,1,0:T(1,128)}), f32[128,1,384]{2,1,0:T(1,128)S(1)}, u32[]{:S(2)}, u32[]{:S(2)}) async-start(f32[128,1,384]{2,1,0:T(1,128)} %bitcast.10), calls=%async_computation.1 | async-start | bytes 393216 | tf_op jit(solution)/shard_map/all_to_all | solution.py:584
  65.1 8.7 %collective-permute-start.4 = (f32[2,64,128]{2,1,0:T(8,128)S(1)}, f32[2,64,128]{2,1,0:T(8,128)S(1)}, u32[]{:S(2)}, u32[]{:S(2)}) collective-permute-start(f32[2,64,128]{2,1,0:T(8,128)S(1)} %get-tuple-element.41), channel_id=1, source_target_pairs={{0,4},{4,0},{8,12},{12,8},{16,20},{20,16},{24,28},{28,24},{32,36},... | collective-permute-start | bytes 196616 | tf_op jit(solution)/shard_map/ppermute | solution.py:596
  65.5 8.3 %collective-permute-start.5 = (f32[2,64,128]{2,1,0:T(8,128)S(1)}, f32[2,64,128]{2,1,0:T(8,128)S(1)}, u32[]{:S(2)}, u32[]{:S(2)}) collective-permute-start(f32[2,64,128]{2,1,0:T(8,128)S(1)} %get-tuple-element.42), channel_id=1, source_target_pairs={{4,8},{12,16},{20,24},{28,32},{36,40},{44,48},{52,56},{60,64},{68,... | collective-permute-start | bytes 196616 | tf_op jit(solution)/shard_map/ppermute | solution.py:597
  67.8 16.4 %all-to-all-start.2 = ((f32[128,1,384]{2,1,0:T(1,128)}), f32[128,1,384]{2,1,0:T(1,128)S(1)}, u32[]{:S(2)}, u32[]{:S(2)}) async-start(f32[128,1,384]{2,1,0:T(1,128)} %bitcast.55), calls=%async_computation.2 | async-start | bytes 393216 | tf_op jit(solution)/shard_map/all_to_all | solution.py:584
  73.8 15.3 %collective-permute-start.7 = (f32[36,2,128]{2,1,0:T(2,128)S(1)}, f32[36,2,128]{2,1,0:T(2,128)S(1)}, u32[]{:S(2)}, u32[]{:S(2)}) collective-permute-start(f32[36,2,128]{2,1,0:T(2,128)S(1)} %pad_maximum_fusion.3), channel_id=1, source_target_pairs={{1,0},{2,1},{3,2},{0,3},{5,4},{6,5},{7,6},{4,7},{9,8},{10,9},{11,1... | collective-permute-start | bytes 110600 | tf_op jit(solution)/shard_map/ppermute | solution.py:606
  77.1 12.0 %collective-permute-start.6 = (f32[36,2,128]{2,1,0:T(2,128)S(1)}, f32[36,2,128]{2,1,0:T(2,128)S(1)}, u32[]{:S(2)}, u32[]{:S(2)}) collective-permute-start(f32[36,2,128]{2,1,0:T(2,128)S(1)} %pad_maximum_fusion.2), channel_id=1, source_target_pairs={{0,1},{1,2},{2,3},{3,0},{4,5},{5,6},{6,7},{7,4},{8,9},{9,10},{10,1... | collective-permute-start | bytes 110600 | tf_op jit(solution)/shard_map/ppermute | solution.py:605
  84.9 14.7 %all-to-all-start.3 = ((f32[128,1,384]{2,1,0:T(1,128)}), f32[128,1,384]{2,1,0:T(1,128)S(1)}, u32[]{:S(2)}, u32[]{:S(2)}) async-start(f32[128,1,384]{2,1,0:T(1,128)} %bitcast.15), calls=%async_computation.3 | async-start | bytes 393216 | tf_op jit(solution)/shard_map/all_to_all | solution.py:584
  99.5 23.7 %copy-start.2 = (f32[16384]{0:T(1024)S(1)}, f32[16384]{0:T(1024)}, u32[]{:S(2)}) copy-start(f32[16384]{0:T(1024)} %param.9) | copy-start | bytes 196612
  109.8 13.4 %collective-permute-start.8 = (f32[1,64,128]{2,1,0:T(8,128)S(1)}, f32[1,64,128]{2,1,0:T(8,128)S(1)}, u32[]{:S(2)}, u32[]{:S(2)}) collective-permute-start(f32[1,64,128]{2,1,0:T(8,128)S(1)} %get-tuple-element.47), channel_id=1, source_target_pairs={{0,4},{4,0},{8,12},{12,8},{16,20},{20,16},{24,28},{28,24},{32,36},... | collective-permute-start | bytes 98312 | tf_op jit(solution)/shard_map/ppermute | solution.py:596
  110.3 13.0 %collective-permute-start.9 = (f32[1,64,128]{2,1,0:T(8,128)S(1)}, f32[1,64,128]{2,1,0:T(8,128)S(1)}, u32[]{:S(2)}, u32[]{:S(2)}) collective-permute-start(f32[1,64,128]{2,1,0:T(8,128)S(1)} %get-tuple-element.48), channel_id=1, source_target_pairs={{4,8},{12,16},{20,24},{28,32},{36,40},{44,48},{52,56},{60,64},{68,... | collective-permute-start | bytes 98312 | tf_op jit(solution)/shard_map/ppermute | solution.py:597
  112.5 16.3 %all-to-all-start.4 = ((f32[128,1,384]{2,1,0:T(1,128)}), f32[128,1,384]{2,1,0:T(1,128)S(1)}, u32[]{:S(2)}, u32[]{:S(2)}) async-start(f32[128,1,384]{2,1,0:T(1,128)} %bitcast.54), calls=%async_computation.4 | async-start | bytes 393216 | tf_op jit(solution)/shard_map/all_to_all | solution.py:584
  118.5 4.7 %collective-permute-start.10 = (f32[32,1,128]{2,1,0:T(1,128)S(1)}, f32[32,1,128]{2,1,0:T(1,128)S(1)}, u32[]{:S(2)}, u32[]{:S(2)}) collective-permute-start(f32[32,1,128]{2,1,0:T(1,128)S(1)} %get-tuple-element.56), channel_id=1, source_target_pairs={{0,1},{1,2},{2,3},{3,0},{4,5},{5,6},{6,7},{7,4},{8,9},{9,10},{10,1... | collective-permute-start | bytes 49160 | tf_op jit(solution)/shard_map/ppermute | solution.py:605
  120.1 3.2 %collective-permute-start.11 = (f32[32,1,128]{2,1,0:T(1,128)S(1)}, f32[32,1,128]{2,1,0:T(1,128)S(1)}, u32[]{:S(2)}, u32[]{:S(2)}) collective-permute-start(f32[32,1,128]{2,1,0:T(1,128)S(1)} %get-tuple-element.55), channel_id=1, source_target_pairs={{1,0},{2,1},{3,2},{0,3},{5,4},{6,5},{7,6},{4,7},{9,8},{10,9},{11,1... | collective-permute-start | bytes 49160 | tf_op jit(solution)/shard_map/ppermute | solution.py:606
